TPU v7x, 16 devices: a 4x2x1 block of a 4x4x8 slice. The times are simulated.
16 devices in a mesh: dp: 2 (over y, z), sp: 8 (over x, core).
Axes of the slice: x: 4, y: 2, z: 1, core: 2. Of those that a mesh axis runs over, the one named last changes fastest.
The devices are a block of a 4x4x8 slice.
Arguments:
- hidden: bfloat16 [49152, 2048], P(('dp', 'sp')), parts along dimension 0
- tok_perm: int32 [49152], P(('dp', 'sp')), parts along dimension 0
- send_off: int32 [128], P(('dp', 'sp')), parts along dimension 0
- send_len: int32 [128], P(('dp', 'sp')), parts along dimension 0
- recv_off: int32 [128], P(('dp', 'sp')), parts along dimension 0
- recv_len: int32 [128], P(('dp', 'sp')), parts along dimension 0
- recv_doc: int32 [24576], P(('dp', 'sp')), parts along dimension 0
- recv_pos: int32 [24576], P(('dp', 'sp')), parts along dimension 0
- g_attn: bfloat16 [2048], replicated
- w_q: bfloat16 [2048, 32, 64], replicated
- w_k: bfloat16 [2048, 32, 64], replicated
- w_v: bfloat16 [2048, 32, 64], replicated
- w_o: bfloat16 [32, 64, 2048], replicated
- g_mlp: bfloat16 [2048], replicated
- w_gate: bfloat16 [2048, 8192], replicated
- w_up: bfloat16 [2048, 8192], replicated
- w_down: bfloat16 [8192, 2048], replicated
Outputs:
- output: bfloat16 [49152, 2048], P(('dp', 'sp')), parts along dimension 0
There are 2 independent parts. A program takes and returns all parts, laid end to end along the dimension named above; an argument that names none is the same for every part.
All inputs are finite; a program needn't handle non-finite values.
Results may differ from a plain program's by a relative error of at most 0.0121102.
Values are sent between devices in bfloat16 or wider.
A program may use at most 768 MiB of HBM per device.

v0:
```python
import jax
import jax.numpy as jnp
from jax import lax
from jax.sharding import PartitionSpec as P

Q_BLOCK = 128
ROPE_BASE = 500000.0
NORM_EPS = 1e-5


def rms_norm(rows_in, gain_vec):
    rows_f = rows_in.astype(jnp.float32)
    inv_rms = lax.rsqrt(jnp.mean(rows_f * rows_f, axis=-1, keepdims=True) + NORM_EPS)
    return (rows_f * inv_rms * gain_vec.astype(jnp.float32)).astype(jnp.bfloat16)


def rope(proj, positions):
    head_dim = proj.shape[-1]
    half_dim = head_dim // 2
    inv_freq = jnp.power(jnp.float32(ROPE_BASE), -2.0 * jnp.arange(half_dim, dtype=jnp.float32) / head_dim)
    angles = positions.astype(jnp.float32)[:, None, None] * inv_freq[None, None, :]
    cos_t = jnp.cos(angles)
    sin_t = jnp.sin(angles)
    lo_half = proj[..., :half_dim]
    hi_half = proj[..., half_dim:]
    return jnp.concatenate([lo_half * cos_t - hi_half * sin_t, hi_half * cos_t + lo_half * sin_t], axis=-1)


def attend(q_rot, k_rot, v_proj, doc_ids, positions):
    n_rows, n_kv, q_per_kv, head_dim = q_rot.shape
    n_blocks = n_rows // Q_BLOCK
    qk_scale = head_dim ** -0.5

    def one_block(blk_args):
        q_blk, doc_q, pos_q = blk_args
        scores = jnp.einsum('qkgd,skd->kgqs', q_blk, k_rot, preferred_element_type=jnp.float32) * qk_scale
        allowed = (doc_q[:, None] == doc_ids[None, :]) & (positions[None, :] <= pos_q[:, None])
        probs_bf = jax.nn.softmax(jnp.where(allowed, scores, -1e30), axis=-1).astype(jnp.bfloat16)
        return jnp.einsum('kgqs,skd->qkgd', probs_bf, v_proj, preferred_element_type=jnp.float32).astype(jnp.bfloat16)

    blocks_out = lax.map(one_block, (q_rot.reshape(n_blocks, Q_BLOCK, n_kv, q_per_kv, head_dim), doc_ids.reshape(n_blocks, Q_BLOCK), positions.reshape(n_blocks, Q_BLOCK)))
    return blocks_out.reshape(n_rows, n_kv, q_per_kv, head_dim)


def layer(dest_rows, doc_ids, positions, g_attn, w_q, w_k, w_v, w_o, g_mlp, w_gate, w_up, w_down):
    n_rows, model_dim = dest_rows.shape
    n_heads = w_q.shape[1]
    head_dim = w_q.shape[2]
    n_kv = w_k.shape[1]
    normed = rms_norm(dest_rows, g_attn)
    q_proj = jnp.einsum('td,dhe->the', normed, w_q, preferred_element_type=jnp.float32)
    k_proj = jnp.einsum('td,dhe->the', normed, w_k, preferred_element_type=jnp.float32)
    v_proj = jnp.einsum('td,dhe->the', normed, w_v, preferred_element_type=jnp.float32).astype(jnp.bfloat16)
    q_rot = rope(q_proj, positions).astype(jnp.bfloat16).reshape(n_rows, n_kv, n_heads // n_kv, head_dim)
    k_rot = rope(k_proj, positions).astype(jnp.bfloat16)
    attn_heads = attend(q_rot, k_rot, v_proj, doc_ids, positions)
    attn_out = jnp.einsum('qkgd,kgde->qe', attn_heads, w_o.reshape(n_kv, n_heads // n_kv, head_dim, model_dim), preferred_element_type=jnp.float32).astype(jnp.bfloat16)
    resid_mid = (dest_rows.astype(jnp.float32) + attn_out.astype(jnp.float32)).astype(jnp.bfloat16)
    normed_mlp = rms_norm(resid_mid, g_mlp)
    gate_proj = jnp.dot(normed_mlp, w_gate, preferred_element_type=jnp.float32)
    up_proj = jnp.dot(normed_mlp, w_up, preferred_element_type=jnp.float32)
    hidden_act = (jax.nn.silu(gate_proj) * up_proj).astype(jnp.bfloat16)
    down_proj = jnp.dot(hidden_act, w_down, preferred_element_type=jnp.float32).astype(jnp.bfloat16)
    return (resid_mid.astype(jnp.float32) + down_proj.astype(jnp.float32)).astype(jnp.bfloat16)


def solution(mesh):
    row_spec = P(('dp', 'sp'), None)
    vec_spec = P(('dp', 'sp'))
    rep_spec = P()

    def per_device(hidden, tok_perm, send_off, send_len, recv_off, recv_len, recv_doc, recv_pos, g_attn, w_q, w_k, w_v, w_o, g_mlp, w_gate, w_up, w_down):
        n_tok, model_dim = hidden.shape
        n_cap = recv_doc.shape[0]
        group_devs = send_off.shape[0]
        zero_val = jnp.zeros((), hidden.dtype)
        pair_row = jnp.arange(n_cap)[None, :]
        dev_base = jnp.arange(group_devs)[None, :] * n_cap
        send_idx = jnp.minimum(send_off[:, None] + pair_row, n_tok - 1).reshape(-1)
        send_buf = jnp.take(hidden, jnp.take(tok_perm, send_idx), axis=0).reshape(group_devs, n_cap, model_dim)
        recv_buf = lax.all_to_all(send_buf, 'sp', 0, 0, tiled=True).reshape(group_devs * n_cap, model_dim)
        slot_idx = jnp.arange(n_cap)[:, None]
        in_run = (slot_idx >= recv_off[None, :]) & (slot_idx < (recv_off + recv_len)[None, :])
        flat_pos = jnp.sum(jnp.where(in_run, dev_base + slot_idx - recv_off[None, :], 0), axis=1)
        dest_rows = jnp.take(recv_buf, flat_pos, axis=0)
        layer_rows = layer(dest_rows, recv_doc, recv_pos, g_attn, w_q, w_k, w_v, w_o, g_mlp, w_gate, w_up, w_down)
        back_idx = jnp.minimum(recv_off[:, None] + pair_row, n_cap - 1).reshape(-1)
        back_buf = jnp.take(layer_rows, back_idx, axis=0).reshape(group_devs, n_cap, model_dim)
        back_recv = lax.all_to_all(back_buf, 'sp', 0, 0, tiled=True).reshape(group_devs * n_cap, model_dim)
        inv_perm = jnp.argsort(tok_perm)[:, None]
        in_back = (inv_perm >= send_off[None, :]) & (inv_perm < (send_off + send_len)[None, :])
        back_pos = jnp.sum(jnp.where(in_back, dev_base + inv_perm - send_off[None, :], 0), axis=1)
        was_sent = jnp.any(in_back, axis=1)
        return jnp.where(was_sent[:, None], jnp.take(back_recv, back_pos, axis=0), zero_val)

    return jax.shard_map(per_device, mesh=mesh, in_specs=(row_spec,) + (vec_spec,) * 7 + (rep_spec,) * 9, out_specs=row_spec, check_vma=False)
```

profile of v0, /device:TPU:113, one launch (start us, length us, event | category | flops | bytes accessed | tf_op | source)
XLA Modules:
  0.0 2408.9 jit_solution(282131502320627551)
XLA Ops:
  0.9 68.0 %gather_fusion = s32[12288]{0:T(1024)S(1)} fusion(s32[3072]{0:T(1024)S(1)} %copy-done, s32[12288]{0:T(1024)S(1)} %broadcast_clamp_fusion.2), kind=kCustom, calls=%fused_computation | custom fusion | bytes 147456 | tf_op jit(solution)/shard_map/jit(_take)/gather | solution.py:80
  69.2 97.5 %gather_fusion.1 = bf16[12288,2048]{1,0:T(8,128)(2,1)} fusion(bf16[3072,2048]{1,0:T(8,128)(2,1)} %param.19, s32[12288]{0:T(1024)S(1)} %broadcast_clamp_fusion.1), kind=kCustom, calls=%fused_computation.1 | custom fusion | bytes 100712448 | tf_op jit(solution)/shard_map/jit(_take)/gather | solution.py:80
  166.8 33.4 %broadcast_select_fusion = bf16[8,1536,2048]{2,1,0:T(8,128)(2,1)} fusion(bf16[8,1536,2048]{2,1,0:T(8,128)(2,1)} %bitcast.101, pred[8,1536]{1,0:T(8,128)(4,1)S(1)} %compare_and_fusion.2), kind=kLoop, calls=%fused_computation.23 | loop fusion | flops 25165824 | bytes 100675584 | tf_op jit(solution)/shard_map/jit(_take)/select_n | solution.py:80
  213.3 539.8 %all-to-all-done = bf16[8,1536,2048]{2,1,0:T(8,128)(2,1)} async-done(((bf16[8,1536,2048]{2,1,0:T(8,128)(2,1)}), bf16[8,1536,2048]{2,1,0:T(8,128)(2,1)}, u32[]{:S(2)}, u32[]{:S(2)}) %all-to-all-start) | async-done | bytes 50331680 | tf_op jit(solution)/shard_map/all_to_all | solution.py:81
  753.2 16.7 gather_fusion.2
  775.6 20.2 fusion.45
  795.9 18.2 fusion.43
  814.1 13.5 subtract_convert_fusion
  854.1 20.3 fusion.41
  886.3 461.4 %while.10 = (s32[]{:T(128)}, bf16[12,128,32,1,64]{1,4,2,3,0:T(8,128)(2,1)}, s32[12,128]{1,0:T(8,128)S(1)}, s32[1536]{0:T(1024)S(1)}, s32[1536]{0:T(1024)S(1)}, /...) while((s32[]{:T(128)}, ...), condition=%wide.region_8.9_spmd, body=%wide.region_5.8_spmd.sunk | while | flops 1661788160 | bytes 114786440 | solution.py:41
  886.5 15.3 fusion.80
  901.8 11.4 fusion.81
  913.2 11.5 fusion.82
  924.9 15.3 fusion.80
  940.2 11.4 fusion.81
  951.6 11.5 fusion.82
  963.4 15.3 fusion.80
  978.6 11.4 fusion.81
  990.0 11.5 fusion.82
  1001.8 15.3 fusion.80
  1028.4 11.5 fusion.82
  1040.2 15.3 fusion.80
  1066.8 11.5 fusion.82
  1078.6 15.3 fusion.80
  1105.3 11.5 fusion.82
  1117.0 15.3 fusion.80
  1143.7 11.5 fusion.82
  1155.4 15.3 fusion.80
  1182.1 11.5 fusion.82
  1193.9 15.3 fusion.80
  1220.5 11.5 fusion.82
  1232.3 15.3 fusion.80
  1258.9 11.5 fusion.82
  1270.7 15.3 fusion.80
  1297.4 11.5 fusion.82
  1309.2 15.3 fusion.80
  1335.8 11.5 fusion.82
  1347.7 16.3 copy.23
  1364.0 12.2 reshape.349
  1376.1 20.6 fusion.21
  1399.5 59.6 %fusion.27 = f32[1536,8192]{1,0:T(8,128)} fusion(bf16[2048,8192]{1,0:T(8,128)(2,1)} %param.33, bf16[1536,2048]{1,0:T(8,128)(2,1)S(1)} %get-tuple-element.104, f32[2048]{0:T(1024)S(1)} %copy-done.14, f32[1536]{0:T(1024)S(1)} %add_rsqrt_fusion), kind=kOutput, calls=%fused_computation.49 | convolution fusion | flops 51552190464 | bytes 90191872 | tf_op jit(solution)/shard_map/dot_general | solution.py:60
  1459.1 69.1 %multiply_convert_fusion.clone.6 = bf16[1536,8192]{1,0:T(8,128)(2,1)} fusion(f32[1536,8192]{1,0:T(8,128)} %fusion.27, bf16[2048,8192]{1,0:T(8,128)(2,1)} %param.34, bf16[1536,2048]{1,0:T(8,128)(2,1)} %copy-done.24, f32[2048]{0:T(1024)S(1)} %copy-done.14, f32[1536]{0:T(1024)S(1)} %add_rsqrt_fusion), kind=kOutput, calls=%fused_computation.22.clone.clone.clone.clone.clone.1 | convolution fusion | flops 51627687936 | bytes 115357696 | tf_op jit(solution)/shard_map/dot_general | solution.py:61
  1528.2 65.5 %fusion.24 = bf16[1536,2048]{1,0:T(8,128)(2,1)} fusion(bf16[1536,2048]{1,0:T(8,128)(2,1)} %copy-done.24, bf16[8192,2048]{1,0:T(8,128)(2,1)} %param.35, bf16[1536,8192]{1,0:T(8,128)(2,1)} %multiply_convert_fusion.clone.6), kind=kOutput, calls=%fused_computation.38 | convolution fusion | flops 51555336192 | bytes 71303168 | tf_op jit(solution)/shard_map/dot_general | solution.py:63
  1593.7 95.0 %gather_fusion.3 = bf16[12288,2048]{1,0:T(8,128)(2,1)} fusion(bf16[1536,2048]{1,0:T(8,128)(2,1)} %fusion.24, s32[12288]{0:T(1024)S(1)} %copy-done.8), kind=kCustom, calls=%fused_computation.3 | custom fusion | bytes 100712448 | tf_op jit(solution)/shard_map/jit(_take)/gather | solution.py:88
  1688.7 33.4 %broadcast_select_fusion.1 = bf16[8,1536,2048]{2,1,0:T(8,128)(2,1)} fusion(bf16[8,1536,2048]{2,1,0:T(8,128)(2,1)} %bitcast.100, pred[8,1536]{1,0:T(8,128)(4,1)S(1)} %copy-done.9), kind=kLoop, calls=%fused_computation.24 | loop fusion | flops 25165824 | bytes 100675584 | tf_op jit(solution)/shard_map/jit(_take)/select_n | solution.py:88
  1738.2 537.0 %all-to-all-done.1 = bf16[8,1536,2048]{2,1,0:T(8,128)(2,1)} async-done(((bf16[8,1536,2048]{2,1,0:T(8,128)(2,1)}), bf16[8,1536,2048]{2,1,0:T(8,128)(2,1)}, u32[]{:S(2)}, u32[]{:S(2)}) %all-to-all-start.1) | async-done | bytes 50331680 | tf_op jit(solution)/shard_map/all_to_all | solution.py:89
  2275.2 121.8 %gather_fusion.4 = bf16[3072,2048]{1,0:T(8,128)(2,1)} fusion(bf16[12288,2048]{1,0:T(8,128)(2,1)} %bitcast.27, s32[3072]{0:T(1024)S(1)} %broadcast_clamp_fusion.3), kind=kCustom, calls=%fused_computation.4 | custom fusion | bytes 25178112 | tf_op jit(solution)/shard_map/jit(_take)/gather | solution.py:94
  2397.0 11.4 select_select_fusion
  (159 shorter events, 182.1 us)
Async XLA Ops:
  0.0 0.9 copy-start
  0.9 68.2 %copy-start.12 = (s32[8]{0:T(128)S(1)}, s32[8]{0:T(128)}, u32[]{:S(2)}) copy-start(s32[8]{0:T(128)} %param.21) | copy-start | bytes 100
  200.2 10.0 copy-start.18
  200.2 10.0 copy-start.5
  200.2 10.0 copy-start.19
  200.2 10.6 copy-start.17
  200.2 10.6 copy-start.22
  200.3 552.9 %all-to-all-start = ((bf16[8,1536,2048]{2,1,0:T(8,128)(2,1)}), bf16[8,1536,2048]{2,1,0:T(8,128)(2,1)}, u32[]{:S(2)}, u32[]{:S(2)}) async-start(bf16[8,1536,2048]{2,1,0:T(8,128)(2,1)} %broadcast_select_fusion), calls=%async_computation | async-start | bytes 100663296 | tf_op jit(solution)/shard_map/all_to_all | solution.py:81
  211.0 558.8 %copy-start.20 = (s32[8]{0:T(128)}, s32[8]{0:T(128)S(1)}, u32[]{:S(2)}) copy-start(s32[8]{0:T(128)S(1)} %iota_multiply_fusion) | copy-start | bytes 100
  211.2 642.9 %copy-start.10 = (pred[1536]{0:T(1024)(128)(4,1)}, pred[1536]{0:T(1024)(128)(4,1)S(1)}, u32[]{:S(2)}) copy-start(pred[1536]{0:T(1024)(128)(4,1)S(1)} %compare_and_fusion.4) | copy-start | bytes 4612
  769.9 26.0 %slice-start = ((s8[6291456]{0:T(1024)(128)(4,1)}), s8[4194304]{0:T(1024)(128)(4,1)S(1)}, s32[]{:S(2)}) async-start(s8[6291456]{0:T(1024)(128)(4,1)} %bitcast.102), calls=%async_computation.2 | async-start | bytes 8388608
  769.9 26.0 %slice-start.2 = ((s8[8388608]{0:T(1024)(128)(4,1)}), s8[4194304]{0:T(1024)(128)(4,1)S(1)}, s32[]{:S(2)}) async-start(s8[8388608]{0:T(1024)(128)(4,1)} %bitcast.123), calls=%async_computation.4 | async-start | bytes 8388608
  775.6 20.2 copy-start.15
  775.6 20.2 slice-start.1
  775.6 20.2 slice-start.3
  846.3 7.8 copy-start.16
  874.5 8.4 copy-start.2
  874.5 8.4 copy-start.3
  882.9 3.4 copy-start.6
  882.9 3.4 copy-start.7
  901.8 11.4 copy-start.4
  940.2 11.4 copy-start.4
  978.6 11.4 copy-start.4
  1017.0 11.4 copy-start.4
  1055.5 11.4 copy-start.4
  1093.9 11.4 copy-start.4
  1132.3 11.4 copy-start.4
  1170.7 11.4 copy-start.4
  1209.1 11.4 copy-start.4
  1247.6 11.4 copy-start.4
  1286.0 11.4 copy-start.4
  1324.4 11.4 copy-start.4
  1364.0 12.2 copy-start.11
  1376.1 23.3 copy-start.14
  1396.8 2.7 copy-start.24
  1528.2 65.5 %copy-start.8 = (s32[12288]{0:T(1024)S(1)}, s32[12288]{0:T(1024)}, u32[]{:S(2)}) copy-start(s32[12288]{0:T(1024)} %broadcast_clamp_fusion) | copy-start | bytes 147460
  1593.7 95.0 %copy-start.9 = (pred[8,1536]{1,0:T(8,128)(4,1)S(1)}, pred[8,1536]{1,0:T(8,128)(4,1)}, u32[]{:S(2)}) copy-start(pred[8,1536]{1,0:T(8,128)(4,1)} %fusion.36) | copy-start | bytes 36868
  1722.1 10.1 copy-start.1
  1722.1 15.9 copy-start.13
  1722.1 15.9 copy-start.23
  1722.1 16.0 copy-start.21
  1722.1 553.1 %all-to-all-start.1 = ((bf16[8,1536,2048]{2,1,0:T(8,128)(2,1)}), bf16[8,1536,2048]{2,1,0:T(8,128)(2,1)}, u32[]{:S(2)}, u32[]{:S(2)}) async-start(bf16[8,1536,2048]{2,1,0:T(8,128)(2,1)} %broadcast_select_fusion.1), calls=%async_computation.1 | async-start | bytes 100663296 | tf_op jit(solution)/shard_map/all_to_all | solution.py:89
where the time goes:
time: 2450 us; the launch traced here: 2410 us
  waiting for transfers between devices  1080 us (44%)
  matrix products  595 us (24%)
  local copies, waits for them, and re-layouts  449 us (18%)
  other arithmetic  267 us (11%)
    all_to_all x1, waiting for transfers between devices, per_device(): lax.all_to_all(send_buf, 'sp', 0, 0, tiled=True)  540 us
    all_to_all x1, waiting for transfers between devices, per_device(): lax.all_to_all(back_buf, 'sp', 0, 0, tiled=True)  537 us
    dot_general x12, matrix products, one_block(): jnp.einsum('qkgd,skd->kgqs', q_blk, k_rot, preferred_element_type=jnp.flo...  183 us
    dot_general x12, matrix products, one_block(): jnp.einsum('kgqs,skd->qkgd', probs_bf, v_proj, preferred_element_type=jnp...  138 us
    reduce_sum x12, other arithmetic, one_block(): jax.nn.softmax(jnp.where(allowed, scores, -1e+30), axis=-1)  136 us
    gather x1, local copies, waits for them, and re-layouts, per_device(): jnp.take(back_recv, back_pos, axis=0)  122 us
    gather x1, local copies, waits for them, and re-layouts, per_device(): jnp.take(hidden, jnp.take(tok_perm, send_idx), axis=0)  97.5 us
    gather x1, local copies, waits for them, and re-layouts, per_device(): jnp.take(layer_rows, back_idx, axis=0).reshape(group_devs, n_cap, model_dim)  95 us
  transfers between devices with their start and end apart: 2, of which 2 were waited for; matrix products, arithmetic and copies ran while one was open for 0% of the time, Pallas kernels for 0%

commit v1 on v0

v1 whole, which is shorter than its diff:
```python
import functools

import jax
import jax.numpy as jnp
import numpy as np
from jax import lax
from jax.experimental import pallas as pl
from jax.experimental.pallas import tpu as pltpu
from jax.sharding import PartitionSpec as P

ROPE_BASE = 500000.0
NORM_EPS = 1e-5
Q_TILE = 256
QKV_TILE = 512


def rms_norm(rows_in, gain_vec):
    rows_f = rows_in.astype(jnp.float32)
    inv_rms = lax.rsqrt(jnp.mean(rows_f * rows_f, axis=-1, keepdims=True) + NORM_EPS)
    return (rows_f * inv_rms * gain_vec.astype(jnp.float32)).astype(jnp.bfloat16)


def rope_tables(positions, head_dim):
    half = head_dim // 2
    inv_freq = jnp.power(jnp.float32(ROPE_BASE), -2.0 * jnp.arange(half, dtype=jnp.float32) / head_dim)
    angles = positions.astype(jnp.float32)[:, None] * inv_freq[None, :]
    cos_t = jnp.cos(angles)
    sin_t = jnp.sin(angles)
    return jnp.concatenate([cos_t] * 4, axis=1), jnp.concatenate([-sin_t, sin_t] * 2, axis=1)


def qkv_proj(normed, w_q, w_k, w_v, cos_t, sin_t):
    rows, model_dim = normed.shape
    n_heads, head_dim = w_q.shape[1:]
    width = n_heads * head_dim
    w_all = [w.transpose(1, 2, 0).reshape(width, model_dim) for w in (w_q, w_k, w_v)]
    outs = []
    for kind, w in enumerate(w_all):
        outs.append(pl.pallas_call(
            functools.partial(qkv_one, head_dim, kind),
            out_shape=jax.ShapeDtypeStruct((rows, width), jnp.bfloat16),
            grid=(width // QKV_TILE,),
            in_specs=[
                pl.BlockSpec((rows, model_dim), lambda n: (0, 0)),
                pl.BlockSpec((QKV_TILE, model_dim), lambda n: (n, 0)),
                pl.BlockSpec(cos_t.shape, lambda n: (0, 0)),
                pl.BlockSpec(sin_t.shape, lambda n: (0, 0)),
            ],
            out_specs=pl.BlockSpec((rows, QKV_TILE), lambda n: (0, n)),
            compiler_params=pltpu.CompilerParams(vmem_limit_bytes=48 * 1024 * 1024),
            cost_estimate=pl.CostEstimate(flops=2 * rows * model_dim * width, bytes_accessed=2 * (2 * rows * model_dim + model_dim * width), transcendentals=0),
            name="qkv",
        )(normed, w, cos_t, sin_t))
    return outs


def qkv_one(head_dim, kind, h_ref, w_ref, cos_ref, sin_ref, o_ref):
    rows, cols = o_ref.shape
    lanes = cos_ref.shape[1]
    half = head_dim // 2
    step = 256
    scale = head_dim ** -0.5 if kind == 0 else 1.0

    @pl.loop(0, rows // step)
    def _(t):
        at = pl.ds(pl.multiple_of(t * step, step), step)
        acc = lax.dot_general(h_ref[at, :], w_ref[...], (((1,), (1,)), ((), ())), preferred_element_type=jnp.float32)
        if kind == 2:
            o_ref[at, :] = acc.astype(o_ref.dtype)
        else:
            cos_t = cos_ref[at, :]
            sin_t = sin_ref[at, :]
            first = lax.rem(lax.broadcasted_iota(jnp.int32, cos_t.shape, 1), head_dim) < half
            for b in range(cols // lanes):
                x = acc[:, b * lanes:(b + 1) * lanes]
                swapped = jnp.where(first, pltpu.roll(x, lanes - half, 1), pltpu.roll(x, half, 1))
                rot = (x * cos_t + swapped * sin_t) * scale
                o_ref[at, b * lanes:(b + 1) * lanes] = rot.astype(o_ref.dtype)


def attn_kernel(head_dim, q_ref, k_ref, v_ref, meta_row_ref, meta_col_ref, o_ref, bias_ref):
    rows, lanes = q_ref.shape
    n_tiles = rows // Q_TILE

    @pl.when(pl.program_id(0) == 0)
    def _():
        for t in range(n_tiles):
            at = slice(t * Q_TILE, (t + 1) * Q_TILE)
            n_keys = (t + 1) * Q_TILE
            ok = (meta_col_ref[at, 0:1] == meta_row_ref[0:1, :n_keys]) & (meta_row_ref[1:2, :n_keys] <= meta_col_ref[at, 1:2])
            bias_ref[at, :n_keys] = jnp.where(ok, 0.0, -1e30).astype(jnp.float32)

    lane = lax.broadcasted_iota(jnp.int32, (Q_TILE, lanes), 1)
    for t in range(n_tiles):
        at = slice(t * Q_TILE, (t + 1) * Q_TILE)
        n_keys = (t + 1) * Q_TILE
        q_blk = q_ref[at, :]
        heads_out = []
        for h in range(lanes // head_dim):
            mine = (lane >= h * head_dim) & (lane < (h + 1) * head_dim)
            q_h = jnp.where(mine, q_blk, jnp.zeros((), q_blk.dtype))
            s = lax.dot_general(q_h, k_ref[:n_keys, :], (((1,), (1,)), ((), ())), preferred_element_type=jnp.float32)
            s = s + bias_ref[at, :n_keys]
            top = jnp.max(s, axis=1, keepdims=True)
            e = jnp.exp(s - top)
            total = jnp.sum(e, axis=1, keepdims=True)
            o_h = jnp.dot(e.astype(jnp.bfloat16), v_ref[:n_keys, :], preferred_element_type=jnp.float32)
            heads_out.append(jnp.where(mine, o_h / total, 0.0))
        o_ref[at, :] = sum(heads_out).astype(o_ref.dtype)


def attention(q, k, v, doc_ids, positions, head_dim):
    rows, width = q.shape
    lanes = 128
    meta = jnp.stack([doc_ids, positions])
    head_spec = pl.BlockSpec((rows, lanes), lambda n: (0, n))
    whole = lambda a: pl.BlockSpec(a.shape, lambda n: (0, 0))
    meta_t = meta.T
    return pl.pallas_call(
        functools.partial(attn_kernel, head_dim),
        out_shape=jax.ShapeDtypeStruct((rows, width), jnp.bfloat16),
        grid=(width // lanes,),
        in_specs=[head_spec, head_spec, head_spec, whole(meta), whole(meta_t)],
        out_specs=head_spec,
        scratch_shapes=[pltpu.VMEM((rows, rows), jnp.float32)],
        compiler_params=pltpu.CompilerParams(vmem_limit_bytes=56 * 1024 * 1024),
        cost_estimate=pl.CostEstimate(flops=3 * rows * rows * width, bytes_accessed=8 * rows * width, transcendentals=rows * rows * width // 128),
        name="attention",
    )(q, k, v, meta, meta_t)


def layer(dest_rows, doc_ids, positions, g_attn, w_q, w_k, w_v, w_o, g_mlp, w_gate, w_up, w_down):
    model_dim = dest_rows.shape[1]
    n_heads, head_dim = w_q.shape[1:]
    cos_t, sin_t = rope_tables(positions, head_dim)
    normed = rms_norm(dest_rows, g_attn)
    q, k, v = qkv_proj(normed, w_q, w_k, w_v, cos_t, sin_t)
    attn_heads = attention(q, k, v, doc_ids, positions, head_dim)
    attn_out = jnp.dot(attn_heads, w_o.reshape(n_heads * head_dim, model_dim), preferred_element_type=jnp.float32).astype(jnp.bfloat16)
    resid_mid = (dest_rows.astype(jnp.float32) + attn_out.astype(jnp.float32)).astype(jnp.bfloat16)
    normed_mlp = rms_norm(resid_mid, g_mlp)
    gate_proj = jnp.dot(normed_mlp, w_gate, preferred_element_type=jnp.float32)
    up_proj = jnp.dot(normed_mlp, w_up, preferred_element_type=jnp.float32)
    hidden_act = (jax.nn.silu(gate_proj) * up_proj).astype(jnp.bfloat16)
    down_proj = jnp.dot(hidden_act, w_down, preferred_element_type=jnp.float32).astype(jnp.bfloat16)
    return (resid_mid.astype(jnp.float32) + down_proj.astype(jnp.float32)).astype(jnp.bfloat16)


def relay_tables(group):
    n_relay = group
    relay_of = np.array([[c for c in range(n_relay)] for i in range(group)])
    source_of = np.array([[i for i in range(group)] for k in range(group)])
    residue = np.array([[int(np.where(relay_of[source_of[k, m]] == k)[0][0]) for m in range(n_relay)] for k in range(group)])
    return relay_of, source_of, residue


def ceil_div(a, b):
    return -((-a) // b)


def pick(table, index, n):
    return jnp.sum(jnp.where(index[:, None] == jnp.arange(n)[None, :], table[None, :], 0), axis=1)


def plan_indices(me, len_ij, tok_perm, n_tok, n_cap, cap1, cap2, relay_of, source_of, residue):
    group, n_relay = relay_of.shape
    off_ij = jnp.cumsum(len_ij, axis=1) - len_ij
    roff_ij = jnp.cumsum(len_ij, axis=0) - len_ij
    res = np.arange(n_relay)
    first = ceil_div(off_ij[:, None, :] - res[None, :, None], n_relay)
    count = ceil_div((off_ij + len_ij)[:, None, :] - res[None, :, None], n_relay) - first
    first_k = first[source_of, residue]
    count_k = count[source_of, residue]
    base_k = jnp.cumsum(count_k, axis=1) - count_k
    end_k = base_k + count_k

    def mine(t):
        return lax.dynamic_index_in_dim(t, me, 0, keepdims=False)

    base_me, end_me, first_me = mine(base_k), mine(end_k), mine(first_k)
    q = jnp.arange(cap2)
    in_m = (q[None, None, :] >= base_me[:, :, None]) & (q[None, None, :] < end_me[:, :, None])
    src = jnp.arange(n_relay)[:, None, None] * cap1 + first_me[:, :, None] + q[None, None, :] - base_me[:, :, None]
    relay_idx = jnp.sum(jnp.where(in_m, src, 0), axis=0).reshape(-1)

    slot = jnp.arange(cap1)
    in_j = (slot[None, None, :] >= first_me[:, :, None]) & (slot[None, None, :] < (first_me + end_me - base_me)[:, :, None])
    back = jnp.arange(group)[None, :, None] * cap2 + base_me[:, :, None] + slot[None, None, :] - first_me[:, :, None]
    relay_back_idx = jnp.sum(jnp.where(in_j, back, 0), axis=1).reshape(-1)

    len_me = lax.dynamic_index_in_dim(len_ij, me, 1, keepdims=False)
    off_me = lax.dynamic_index_in_dim(off_ij, me, 1, keepdims=False)
    roff_me = lax.dynamic_index_in_dim(roff_ij, me, 1, keepdims=False)
    base_ic = jnp.zeros((group, n_relay), jnp.int32)
    base_to_me = lax.dynamic_index_in_dim(base_k, me, 2, keepdims=False)
    first_to_me = lax.dynamic_index_in_dim(first, me, 2, keepdims=False)
    place = np.zeros((group, n_relay), np.int32)
    for k in range(group):
        for m in range(n_relay):
            place[source_of[k, m], residue[k, m]] = k * n_relay + m
    base_ic = base_to_me.reshape(-1)[place]
    table = relay_of * cap2 + base_ic - first_to_me
    u = jnp.arange(n_cap)
    in_i = (u[:, None] >= roff_me[None, :]) & (u[:, None] < (roff_me + len_me)[None, :])
    r_of_u = jnp.sum(jnp.where(in_i, off_me[None, :] + u[:, None] - roff_me[None, :], 0), axis=1)
    i_of_u = jnp.sum(jnp.where(in_i, np.arange(group)[None, :], 0), axis=1)
    c_of_u = lax.rem(r_of_u, n_relay)
    dest_idx = pick(table.reshape(-1), i_of_u * n_relay + c_of_u, group * n_relay) + r_of_u // n_relay

    count_to_me = lax.dynamic_index_in_dim(count_k, me, 2, keepdims=False)
    first_km = lax.dynamic_index_in_dim(first_k, me, 2, keepdims=False)
    in_km = (q[None, None, :] >= base_to_me[:, :, None]) & (q[None, None, :] < (base_to_me + count_to_me)[:, :, None])
    r_km = (first_km[:, :, None] + q[None, None, :] - base_to_me[:, :, None]) * n_relay + residue[:, :, None]
    u_km = r_km + (roff_me - off_me)[source_of][:, :, None]
    dest_back_idx = jnp.sum(jnp.where(in_km, u_km, 0), axis=1).reshape(-1)

    used = jnp.sum(lax.dynamic_index_in_dim(len_ij, me, 0, keepdims=False))
    r = jnp.arange(cap1)[None, :] * n_relay + res[:, None]
    send_idx = jnp.pad(tok_perm, (0, cap1 * n_relay - n_tok)).reshape(cap1, n_relay).T.reshape(-1)
    inv_perm = jnp.argsort(tok_perm)
    final_idx = lax.rem(inv_perm, n_relay) * cap1 + inv_perm // n_relay
    return send_idx, relay_idx, dest_idx, dest_back_idx, relay_back_idx, final_idx, inv_perm < used


def solution(mesh):
    row_spec = P(('dp', 'sp'), None)
    vec_spec = P(('dp', 'sp'))
    rep_spec = P()

    def per_device(hidden, tok_perm, send_off, send_len, recv_off, recv_len, recv_doc, recv_pos, g_attn, w_q, w_k, w_v, w_o, g_mlp, w_gate, w_up, w_down):
        n_tok, model_dim = hidden.shape
        n_cap = recv_doc.shape[0]
        group = send_off.shape[0]
        relay_of, source_of, residue = relay_tables(group)
        n_relay = relay_of.shape[1]
        cap1 = -(-n_tok // n_relay)
        cap2 = -(-(n_cap + n_relay * (n_relay - 1)) // n_relay)
        cap2 = -(-cap2 // 8) * 8
        me = lax.axis_index('sp')
        len_ij = lax.all_gather(send_len, 'sp')
        send_idx, relay_idx, dest_idx, dest_back_idx, relay_back_idx, final_idx, was_sent = plan_indices(
            me, len_ij, tok_perm, n_tok, n_cap, cap1, cap2, relay_of, source_of, residue)

        def take(rows, index):
            return rows.at[index].get(mode='promise_in_bounds')

        def exchange(rows, cap):
            return lax.all_to_all(rows.reshape(-1, cap, model_dim), 'sp', 0, 0, tiled=True).reshape(-1, model_dim)

        relay_rows = exchange(take(hidden, send_idx), cap1)
        dest_rows = take(exchange(take(relay_rows, relay_idx), cap2), dest_idx)
        out_rows = layer(dest_rows, recv_doc, recv_pos, g_attn, w_q, w_k, w_v, w_o, g_mlp, w_gate, w_up, w_down)
        relay_back = exchange(take(out_rows, dest_back_idx), cap2)
        src_back = exchange(take(relay_back, relay_back_idx), cap1)
        return jnp.where(was_sent[:, None], take(src_back, final_idx), jnp.zeros((), hidden.dtype))

    return jax.shard_map(per_device, mesh=mesh, in_specs=(row_spec,) + (vec_spec,) * 7 + (rep_spec,) * 9, out_specs=row_spec, check_vma=False)
```

time: 2450 us -> 1030 us (0.42); the launches traced: 2410 us -> 1020 us
  waiting for transfers between devices: 1080 us -> 268 us
  matrix products: 595 us -> 213 us
  local copies, waits for them, and re-layouts: 449 us -> 153 us
  other arithmetic: 267 us -> 37.4 us
  Pallas kernels: 0 us -> 180 us
  blocking collectives: 0 us -> 139 us
    all_to_all x2 -> x4, waiting for transfers between devices: 1080 us -> 268 us  [exchange(): lax.all_to_all(rows.reshape(-1, cap, model_dim), 'sp', 0, 0, tiled=True)]
    dot_general x25 -> x1, matrix products: 342 us -> 18.5 us  [layer(): jnp.dot(attn_heads, w_o.reshape(n_heads * head_dim, model_dim), preferred...]
    gather x6 -> x11, local copies, waits for them, and re-layouts: 399 us -> 146 us  [the longest x6 143 us: take(): return rows.at[index].get(mode='promise_in_bounds')]
    pallas_call x0 -> x4, Pallas kernels: none -> 180 us  [the longest x1 99.1 us: attention(): pl.pallas_call(functools.partial(attn_kernel, head_dim), out_shape=jax.Sh...]
    unnamed x0 -> x1, blocking collectives: none -> 139 us
    reduce_sum x14 -> x6, other arithmetic: 137 us -> 1.98 us  [the longest x1 1.39 us: plan_indices(): used = jnp.sum(lax.dynamic_index_in_dim(len_ij, me, 0, keepdims=False))]
    select_n x8 -> x6, other arithmetic: 78.5 us -> 11.2 us  [the longest x1 11.1 us: per_device(): jnp.where(was_sent[:, None], take(src_back, final_idx), jnp.zeros((), hid...]
    unnamed x3 -> x0, matrix products: 58.8 us -> none
  transfers between devices with their start and end apart: 2 -> 4, of which waited for: 2 -> 3; matrix products, arithmetic and copies ran while one was open for 0% -> 2% of each run, Pallas kernels for 0% -> 0%
where the time goes in v1:
time: 1030 us; the launch traced here: 1020 us
  waiting for transfers between devices  268 us (26%)
  matrix products  213 us (21%)
  Pallas kernels  180 us (17%)
  local copies, waits for them, and re-layouts  153 us (15%)
  blocking collectives  139 us (13%)
  other arithmetic  37.4 us (4%)
  starting transfers between devices  25.8 us (3%)
    all_to_all x4, waiting for transfers between devices, exchange(): lax.all_to_all(rows.reshape(-1, cap, model_dim), 'sp', 0, 0, tiled=True)  268 us
    gather x6, local copies, waits for them, and re-layouts, take(): return rows.at[index].get(mode='promise_in_bounds')  143 us
    unnamed x1, blocking collectives  139 us
    pallas_call x1, Pallas kernels, attention(): pl.pallas_call(functools.partial(attn_kernel, head_dim), out_shape=jax.Sh...  99.1 us
    pallas_call x3, Pallas kernels, qkv_proj(): pl.pallas_call(functools.partial(qkv_one, head_dim, kind), out_shape=jax....  81 us
    dot_general x1, matrix products, layer(): up_proj = jnp.dot(normed_mlp, w_up, preferred_element_type=jnp.float32)  68.9 us
    dot_general x1, matrix products, layer(): jnp.dot(hidden_act, w_down, preferred_element_type=jnp.float32)  65.5 us
    dot_general x1, matrix products, layer(): gate_proj = jnp.dot(normed_mlp, w_gate, preferred_element_type=jnp.float32)  59.7 us
  transfers between devices with their start and end apart: 4, of which 3 were waited for; matrix products, arithmetic and copies ran while one was open for 2% of the time, Pallas kernels for 0%

profile of v1, /device:TPU:113, one launch (start us, length us, event | category | flops | bytes accessed | tf_op | source)
XLA Modules:
  0.0 1018.0 jit_solution(445180204571231319)
XLA Ops:
  0.0 0.8 reshape.354
  1.0 30.0 %gather_fusion = bf16[3072,2048]{1,0:T(8,128)(2,1)} fusion(bf16[3072,2048]{1,0:T(8,128)(2,1)} %param.31, s32[3072]{0:T(1024)S(1)} %broadcast_clamp_fusion.1), kind=kCustom, calls=%fused_computation | custom fusion | bytes 25178112 | tf_op jit(solution)/shard_map/gather | solution.py:245
  31.0 6.1 all-to-all-start
  37.2 0.6 dynamic-slice
  38.4 0.2 dynamic-update-slice
  38.6 138.9 %all-reduce = s32[64]{0:T(128)S(1)} all-reduce(s32[64]{0:T(128)S(1)} %dynamic-update-slice), channel_id=2, replica_groups=mesh['dp'=2,'sp'=8] {'sp'}, use_global_device_ids=true, to_apply=%add | all-reduce | flops 64 | bytes 512
  177.6 0.2 reduce_window_sum.33
  177.9 0.8 gather_fusion.1
  178.7 0.8 gather_fusion.2
  179.5 0.6 add_subtract_fusion
  180.1 0.6 copy-done.3
  180.7 0.6 broadcast_add_fusion
  181.5 20.5 %gather_fusion.3 = bf16[1600,2048]{1,0:T(8,128)(2,1)} fusion(bf16[3072,2048]{1,0:T(8,128)(2,1)} %bitcast.4, s32[2048]{0:T(1024)S(1)} %pad_clamp_fusion.2), kind=kCustom, calls=%fused_computation.3 | custom fusion | bytes 13113600 | tf_op jit(solution)/shard_map/gather | solution.py:245
  202.1 7.5 all-to-all-start.1
  209.6 0.2 dynamic-slice_reduce_fusion.4
  209.8 0.6 add_reduce_fusion
  210.5 0.8 gather_fusion.4
  211.3 0.3 dynamic-slice_reduce_fusion.1
  211.8 1.2 copy.40
  213.0 0.2 dynamic-slice_reduce_fusion.3
  213.3 0.8 gather_fusion.6
  214.8 0.6 pad_clamp_fusion
  215.4 2.8 fusion.12
  218.2 1.3 pad_maximum_fusion
  219.5 63.9 %all-to-all-done.1 = bf16[8,200,2048]{2,1,0:T(8,128)(2,1)} async-done(((bf16[8,200,2048]{2,1,0:T(8,128)(2,1)}), bf16[8,200,2048]{2,1,0:T(8,128)(2,1)}, u32[]{:S(2)}, u32[]{:S(2)}) %all-to-all-start.1) | async-done | bytes 6553632 | tf_op jit(solution)/shard_map/all_to_all | solution.py:248
  283.4 16.4 %gather_fusion.5 = bf16[1536,2048]{1,0:T(8,128)(2,1)} fusion(bf16[1600,2048]{1,0:T(8,128)(2,1)} %bitcast.11, s32[2048]{0:T(1024)S(1)} %pad_clamp_fusion.1), kind=kCustom, calls=%fused_computation.5 | custom fusion | bytes 12589056 | tf_op jit(solution)/shard_map/gather | solution.py:245
  299.8 4.1 fusion
  303.9 6.9 fusion.2.h_ref
  310.8 22.5 %qkv.5.v_ref = bf16[1536,2048]{1,0:T(8,128)(2,1)} custom-call(bf16[1536,2048]{1,0:T(8,128)(2,1)} %fusion.2.h_ref, bf16[2048,2048]{1,0:T(8,128)(2,1)} %bitcast.72, f32[1536,128]{1,0:T(8,128)S(1)} %get-tuple-element.31.cos_ref, f32[1536,128]{1,0:T(8,128)S(1)} %get-tuple-element.32.sin_ref), custom_call_target="tpu_custom_call" | custom-call | flops 12884901888 | bytes 20971520 | tf_op jit(solution)/shard_map/qkv/pallas_call | solution.py:39
  333.3 29.4 %qkv.4.k_ref = bf16[1536,2048]{1,0:T(8,128)(2,1)} custom-call(bf16[1536,2048]{1,0:T(8,128)(2,1)} %fusion.2.h_ref, bf16[2048,2048]{1,0:T(8,128)(2,1)} %bitcast.73, f32[1536,128]{1,0:T(8,128)S(1)} %get-tuple-element.31.cos_ref, f32[1536,128]{1,0:T(8,128)S(1)} %get-tuple-element.32.sin_ref), custom_call_target="tpu_custom_call" | custom-call | flops 12884901888 | bytes 20971520 | tf_op jit(solution)/shard_map/qkv/pallas_call | solution.py:39
  362.7 29.1 %qkv.3.q_ref = bf16[1536,2048]{1,0:T(8,128)(2,1)} custom-call(bf16[1536,2048]{1,0:T(8,128)(2,1)} %fusion.2.h_ref, bf16[2048,2048]{1,0:T(8,128)(2,1)} %bitcast.74, f32[1536,128]{1,0:T(8,128)S(1)} %get-tuple-element.31.cos_ref, f32[1536,128]{1,0:T(8,128)S(1)} %get-tuple-element.32.sin_ref), custom_call_target="tpu_custom_call" | custom-call | flops 12884901888 | bytes 20971520 | tf_op jit(solution)/shard_map/qkv/pallas_call | solution.py:39
  391.8 99.1 %attention.1 = bf16[1536,2048]{1,0:T(8,128)(2,1)} custom-call(bf16[1536,2048]{1,0:T(8,128)(2,1)} %qkv.3.q_ref, bf16[1536,2048]{1,0:T(8,128)(2,1)} %qkv.4.k_ref, bf16[1536,2048]{1,0:T(8,128)(2,1)} %qkv.5.v_ref, s32[2,1536]{1,0:T(2,128)} %copy-done.2, s32[1536,2]{1,0:T(8,128)} %bitcast.60), custom_call_target="tpu_custom_call" | custom-call | flops 14495514624 | bytes 25165824 | tf_op jit(solution)/shard_map/attention/pallas_call | solution.py:119
  491.0 18.5 %fusion.4 = (f32[1536]{0:T(1024)S(1)}, bf16[1536,2048]{1,0:T(8,128)(2,1)S(1)}) fusion(bf16[1536,2048]{1,0:T(8,128)(2,1)} %attention.1, bf16[2048,2048]{1,0:T(8,128)(2,1)} %bitcast.75, bf16[1536,2048]{1,0:T(8,128)(2,1)S(1)} %bitcast.55), kind=kOutput, calls=%fused_computation.21 | convolution fusion | flops 12910065664 | bytes 27269120 | tf_op jit(solution)/shard_map/dot_general | solution.py:139
  509.4 2.7 copy-done.18
  512.1 59.7 %fusion.10 = f32[1536,8192]{1,0:T(8,128)} fusion(bf16[2048,8192]{1,0:T(8,128)(2,1)} %param.42, bf16[1536,2048]{1,0:T(8,128)(2,1)S(1)} %get-tuple-element.25, f32[2048]{0:T(1024)S(1)} %convert_element_type.52, f32[1536]{0:T(1024)S(1)} %add_rsqrt_fusion), kind=kOutput, calls=%fused_computation.28 | convolution fusion | flops 51552190464 | bytes 90191872 | tf_op jit(solution)/shard_map/dot_general | solution.py:142
  571.8 68.9 %multiply_convert_fusion.clone.6 = bf16[1536,8192]{1,0:T(8,128)(2,1)} fusion(f32[1536,8192]{1,0:T(8,128)} %fusion.10, bf16[2048,8192]{1,0:T(8,128)(2,1)} %param.43, bf16[1536,2048]{1,0:T(8,128)(2,1)} %copy-done.18, f32[2048]{0:T(1024)S(1)} %convert_element_type.52, f32[1536]{0:T(1024)S(1)} %add_rsqrt_fusion), kind=kOutput, calls=%fused_computation.10.clone.clone.clone.clone.clone.1 | convolution fusion | flops 51627687936 | bytes 115357696 | tf_op jit(solution)/shard_map/dot_general | solution.py:143
  640.7 65.5 %fusion.7 = bf16[1536,2048]{1,0:T(8,128)(2,1)} fusion(bf16[1536,2048]{1,0:T(8,128)(2,1)} %copy-done.18, bf16[8192,2048]{1,0:T(8,128)(2,1)} %param.44, bf16[1536,8192]{1,0:T(8,128)(2,1)} %multiply_convert_fusion.clone.6), kind=kOutput, calls=%fused_computation.24 | convolution fusion | flops 51555336192 | bytes 71303168 | tf_op jit(solution)/shard_map/dot_general | solution.py:145
  706.2 18.1 %gather_fusion.7 = bf16[1600,2048]{1,0:T(8,128)(2,1)} fusion(bf16[1536,2048]{1,0:T(8,128)(2,1)} %fusion.7, s32[2048]{0:T(1024)S(1)} %copy-done.6), kind=kCustom, calls=%fused_computation.7 | custom fusion | bytes 13113600 | tf_op jit(solution)/shard_map/gather | solution.py:245
  724.3 5.7 all-to-all-start.2
  730.3 73.7 %all-to-all-done.2 = bf16[8,200,2048]{2,1,0:T(8,128)(2,1)} async-done(((bf16[8,200,2048]{2,1,0:T(8,128)(2,1)}), bf16[8,200,2048]{2,1,0:T(8,128)(2,1)}, u32[]{:S(2)}, u32[]{:S(2)}) %all-to-all-start.2) | async-done | bytes 6553632 | tf_op jit(solution)/shard_map/all_to_all | solution.py:248
  804.0 27.5 %gather_fusion.8 = bf16[3072,2048]{1,0:T(8,128)(2,1)} fusion(bf16[1600,2048]{1,0:T(8,128)(2,1)} %bitcast.21, s32[3072]{0:T(1024)S(1)} %broadcast_clamp_fusion), kind=kCustom, calls=%fused_computation.8 | custom fusion | bytes 25178112 | tf_op jit(solution)/shard_map/gather | solution.py:245
  831.5 6.4 all-to-all-start.3
  838.0 1.4 fusion.48
  839.3 5.8 sort.17
  845.1 0.7 broadcast_compare_fusion
  845.8 130.7 %all-to-all-done.3 = bf16[8,384,2048]{2,1,0:T(8,128)(2,1)} async-done(((bf16[8,384,2048]{2,1,0:T(8,128)(2,1)}), bf16[8,384,2048]{2,1,0:T(8,128)(2,1)}, u32[]{:S(2)}, u32[]{:S(2)}) %all-to-all-start.3) | async-done | bytes 12582944 | tf_op jit(solution)/shard_map/all_to_all | solution.py:248
  976.5 30.0 %gather_fusion.9 = bf16[3072,2048]{1,0:T(8,128)(2,1)} fusion(bf16[3072,2048]{1,0:T(8,128)(2,1)} %bitcast.24, s32[3072]{0:T(1024)S(1)} %fusion.40), kind=kCustom, calls=%fused_computation.9 | custom fusion | bytes 25178112 | tf_op jit(solution)/shard_map/gather | solution.py:245
  1006.5 11.1 %broadcast_select_fusion = bf16[3072,2048]{1,0:T(8,128)(2,1)} fusion(bf16[3072,2048]{1,0:T(8,128)(2,1)} %gather_fusion.9, pred[3072]{0:T(1024)(128)(4,1)S(1)} %broadcast_compare_fusion), kind=kLoop, calls=%fused_computation.25 | loop fusion | flops 6291456 | bytes 25168896 | tf_op jit(solution)/shard_map/jit(_where)/select_n | solution.py:255
  (92 shorter events, 1.8 us)
Async XLA Ops:
  31.0 6.2 copy-start.17
  31.0 7.4 copy-start.15
  31.0 150.5 %all-to-all-start = ((bf16[8,384,2048]{2,1,0:T(8,128)(2,1)}), bf16[8,384,2048]{2,1,0:T(8,128)(2,1)}, u32[]{:S(2)}, u32[]{:S(2)}) async-start(bf16[8,384,2048]{2,1,0:T(8,128)(2,1)} %bitcast.56), calls=%async_computation | async-start | bytes 25165824 | tf_op jit(solution)/shard_map/all_to_all | solution.py:248
  177.6 32.0 %copy-start = (s32[8,8]{1,0:T(8,128)}, s32[8,8]{1,0:T(8,128)S(1)}, u32[]{:S(2)}) copy-start(s32[8,8]{1,0:T(8,128)S(1)} %reshape.448) | copy-start | bytes 772
  180.1 0.6 copy-start.3
  202.0 7.8 copy-start.5
  202.0 8.4 copy-start.14
  202.0 9.2 copy-start.16
  202.0 9.7 copy-start.10
  202.0 9.7 copy-start.9
  202.1 11.0 %copy-start.11 = (bf16[2048]{0:T(1024)(128)(2,1)S(1)}, bf16[2048]{0:T(1024)(128)(2,1)}, u32[]{:S(2)}) copy-start(bf16[2048]{0:T(1024)(128)(2,1)} %param.41) | copy-start | bytes 12292
  202.1 11.2 %copy-start.13 = (s32[64]{0:T(128)S(1)}, s32[64]{0:T(128)}, u32[]{:S(2)}) copy-start(s32[64]{0:T(128)} %constant.203) | copy-start | bytes 772
  202.1 12.1 %copy-start.12 = (s32[8,8]{1,0:T(8,128)S(1)}, s32[8,8]{1,0:T(8,128)}, u32[]{:S(2)}) copy-start(s32[8,8]{1,0:T(8,128)} %constant.159) | copy-start | bytes 772
  202.1 81.3 %all-to-all-start.1 = ((bf16[8,200,2048]{2,1,0:T(8,128)(2,1)}), bf16[8,200,2048]{2,1,0:T(8,128)(2,1)}, u32[]{:S(2)}, u32[]{:S(2)}) async-start(bf16[8,200,2048]{2,1,0:T(8,128)(2,1)} %bitcast.58), calls=%async_computation.1 | async-start | bytes 13107200 | tf_op jit(solution)/shard_map/all_to_all | solution.py:248
  211.8 88.0 %copy-start.2 = (s32[2,1536]{1,0:T(2,128)}, s32[2,1536]{1,0:T(2,128)S(1)}, u32[]{:S(2)}) copy-start(s32[2,1536]{1,0:T(2,128)S(1)} %pad_add_fusion.meta_row_ref) | copy-start | bytes 36868
  362.7 128.3 %slice-start = ((s8[6291456]{0:T(1024)(128)(4,1)}), s8[4194304]{0:T(1024)(128)(4,1)S(1)}, s32[]{:S(2)}) async-start(s8[6291456]{0:T(1024)(128)(4,1)} %bitcast.54), calls=%async_computation.4 | async-start | bytes 8388608
  391.8 99.1 %slice-start.1 = ((s8[6291456]{0:T(1024)(128)(4,1)}), s8[2097152]{0:T(1024)(128)(4,1)S(1)}, s32[]{:S(2)}) async-start(s8[6291456]{0:T(1024)(128)(4,1)} %bitcast.54), calls=%async_computation.5 | async-start | bytes 4194304
  509.4 2.7 copy-start.18
  640.7 65.5 %copy-start.6 = (s32[2048]{0:T(1024)S(1)}, s32[2048]{0:T(1024)}, u32[]{:S(2)}) copy-start(s32[2048]{0:T(1024)} %pad_clamp_fusion) | copy-start | bytes 24580
  724.3 5.7 copy-start.4
  724.3 5.7 copy-start.7
  724.3 5.7 copy-start.8
  724.3 79.7 %all-to-all-start.2 = ((bf16[8,200,2048]{2,1,0:T(8,128)(2,1)}), bf16[8,200,2048]{2,1,0:T(8,128)(2,1)}, u32[]{:S(2)}, u32[]{:S(2)}) async-start(bf16[8,200,2048]{2,1,0:T(8,128)(2,1)} %bitcast.59), calls=%async_computation.2 | async-start | bytes 13107200 | tf_op jit(solution)/shard_map/all_to_all | solution.py:248
  831.5 7.8 copy-start.1
  831.5 145.0 %all-to-all-start.3 = ((bf16[8,384,2048]{2,1,0:T(8,128)(2,1)}), bf16[8,384,2048]{2,1,0:T(8,128)(2,1)}, u32[]{:S(2)}, u32[]{:S(2)}) async-start(bf16[8,384,2048]{2,1,0:T(8,128)(2,1)} %bitcast.57), calls=%async_computation.3 | async-start | bytes 25165824 | tf_op jit(solution)/shard_map/all_to_all | solution.py:248

commit v2 on v1

--- a/solution.py
+++ b/solution.py
@@ -147,10 +147,12 @@
 
 
 def relay_tables(group):
-    n_relay = group
-    relay_of = np.array([[c for c in range(n_relay)] for i in range(group)])
-    source_of = np.array([[i for i in range(group)] for k in range(group)])
-    residue = np.array([[int(np.where(relay_of[source_of[k, m]] == k)[0][0]) for m in range(n_relay)] for k in range(group)])
+    def at(dev, chips_on, flip):
+        return (dev // 2 + chips_on) % (group // 2) * 2 + (dev % 2 ^ int(flip))
+
+    relay_of = np.array([[at(i, o, f) for o, f in RELAYS] for i in range(group)])
+    source_of = np.array([[at(k, -o, f) for o, f in RELAYS] for k in range(group)])
+    residue = np.array([range(len(RELAYS))] * group)
     return relay_of, source_of, residue
 
 
@@ -186,7 +188,7 @@
     slot = jnp.arange(cap1)
     in_j = (slot[None, None, :] >= first_me[:, :, None]) & (slot[None, None, :] < (first_me + end_me - base_me)[:, :, None])
     back = jnp.arange(group)[None, :, None] * cap2 + base_me[:, :, None] + slot[None, None, :] - first_me[:, :, None]
-    relay_back_idx = jnp.sum(jnp.where(in_j, back, 0), axis=1).reshape(-1)
+    relay_back_idx = jnp.sum(jnp.where(in_j, back + 1, 0), axis=1).reshape(-1) - 1
 
     len_me = lax.dynamic_index_in_dim(len_ij, me, 1, keepdims=False)
     off_me = lax.dynamic_index_in_dim(off_ij, me, 1, keepdims=False)
@@ -214,12 +216,116 @@
     u_km = r_km + (roff_me - off_me)[source_of][:, :, None]
     dest_back_idx = jnp.sum(jnp.where(in_km, u_km, 0), axis=1).reshape(-1)
 
-    used = jnp.sum(lax.dynamic_index_in_dim(len_ij, me, 0, keepdims=False))
-    r = jnp.arange(cap1)[None, :] * n_relay + res[:, None]
     send_idx = jnp.pad(tok_perm, (0, cap1 * n_relay - n_tok)).reshape(cap1, n_relay).T.reshape(-1)
     inv_perm = jnp.argsort(tok_perm)
     final_idx = lax.rem(inv_perm, n_relay) * cap1 + inv_perm // n_relay
-    return send_idx, relay_idx, dest_idx, dest_back_idx, relay_back_idx, final_idx, inv_perm < used
+    return send_idx, relay_idx, dest_idx, dest_back_idx, relay_back_idx, final_idx
+
+
+N_TILE = 512
+RELAYS = ((0, False), (0, True), (1, False), (1, True), (-1, False), (-1, True))
+NEAR_ORDER = (2, 4, 3, 5, 1, 0)
+FAR_ORDER = ((2, False), (1, False), (-1, False), (2, True), (1, True), (-1, True), (0, True), (0, False))
+
+
+def peer(me, group, chips_on, flip):
+    n_chips = group // 2
+    chip = lax.rem(me // 2 + chips_on + n_chips, n_chips)
+    core = lax.rem(me, 2)
+    if flip:
+        core = 1 - core
+    return chip * 2 + core
+
+
+def build_pick(idx_ref, at, pick_ref, n_src):
+    lane = lax.broadcasted_iota(jnp.int32, (at.size, n_src), 1)
+    pick_ref[:at.size, :n_src] = (idx_ref[at, :] == lane).astype(jnp.float32).astype(pick_ref.dtype)
+
+
+def gather_rows(src_ref, pick_ref, dst_ref, dst_at):
+    n_src, width = src_ref.shape
+
+    @pl.loop(0, width // N_TILE)
+    def _(n):
+        cols = pl.ds(pl.multiple_of(n * N_TILE, N_TILE), N_TILE)
+        rows = jnp.dot(pick_ref[:dst_at.size, :n_src], src_ref[:, cols], preferred_element_type=jnp.float32)
+        dst_ref[dst_at, cols] = rows.astype(dst_ref.dtype)
+
+
+def hop(src_ref, idx_ref, pick_ref, buf_ref, land_ref, land_local, cap, targets, send_sem, recv_sem):
+    copies = []
+    for t, (dev, block, slot) in enumerate(targets):
+        build_pick(idx_ref, pl.ds(pl.multiple_of(block * cap, 16), cap), pick_ref, src_ref.shape[0])
+        if copies:
+            copies[-1].start()
+        here = pl.ds(t * cap, cap)
+        there = pl.ds(pl.multiple_of(slot * cap, 16), cap)
+        if dev is None and land_local:
+            gather_rows(src_ref, pick_ref, land_ref, there)
+            continue
+        gather_rows(src_ref, pick_ref, buf_ref, here)
+        if dev is None:
+            copies.append(pltpu.make_async_copy(buf_ref.at[here, :], land_ref.at[there, :], recv_sem.at[t]))
+        else:
+            copies.append(pltpu.make_async_remote_copy(
+                src_ref=buf_ref.at[here, :],
+                dst_ref=land_ref.at[there, :],
+                send_sem=send_sem.at[t],
+                recv_sem=recv_sem.at[t],
+                device_id={'sp': dev},
+                device_id_type=pl.DeviceIdType.MESH,
+            ))
+    if not land_local:
+        copies[-1].start()
+    for copy in copies:
+        copy.wait()
+
+
+def two_hop_kernel(group, near_first, cap_a, cap_b, src_ref, idx_a_ref, idx_b_ref, out_ref, pick_ref, buf_a_ref, mid_ref, buf_b_ref, sem_a_send, sem_a_recv, sem_b_send, sem_b_recv):
+    me = lax.axis_index('sp')
+    barrier = pltpu.get_barrier_semaphore()
+    for other in range(1, group):
+        pl.semaphore_signal(barrier, inc=1, device_id={'sp': lax.rem(me + other, group)}, device_id_type=pl.DeviceIdType.MESH)
+    pl.semaphore_wait(barrier, group - 1)
+    near = []
+    sign = 1 if near_first else -1
+    for block in NEAR_ORDER:
+        chips_on, flip = RELAYS[block]
+        dev = None if (chips_on == 0 and not flip) else peer(me, group, sign * chips_on, flip)
+        near.append((dev, block, block))
+    far = []
+    for chips_on, flip in FAR_ORDER:
+        dev = peer(me, group, chips_on, flip)
+        far.append((None if (chips_on == 0 and not flip) else dev, dev, me))
+    first, second = (near, far) if near_first else (far, near)
+    hop(src_ref, idx_a_ref, pick_ref, buf_a_ref, mid_ref, True, cap_a, first, sem_a_send, sem_a_recv)
+    hop(mid_ref, idx_b_ref, pick_ref, buf_b_ref, out_ref, False, cap_b, second, sem_b_send, sem_b_recv)
+
+
+def two_hop(src, idx_a, idx_b, group, near_first, collective_id):
+    n_src, width = src.shape
+    n_a = len(RELAYS) if near_first else group
+    n_b = group if near_first else len(RELAYS)
+    rows_a, rows_b = idx_a.shape[0], idx_b.shape[0]
+    vmem = pl.BlockSpec(memory_space=pltpu.VMEM)
+    return pl.pallas_call(
+        functools.partial(two_hop_kernel, group, near_first, rows_a // n_a, rows_b // n_b),
+        out_shape=jax.ShapeDtypeStruct((rows_b, width), src.dtype),
+        in_specs=[vmem, vmem, vmem],
+        out_specs=pl.BlockSpec(memory_space=pl.ANY),
+        scratch_shapes=[
+            pltpu.VMEM((max(rows_a // n_a, rows_b // n_b), max(n_src, rows_a)), src.dtype),
+            pltpu.VMEM((rows_a, width), src.dtype),
+            pltpu.VMEM((rows_a, width), src.dtype),
+            pltpu.VMEM((rows_b, width), src.dtype),
+            pltpu.SemaphoreType.DMA((n_a,)),
+            pltpu.SemaphoreType.DMA((n_a,)),
+            pltpu.SemaphoreType.DMA((n_b,)),
+            pltpu.SemaphoreType.DMA((n_b,)),
+        ],
+        compiler_params=pltpu.CompilerParams(collective_id=collective_id, has_side_effects=True, vmem_limit_bytes=60 * 1024 * 1024),
+        name="two_hop_out" if near_first else "two_hop_back",
+    )(src, idx_a[:, None], idx_b[:, None])
 
 
 def solution(mesh):
@@ -235,23 +341,19 @@
         n_relay = relay_of.shape[1]
         cap1 = -(-n_tok // n_relay)
         cap2 = -(-(n_cap + n_relay * (n_relay - 1)) // n_relay)
-        cap2 = -(-cap2 // 8) * 8
+        cap2 = -(-cap2 // 16) * 16
         me = lax.axis_index('sp')
         len_ij = lax.all_gather(send_len, 'sp')
-        send_idx, relay_idx, dest_idx, dest_back_idx, relay_back_idx, final_idx, was_sent = plan_indices(
+        send_idx, relay_idx, dest_idx, dest_back_idx, relay_back_idx, final_idx = plan_indices(
             me, len_ij, tok_perm, n_tok, n_cap, cap1, cap2, relay_of, source_of, residue)
 
         def take(rows, index):
             return rows.at[index].get(mode='promise_in_bounds')
 
-        def exchange(rows, cap):
-            return lax.all_to_all(rows.reshape(-1, cap, model_dim), 'sp', 0, 0, tiled=True).reshape(-1, model_dim)
-
-        relay_rows = exchange(take(hidden, send_idx), cap1)
-        dest_rows = take(exchange(take(relay_rows, relay_idx), cap2), dest_idx)
+        out_at_dest = two_hop(hidden, send_idx, relay_idx, group, True, 0)
+        dest_rows = take(out_at_dest, dest_idx)
         out_rows = layer(dest_rows, recv_doc, recv_pos, g_attn, w_q, w_k, w_v, w_o, g_mlp, w_gate, w_up, w_down)
-        relay_back = exchange(take(out_rows, dest_back_idx), cap2)
-        src_back = exchange(take(relay_back, relay_back_idx), cap1)
-        return jnp.where(was_sent[:, None], take(src_back, final_idx), jnp.zeros((), hidden.dtype))
+        src_back = two_hop(out_rows, dest_back_idx, relay_back_idx, group, False, 1)
+        return take(src_back, final_idx)
 
     return jax.shard_map(per_device, mesh=mesh, in_specs=(row_spec,) + (vec_spec,) * 7 + (rep_spec,) * 9, out_specs=row_spec, check_vma=False)

time: 1030 us -> 936 us (0.909)
  Pallas kernels: 180 us -> 612 us
  waiting for transfers between devices: 268 us -> 0 us
  blocking collectives: 139 us -> 8.9 us
  local copies, waits for them, and re-layouts: 153 us -> 67 us
  starting transfers between devices: 25.8 us -> 0 us
  other arithmetic: 37.4 us -> 24.9 us
    pallas_call x0 -> x2, Pallas kernels: none -> 432 us  [two_hop(): pl.pallas_call(functools.partial(two_hop_kernel, group, near_first, rows_...]
    all_to_all x4 -> x0, waiting for transfers between devices: 268 us -> none  [exchange(): lax.all_to_all(rows.reshape(-1, cap, model_dim), 'sp', 0, 0, tiled=True)]
    unnamed x1, blocking collectives: 139 us -> 8.9 us
    gather x6 -> x2, local copies, waits for them, and re-layouts: 143 us -> 47.6 us  [take(): return rows.at[index].get(mode='promise_in_bounds')]
    all_to_all x4 -> x0, starting transfers between devices: 25.8 us -> none  [exchange(): lax.all_to_all(rows.reshape(-1, cap, model_dim), 'sp', 0, 0, tiled=True)]
    select_n x1 -> x0, other arithmetic: 11.1 us -> none  [per_device(): jnp.where(was_sent[:, None], take(src_back, final_idx), jnp.zeros((), hid...]
  transfers between devices with their start and end apart: 4 -> 0, of which waited for: 3 -> 0; matrix products, arithmetic and copies ran while one was open for 2% -> 0% of each run, Pallas kernels for 0% -> 0%
where the time goes in v2:
time: 936 us; the launch traced here: 927 us
  Pallas kernels  612 us (65%)
  matrix products  213 us (23%)
  local copies, waits for them, and re-layouts  67 us (7%)
  other arithmetic  24.9 us (3%)
    pallas_call x2, Pallas kernels, two_hop(): pl.pallas_call(functools.partial(two_hop_kernel, group, near_first, rows_...  432 us
    pallas_call x1, Pallas kernels, attention(): pl.pallas_call(functools.partial(attn_kernel, head_dim), out_shape=jax.Sh...  99.3 us
    pallas_call x3, Pallas kernels, qkv_proj(): pl.pallas_call(functools.partial(qkv_one, head_dim, kind), out_shape=jax....  80.8 us
    dot_general x1, matrix products, layer(): up_proj = jnp.dot(normed_mlp, w_up, preferred_element_type=jnp.float32)  68.8 us
    dot_general x1, matrix products, layer(): jnp.dot(hidden_act, w_down, preferred_element_type=jnp.float32)  65.4 us
    dot_general x1, matrix products, layer(): gate_proj = jnp.dot(normed_mlp, w_gate, preferred_element_type=jnp.float32)  60 us
    gather x2, local copies, waits for them, and re-layouts, take(): return rows.at[index].get(mode='promise_in_bounds')  47.6 us

profile of v2, /device:TPU:113, one launch (start us, length us, event | category | flops | bytes accessed | tf_op | source)
XLA Modules:
  0.0 927.1 jit_solution(11877091230122199745)
XLA Ops:
  0.0 1.2 dynamic-slice
  1.9 0.9 dynamic-update-slice
  2.8 8.9 all-reduce
  11.7 0.2 reduce_window_sum.33
  12.0 0.9 gather_fusion
  13.1 1.3 reduce_window_sum.34
  14.4 0.9 gather_fusion.1
  15.7 0.6 add_subtract_fusion
  16.3 0.1 select_reduce_fusion.3
  16.4 1.5 broadcast_in_dim_reshape.14.idx_b_ref
  17.9 0.9 reshape.207
  18.8 0.1 copy.73
  19.0 1.7 copy.91
  20.7 220.9 %two_hop_out.1 = bf16[2176,2048]{1,0:T(8,128)(2,1)} custom-call(bf16[3072,2048]{1,0:T(8,128)(2,1)} %src_ref.1, s32[3072,1]{1,0:T(8,128)} %bitcast.56, s32[2176,1]{1,0:T(8,128)} %broadcast_in_dim_reshape.14.idx_b_ref), custom_call_target="tpu_custom_call" | custom-call | tf_op jit(solution)/shard_map/two_hop_out/pallas_call | solution.py:311
  241.5 0.2 dynamic-slice_reduce_fusion
  241.7 0.2 dynamic-slice_reduce_fusion.1
  241.9 0.6 fusion.43
  242.5 0.1 fusion.16
  242.7 0.6 add_bitcast_fusion.1
  243.4 0.8 gather_fusion.2
  244.3 0.1 copy.81
  244.5 0.1 select_reduce_fusion
  244.7 17.5 %gather_fusion.3 = bf16[1536,2048]{1,0:T(8,128)(2,1)} fusion(bf16[2176,2048]{1,0:T(8,128)(2,1)} %two_hop_out.1, s32[2048]{0:T(1024)S(1)} %pad_clamp_fusion), kind=kCustom, calls=%fused_computation.3 | custom fusion | bytes 12589056 | tf_op jit(solution)/shard_map/gather | solution.py:351
  262.3 4.1 fusion
  266.4 6.9 fusion.2.h_ref
  273.3 2.8 fusion.12
  276.2 1.3 pad_maximum_fusion
  277.4 22.5 %qkv.5.v_ref = bf16[1536,2048]{1,0:T(8,128)(2,1)} custom-call(bf16[1536,2048]{1,0:T(8,128)(2,1)} %fusion.2.h_ref, bf16[2048,2048]{1,0:T(8,128)(2,1)} %bitcast.67, f32[1536,128]{1,0:T(8,128)S(1)} %get-tuple-element.31.cos_ref, f32[1536,128]{1,0:T(8,128)S(1)} %get-tuple-element.32.sin_ref), custom_call_target="tpu_custom_call" | custom-call | flops 12884901888 | bytes 20971520 | tf_op jit(solution)/shard_map/qkv/pallas_call | solution.py:39
  299.9 29.1 %qkv.4.k_ref = bf16[1536,2048]{1,0:T(8,128)(2,1)} custom-call(bf16[1536,2048]{1,0:T(8,128)(2,1)} %fusion.2.h_ref, bf16[2048,2048]{1,0:T(8,128)(2,1)} %bitcast.68, f32[1536,128]{1,0:T(8,128)S(1)} %get-tuple-element.31.cos_ref, f32[1536,128]{1,0:T(8,128)S(1)} %get-tuple-element.32.sin_ref), custom_call_target="tpu_custom_call" | custom-call | flops 12884901888 | bytes 20971520 | tf_op jit(solution)/shard_map/qkv/pallas_call | solution.py:39
  329.0 29.3 %qkv.3.q_ref = bf16[1536,2048]{1,0:T(8,128)(2,1)} custom-call(bf16[1536,2048]{1,0:T(8,128)(2,1)} %fusion.2.h_ref, bf16[2048,2048]{1,0:T(8,128)(2,1)} %bitcast.69, f32[1536,128]{1,0:T(8,128)S(1)} %get-tuple-element.31.cos_ref, f32[1536,128]{1,0:T(8,128)S(1)} %get-tuple-element.32.sin_ref), custom_call_target="tpu_custom_call" | custom-call | flops 12884901888 | bytes 20971520 | tf_op jit(solution)/shard_map/qkv/pallas_call | solution.py:39
  358.4 1.2 copy.83
  359.6 99.3 %attention.1 = bf16[1536,2048]{1,0:T(8,128)(2,1)} custom-call(bf16[1536,2048]{1,0:T(8,128)(2,1)} %qkv.3.q_ref, bf16[1536,2048]{1,0:T(8,128)(2,1)} %qkv.4.k_ref, bf16[1536,2048]{1,0:T(8,128)(2,1)} %qkv.5.v_ref, s32[2,1536]{1,0:T(2,128)} %copy-done.3, s32[1536,2]{1,0:T(8,128)} %bitcast.59), custom_call_target="tpu_custom_call" | custom-call | flops 14495514624 | bytes 25165824 | tf_op jit(solution)/shard_map/attention/pallas_call | solution.py:119
  458.9 18.5 %fusion.4 = (f32[1536]{0:T(1024)S(1)}, bf16[1536,2048]{1,0:T(8,128)(2,1)S(1)}) fusion(bf16[1536,2048]{1,0:T(8,128)(2,1)} %attention.1, bf16[2048,2048]{1,0:T(8,128)(2,1)} %bitcast.70, bf16[1536,2048]{1,0:T(8,128)(2,1)S(1)} %bitcast.55), kind=kOutput, calls=%fused_computation.17 | convolution fusion | flops 12910065664 | bytes 27269120 | tf_op jit(solution)/shard_map/dot_general | solution.py:139
  477.5 2.7 copy-done.19
  480.1 60.0 %fusion.10 = f32[1536,8192]{1,0:T(8,128)} fusion(bf16[2048,8192]{1,0:T(8,128)(2,1)} %param.42, bf16[1536,2048]{1,0:T(8,128)(2,1)S(1)} %get-tuple-element.26, f32[2048]{0:T(1024)S(1)} %convert_element_type.52, f32[1536]{0:T(1024)S(1)} %add_rsqrt_fusion), kind=kOutput, calls=%fused_computation.23 | convolution fusion | flops 51552190464 | bytes 90191872 | tf_op jit(solution)/shard_map/dot_general | solution.py:142
  540.1 68.8 %multiply_convert_fusion.clone.6 = bf16[1536,8192]{1,0:T(8,128)(2,1)} fusion(f32[1536,8192]{1,0:T(8,128)} %fusion.10, bf16[2048,8192]{1,0:T(8,128)(2,1)} %param.43, bf16[1536,2048]{1,0:T(8,128)(2,1)} %copy-done.19, f32[2048]{0:T(1024)S(1)} %convert_element_type.52, f32[1536]{0:T(1024)S(1)} %add_rsqrt_fusion), kind=kOutput, calls=%fused_computation.6.clone.clone.clone.clone.clone.1 | convolution fusion | flops 51627687936 | bytes 115357696 | tf_op jit(solution)/shard_map/dot_general | solution.py:143
  609.0 65.4 %fusion.7.src_ref = bf16[1536,2048]{1,0:T(8,128)(2,1)} fusion(bf16[1536,2048]{1,0:T(8,128)(2,1)} %copy-done.19, bf16[8192,2048]{1,0:T(8,128)(2,1)} %param.44, bf16[1536,8192]{1,0:T(8,128)(2,1)} %multiply_convert_fusion.clone.6), kind=kOutput, calls=%fused_computation.20 | convolution fusion | flops 51555336192 | bytes 71303168 | tf_op jit(solution)/shard_map/dot_general | solution.py:145
  674.5 0.1 select_reduce_fusion.1
  674.6 1.7 copy.93
  676.4 0.8 gather_fusion.4
  677.2 0.1 copy.87
  677.5 0.7 dynamic-slice_bitcast_fusion
  678.2 0.1 copy.86
  678.2 0.1 select_reduce_fusion.2
  678.4 1.4 broadcast_in_dim_reshape.15.idx_a_ref
  679.8 211.1 %two_hop_back.1 = bf16[3072,2048]{1,0:T(8,128)(2,1)} custom-call(bf16[1536,2048]{1,0:T(8,128)(2,1)} %fusion.7.src_ref, s32[2176,1]{1,0:T(8,128)} %broadcast_in_dim_reshape.15.idx_a_ref, s32[3072,1]{1,0:T(8,128)} %bitcast.57), custom_call_target="tpu_custom_call" | custom-call | tf_op jit(solution)/shard_map/two_hop_back/pallas_call | solution.py:311
  890.9 5.8 sort.17
  896.7 30.0 %gather_fusion.5 = bf16[3072,2048]{1,0:T(8,128)(2,1)} fusion(bf16[3072,2048]{1,0:T(8,128)(2,1)} %two_hop_back.1, s32[3072]{0:T(1024)S(1)} %fusion.36), kind=kCustom, calls=%fused_computation.5 | custom fusion | bytes 25178112 | tf_op jit(solution)/shard_map/gather | solution.py:351
  (90 shorter events, 1.6 us)
Async XLA Ops:
  15.5 0.9 copy-start.1
  15.7 0.6 copy-start.4
  19.0 224.4 %copy-start.17 = (s32[48]{0:T(128)S(1)}, s32[48]{0:T(128)}, u32[]{:S(2)}) copy-start(s32[48]{0:T(128)} %constant.178) | copy-start | bytes 580
  20.7 223.5 %copy-start.18 = (s32[48]{0:T(128)S(1)}, s32[48]{0:T(128)}, u32[]{:S(2)}) copy-start(s32[48]{0:T(128)} %constant.180) | copy-start | bytes 580
  243.3 19.0 %copy-start.6 = (s32[8,6,1]{1,0,2:T(8,128)}, s32[8,6,1]{1,0,2:T(8,128)S(1)}, u32[]{:S(2)}) copy-start(s32[8,6,1]{1,0,2:T(8,128)S(1)} %get-tuple-element.10) | copy-start | bytes 580
  244.7 21.7 %copy-start.13 = (bf16[2048]{0:T(1024)(128)(2,1)S(1)}, bf16[2048]{0:T(1024)(128)(2,1)}, u32[]{:S(2)}) copy-start(bf16[2048]{0:T(1024)(128)(2,1)} %param.36) | copy-start | bytes 12292
  262.3 11.0 %copy-start.8 = (s32[1536]{0:T(1024)S(1)}, s32[1536]{0:T(1024)}, u32[]{:S(2)}) copy-start(s32[1536]{0:T(1024)} %param.35) | copy-start | bytes 18436
  329.0 29.3 %copy-start.12 = (s32[1536]{0:T(1024)S(1)}, s32[1536]{0:T(1024)}, u32[]{:S(2)}) copy-start(s32[1536]{0:T(1024)} %param.34) | copy-start | bytes 18436
  329.0 129.9 %slice-start = ((s8[6291456]{0:T(1024)(128)(4,1)}), s8[2097152]{0:T(1024)(128)(4,1)S(1)}, s32[]{:S(2)}) async-start(s8[6291456]{0:T(1024)(128)(4,1)} %bitcast.54), calls=%async_computation | async-start | bytes 4194304
  358.3 1.3 copy-start.3
  359.6 99.3 %slice-start.1 = ((s8[6291456]{0:T(1024)(128)(4,1)}), s8[4194304]{0:T(1024)(128)(4,1)S(1)}, s32[]{:S(2)}) async-start(s8[6291456]{0:T(1024)(128)(4,1)} %bitcast.54), calls=%async_computation.1 | async-start | bytes 8388608
  458.9 18.5 %copy-start.14 = (bf16[2048]{0:T(1024)(128)(2,1)S(1)}, bf16[2048]{0:T(1024)(128)(2,1)}, u32[]{:S(2)}) copy-start(bf16[2048]{0:T(1024)(128)(2,1)} %param.41) | copy-start | bytes 12292
  477.4 2.7 copy-start.19
  609.0 65.5 %copy-start.5 = (s32[1,6,8]{2,1,0:T(8,128)S(1)}, s32[1,6,8]{2,1,0:T(8,128)}, u32[]{:S(2)}) copy-start(s32[1,6,8]{2,1,0:T(8,128)} %copy-done.4) | copy-start | bytes 580
  609.0 65.5 %copy-start.9 = (s32[6,8]{1,0:T(8,128)S(1)}, s32[6,8]{1,0:T(8,128)}, u32[]{:S(2)}) copy-start(s32[6,8]{1,0:T(8,128)} %get-tuple-element.16) | copy-start | bytes 580
  609.0 65.5 %copy-start.10 = (s32[6,8]{1,0:T(8,128)S(1)}, s32[6,8]{1,0:T(8,128)}, u32[]{:S(2)}) copy-start(s32[6,8]{1,0:T(8,128)} %get-tuple-element.17) | copy-start | bytes 580
  609.0 67.4 %copy-start.16 = (s32[48]{0:T(128)S(1)}, s32[48]{0:T(128)}, u32[]{:S(2)}) copy-start(s32[48]{0:T(128)} %constant.179) | copy-start | bytes 580
  609.0 67.4 %copy-start = (s32[8]{0:T(128)S(1)}, s32[8]{0:T(128)}, u32[]{:S(2)}) copy-start(s32[8]{0:T(128)} %get-tuple-element.23) | copy-start | bytes 100
  609.0 68.3 %copy-start.7 = (s32[8,6,1]{1,0,2:T(8,128)S(1)}, s32[8,6,1]{1,0,2:T(8,128)}, u32[]{:S(2)}) copy-start(s32[8,6,1]{1,0,2:T(8,128)} %copy-done.6) | copy-start | bytes 580
  609.0 68.4 %copy-start.11 = (s32[8,6]{1,0:T(8,128)S(1)}, s32[8,6]{1,0:T(8,128)}, u32[]{:S(2)}) copy-start(s32[8,6]{1,0:T(8,128)} %get-tuple-element.9) | copy-start | bytes 580
  609.0 69.2 %copy-start.15 = (s32[8,6]{0,1:T(8,128)S(1)}, s32[8,6]{0,1:T(8,128)}, u32[]{:S(2)}) copy-start(s32[8,6]{0,1:T(8,128)} %constant.135) | copy-start | bytes 580
  676.4 214.5 %copy-start.2 = (s32[3072]{0:T(1024)S(1)}, s32[3072]{0:T(1024)}, u32[]{:S(2)}) copy-start(s32[3072]{0:T(1024)} %param.32) | copy-start | bytes 36868

commit v3 on v2

v3 whole, which is shorter than its diff:
```python
import functools

import jax
import jax.numpy as jnp
import numpy as np
from jax import lax
from jax.experimental import pallas as pl
from jax.experimental.pallas import tpu as pltpu
from jax.sharding import PartitionSpec as P

ROPE_BASE = 500000.0
NORM_EPS = 1e-5
Q_TILE = 256
QKV_TILE = 256


def rms_norm(rows_in, gain_vec):
    rows_f = rows_in.astype(jnp.float32)
    inv_rms = lax.rsqrt(jnp.mean(rows_f * rows_f, axis=-1, keepdims=True) + NORM_EPS)
    return (rows_f * inv_rms * gain_vec.astype(jnp.float32)).astype(jnp.bfloat16)


def rope_tables(positions, head_dim):
    half = head_dim // 2
    inv_freq = jnp.power(jnp.float32(ROPE_BASE), -2.0 * jnp.arange(half, dtype=jnp.float32) / head_dim)
    angles = positions.astype(jnp.float32)[:, None] * inv_freq[None, :]
    cos_t = jnp.cos(angles)
    sin_t = jnp.sin(angles)
    return jnp.concatenate([cos_t] * 4, axis=1), jnp.concatenate([-sin_t, sin_t] * 2, axis=1)


def qkv_proj(normed, w_q, w_k, w_v, cos_t, sin_t):
    rows, model_dim = normed.shape
    n_heads, head_dim = w_q.shape[1:]
    width = n_heads * head_dim
    w_all = [w.transpose(1, 2, 0).reshape(width, model_dim) for w in (w_q, w_k, w_v)]
    outs = []
    for kind, w in enumerate(w_all):
        outs.append(pl.pallas_call(
            functools.partial(qkv_one, head_dim, kind),
            out_shape=jax.ShapeDtypeStruct((rows, width), jnp.bfloat16),
            grid=(width // QKV_TILE,),
            in_specs=[
                pl.BlockSpec((rows, model_dim), lambda n: (0, 0), pipeline_mode=pl.Buffered(1)),
                pl.BlockSpec((QKV_TILE, model_dim), lambda n: (n, 0)),
                pl.BlockSpec(cos_t.shape, lambda n: (0, 0), pipeline_mode=pl.Buffered(1)),
                pl.BlockSpec(sin_t.shape, lambda n: (0, 0), pipeline_mode=pl.Buffered(1)),
            ],
            out_specs=pl.BlockSpec((rows, QKV_TILE), lambda n: (0, n)),
            compiler_params=pltpu.CompilerParams(vmem_limit_bytes=48 * 1024 * 1024),
            cost_estimate=pl.CostEstimate(flops=2 * rows * model_dim * width, bytes_accessed=2 * (2 * rows * model_dim + model_dim * width), transcendentals=0),
            name="qkv",
        )(normed, w, cos_t, sin_t))
    return outs


def qkv_one(head_dim, kind, h_ref, w_ref, cos_ref, sin_ref, o_ref):
    lanes = cos_ref.shape[1]
    half = head_dim // 2
    acc = lax.dot_general(h_ref[...], w_ref[...], (((1,), (1,)), ((), ())), preferred_element_type=jnp.float32)
    if kind == 2:
        o_ref[...] = acc.astype(o_ref.dtype)
        return
    first = lax.rem(lax.broadcasted_iota(jnp.int32, (1, lanes), 1), head_dim) < half
    for b in range(o_ref.shape[1] // lanes):
        x = acc[:, b * lanes:(b + 1) * lanes]
        swapped = jnp.where(first, pltpu.roll(x, lanes - half, 1), pltpu.roll(x, half, 1))
        rot = x * cos_ref[...] + swapped * sin_ref[...]
        if kind == 0:
            rot = rot * (head_dim ** -0.5)
        o_ref[:, b * lanes:(b + 1) * lanes] = rot.astype(o_ref.dtype)


def attn_kernel(head_dim, q_ref, k_ref, v_ref, meta_row_ref, meta_col_ref, o_ref, bias_ref):
    rows, lanes = q_ref.shape
    n_tiles = rows // Q_TILE

    @pl.when(pl.program_id(0) == 0)
    def _():
        for t in range(n_tiles):
            at = slice(t * Q_TILE, (t + 1) * Q_TILE)
            n_keys = (t + 1) * Q_TILE
            ok = (meta_col_ref[at, 0:1] == meta_row_ref[0:1, :n_keys]) & (meta_row_ref[1:2, :n_keys] <= meta_col_ref[at, 1:2])
            bias_ref[at, :n_keys] = jnp.where(ok, 0.0, -1e30).astype(jnp.float32)

    low = lax.broadcasted_iota(jnp.int32, (Q_TILE, lanes), 1) < head_dim

    def scores(t):
        q = q_ref[t * Q_TILE:(t + 1) * Q_TILE, :]
        zero = jnp.zeros((), q.dtype)
        both = jnp.concatenate([jnp.where(low, q, zero), jnp.where(low, zero, q)], axis=0)
        return lax.dot_general(both, k_ref[:(t + 1) * Q_TILE, :], (((1,), (1,)), ((), ())), preferred_element_type=jnp.float32)

    def outputs(t, s):
        at = slice(t * Q_TILE, (t + 1) * Q_TILE)
        n_keys = (t + 1) * Q_TILE
        s = s.reshape(2, Q_TILE, n_keys) + bias_ref[at, :n_keys][None]
        e = jnp.exp(s - jnp.max(s, axis=2, keepdims=True))
        total = jnp.sum(e, axis=2, keepdims=True)
        o = jnp.dot(e.astype(jnp.bfloat16).reshape(2 * Q_TILE, n_keys), v_ref[:n_keys, :], preferred_element_type=jnp.float32)
        o = o.reshape(2, Q_TILE, lanes) / total
        o_ref[at, :] = jnp.where(low, o[0], o[1]).astype(o_ref.dtype)

    ahead = scores(0)
    for t in range(n_tiles):
        s = ahead
        if t + 1 < n_tiles:
            ahead = scores(t + 1)
        outputs(t, s)


def attention(q, k, v, doc_ids, positions, head_dim):
    rows, width = q.shape
    lanes = 2 * head_dim
    meta = jnp.stack([doc_ids, positions])
    head_spec = pl.BlockSpec((rows, lanes), lambda n: (0, n))
    whole = lambda a: pl.BlockSpec(a.shape, lambda n: (0, 0))
    meta_t = meta.T
    return pl.pallas_call(
        functools.partial(attn_kernel, head_dim),
        out_shape=jax.ShapeDtypeStruct((rows, width), jnp.bfloat16),
        grid=(width // lanes,),
        in_specs=[head_spec, head_spec, head_spec, whole(meta), whole(meta_t)],
        out_specs=head_spec,
        scratch_shapes=[pltpu.VMEM((rows, rows), jnp.float32)],
        compiler_params=pltpu.CompilerParams(vmem_limit_bytes=56 * 1024 * 1024),
        cost_estimate=pl.CostEstimate(flops=3 * rows * rows * width, bytes_accessed=8 * rows * width, transcendentals=rows * rows * width // 128),
        name="attention",
    )(q, k, v, meta, meta_t)


def attn_layer(dest_rows, doc_ids, positions, g_attn, w_q, w_k, w_v, w_o):
    model_dim = dest_rows.shape[1]
    n_heads, head_dim = w_q.shape[1:]
    cos_t, sin_t = rope_tables(positions, head_dim)
    normed = rms_norm(dest_rows, g_attn)
    q, k, v = qkv_proj(normed, w_q, w_k, w_v, cos_t, sin_t)
    attn_heads = attention(q, k, v, doc_ids, positions, head_dim)
    attn_out = jnp.dot(attn_heads, w_o.reshape(n_heads * head_dim, model_dim), preferred_element_type=jnp.float32).astype(jnp.bfloat16)
    return (dest_rows.astype(jnp.float32) + attn_out.astype(jnp.float32)).astype(jnp.bfloat16)


def relay_tables(group):
    def at(dev, chips_on, flip):
        return (dev // 2 + chips_on) % (group // 2) * 2 + (dev % 2 ^ int(flip))

    relay_of = np.array([[at(i, o, f) for o, f in RELAYS] for i in range(group)])
    source_of = np.array([[at(k, -o, f) for o, f in RELAYS] for k in range(group)])
    return relay_of, source_of


def ceil_div(a, b):
    return -((-a) // b)


def pick(table, index, n):
    return jnp.sum(jnp.where(index[:, None] == jnp.arange(n)[None, :], table[None, :], 0), axis=1)


def run_tables(len_ij, n_classes):
    off_ij = jnp.cumsum(len_ij, axis=1) - len_ij
    res = np.arange(n_classes)
    first = ceil_div(off_ij[:, None, :] - res[None, :, None], n_classes)
    count = ceil_div((off_ij + len_ij)[:, None, :] - res[None, :, None], n_classes) - first
    return first, count


def out_indices(me, len_ij, tok_perm, n_cap, cap1, cap2, relay_of, source_of):
    group, n_relay = relay_of.shape
    off_ij = jnp.cumsum(len_ij, axis=1) - len_ij
    roff_ij = jnp.cumsum(len_ij, axis=0) - len_ij
    first, count = run_tables(len_ij, n_relay)
    res = np.arange(n_relay)
    first_k = first[source_of, res]
    count_k = count[source_of, res]
    base_k = jnp.cumsum(count_k, axis=1) - count_k

    def mine(t, axis=0):
        return lax.dynamic_index_in_dim(t, me, axis, keepdims=False)

    base_me, count_me, first_me = mine(base_k), mine(count_k), mine(first_k)
    q = jnp.arange(cap2)
    in_m = (q >= base_me[:, :, None]) & (q < (base_me + count_me)[:, :, None])
    src = np.arange(n_relay)[:, None, None] * cap1 + first_me[:, :, None] + q - base_me[:, :, None]
    relay_idx = jnp.sum(jnp.where(in_m, src, 0), axis=0).reshape(-1)

    len_me, off_me, roff_me = mine(len_ij, 1), mine(off_ij, 1), mine(roff_ij, 1)
    base_to_me, first_to_me = mine(base_k, 2), mine(first, 2)
    place = np.zeros((group, n_relay), np.int32)
    place[source_of, res] = np.arange(group)[:, None] * n_relay + res
    table = relay_of * cap2 + base_to_me.reshape(-1)[place] - first_to_me
    u = jnp.arange(n_cap)
    in_i = (u[:, None] >= roff_me[None, :]) & (u[:, None] < (roff_me + len_me)[None, :])
    r_of_u = jnp.sum(jnp.where(in_i, off_me[None, :] + u[:, None] - roff_me[None, :], 0), axis=1)
    i_of_u = jnp.sum(jnp.where(in_i, np.arange(group)[None, :], 0), axis=1)
    dest_idx = pick(table.reshape(-1), i_of_u * n_relay + lax.rem(r_of_u, n_relay), group * n_relay) + r_of_u // n_relay

    send_idx = jnp.pad(tok_perm, (0, cap1 * n_relay - tok_perm.shape[0])).reshape(cap1, n_relay).T.reshape(-1)
    return send_idx, relay_idx, dest_idx


def back_indices(me, len_ij, tok_perm, n_rows, cap1, cap2, source_of, n_chunks):
    group, n_relay = source_of.shape
    n_classes = n_relay * n_chunks
    off_ij = jnp.cumsum(len_ij, axis=1) - len_ij
    roff_ij = jnp.cumsum(len_ij, axis=0) - len_ij
    first, count = run_tables(len_ij, n_classes)
    cls = (np.arange(n_chunks)[:, None] * n_relay + np.arange(n_relay)[None, :])
    first_k = first[source_of[:, None, :], cls[None]]
    count_k = count[source_of[:, None, :], cls[None]]
    base_k = jnp.cumsum(count_k, axis=2) - count_k

    def mine(t, axis=0):
        return lax.dynamic_index_in_dim(t, me, axis, keepdims=False)

    cnt = mine(count_k, 3).transpose(1, 0, 2).reshape(n_chunks, -1)
    fst = mine(first_k, 3).transpose(1, 0, 2).reshape(n_chunks, -1)
    start = jnp.cumsum(cnt, axis=1) - cnt
    shift = jnp.broadcast_to(cls[:, None, :] + mine(roff_ij - off_ij, 1)[source_of][None], (n_chunks, group, n_relay)).reshape(n_chunks, -1)
    p = jnp.arange(n_rows)
    in_run = (p >= start[:, :, None]) & (p < (start + cnt)[:, :, None])
    u_of_p = (fst[:, :, None] + p - start[:, :, None]) * n_classes + shift[:, :, None]
    chunk_idx = jnp.sum(jnp.where(in_run, u_of_p + 1, 0), axis=1).reshape(-1) - 1

    n_k = jnp.sum(cnt.reshape(n_chunks, group, n_relay), axis=2)
    start_k = jnp.cumsum(n_k, axis=1) - n_k
    q = jnp.arange(cap2)
    far_idx = jnp.where(q < n_k[:, :, None], start_k[:, :, None] + q, -1).reshape(-1)

    base_me, count_me, first_me = mine(base_k), mine(count_k), mine(first_k)
    slot = jnp.arange(cap1)
    in_j = (slot >= first_me[..., None]) & (slot < (first_me + count_me)[..., None])
    back = np.arange(group)[:, None] * cap2 + base_me[..., None] + slot - first_me[..., None]
    near_idx = jnp.sum(jnp.where(in_j, back + 1, 0), axis=2).reshape(-1) - 1

    inv_perm = jnp.argsort(tok_perm)
    group_no = inv_perm // n_relay
    final_idx = (lax.rem(group_no, n_chunks) * n_relay + lax.rem(inv_perm, n_relay)) * cap1 + group_no // n_chunks
    return chunk_idx, far_idx, near_idx, final_idx


N_TILE = 512
RELAYS = ((0, False), (0, True), (1, False), (1, True), (-1, False), (-1, True))
NEAR_ORDER = (2, 4, 3, 5, 1, 0)
FAR_ORDER = ((2, False), (1, False), (-1, False), (2, True), (1, True), (-1, True), (0, True), (0, False))


def peer(me, group, chips_on, flip):
    n_chips = group // 2
    chip = lax.rem(me // 2 + chips_on + n_chips, n_chips)
    core = lax.rem(me, 2)
    if flip:
        core = 1 - core
    return chip * 2 + core


def row_block(n, most):
    return max(d for d in range(16, most + 1, 16) if n % d == 0)


def build_pick(idx_ref, at, pick_ref, n_src):
    block = row_block(at.size, 288)

    @pl.loop(0, at.size // block)
    def _(b):
        off = pl.multiple_of(b * block, 16)
        lane = lax.broadcasted_iota(jnp.int32, (block, n_src), 1)
        hit = idx_ref[pl.ds(pl.multiple_of(at.start + off, 16), block), :] == lane
        pick_ref[pl.ds(off, block), :n_src] = hit.astype(jnp.float32).astype(pick_ref.dtype)


def gather_rows(src_ref, pick_ref, dst_ref, dst_at):
    n_src, width = src_ref.shape

    @pl.loop(0, width // N_TILE)
    def _(n):
        cols = pl.ds(pl.multiple_of(n * N_TILE, N_TILE), N_TILE)
        rows = jnp.dot(pick_ref[:dst_at.size, :n_src], src_ref[:, cols], preferred_element_type=jnp.float32)
        dst_ref[dst_at, cols] = rows.astype(dst_ref.dtype)


def hop(src_ref, idx_ref, pick_ref, buf_ref, land_ref, land_local, cap, targets, send_sem, recv_sem):
    copies = []
    for t, (dev, block, slot) in enumerate(targets):
        build_pick(idx_ref, pl.ds(pl.multiple_of(block * cap, 16), cap), pick_ref, src_ref.shape[0])
        if copies:
            copies[-1].start()
        here = pl.ds(t * cap, cap)
        there = pl.ds(pl.multiple_of(slot * cap, 16), cap)
        if dev is None and land_local:
            gather_rows(src_ref, pick_ref, land_ref, there)
            continue
        gather_rows(src_ref, pick_ref, buf_ref, here)
        if dev is None:
            copies.append(pltpu.make_async_copy(buf_ref.at[here, :], land_ref.at[there, :], recv_sem.at[t]))
        else:
            copies.append(pltpu.make_async_remote_copy(
                src_ref=buf_ref.at[here, :],
                dst_ref=land_ref.at[there, :],
                send_sem=send_sem.at[t],
                recv_sem=recv_sem.at[t],
                device_id={'sp': dev},
                device_id_type=pl.DeviceIdType.MESH,
            ))
    if not land_local:
        copies[-1].start()
    for copy in copies:
        copy.wait()


def two_hop_kernel(group, near_first, cap_a, cap_b, src_ref, idx_a_ref, idx_b_ref, out_ref, pick_ref, buf_a_ref, mid_ref, buf_b_ref, sem_a_send, sem_a_recv, sem_b_send, sem_b_recv):
    me = lax.axis_index('sp')
    barrier = pltpu.get_barrier_semaphore()
    for other in range(1, group):
        pl.semaphore_signal(barrier, inc=1, device_id={'sp': lax.rem(me + other, group)}, device_id_type=pl.DeviceIdType.MESH)
    pl.semaphore_wait(barrier, group - 1)
    near = []
    sign = 1 if near_first else -1
    for block in NEAR_ORDER:
        chips_on, flip = RELAYS[block]
        dev = None if (chips_on == 0 and not flip) else peer(me, group, sign * chips_on, flip)
        near.append((dev, block, block))
    far = []
    for chips_on, flip in FAR_ORDER:
        dev = peer(me, group, chips_on, flip)
        far.append((None if (chips_on == 0 and not flip) else dev, dev, me))
    first, second = (near, far) if near_first else (far, near)
    hop(src_ref, idx_a_ref, pick_ref, buf_a_ref, mid_ref, True, cap_a, first, sem_a_send, sem_a_recv)
    hop(mid_ref, idx_b_ref, pick_ref, buf_b_ref, out_ref, False, cap_b, second, sem_b_send, sem_b_recv)


def two_hop(src, idx_a, idx_b, group, near_first, collective_id):
    n_src, width = src.shape
    n_a = len(RELAYS) if near_first else group
    n_b = group if near_first else len(RELAYS)
    rows_a, rows_b = idx_a.shape[0], idx_b.shape[0]
    vmem = pl.BlockSpec(memory_space=pltpu.VMEM)
    return pl.pallas_call(
        functools.partial(two_hop_kernel, group, near_first, rows_a // n_a, rows_b // n_b),
        out_shape=jax.ShapeDtypeStruct((rows_b, width), src.dtype),
        in_specs=[vmem, vmem, vmem],
        out_specs=pl.BlockSpec(memory_space=pl.ANY),
        scratch_shapes=[
            pltpu.VMEM((max(rows_a // n_a, rows_b // n_b), max(n_src, rows_a)), src.dtype),
            pltpu.VMEM((rows_a, width), src.dtype),
            pltpu.VMEM((rows_a, width), src.dtype),
            pltpu.VMEM((rows_b, width), src.dtype),
            pltpu.SemaphoreType.DMA((n_a,)),
            pltpu.SemaphoreType.DMA((n_a,)),
            pltpu.SemaphoreType.DMA((n_b,)),
            pltpu.SemaphoreType.DMA((n_b,)),
        ],
        compiler_params=pltpu.CompilerParams(collective_id=collective_id, has_side_effects=True, vmem_limit_bytes=60 * 1024 * 1024),
        name="two_hop_out" if near_first else "two_hop_back",
    )(src, idx_a[:, None], idx_b[:, None])


FF_TILE = 512
BACK_CHUNKS = 3


def mlp_back_kernel(group, n_chunks, cap_far, cap_near, z_ref, gain_ref, chunk_idx_ref, far_idx_ref, near_idx_ref, wg_ref, wu_ref, wd_ref, out_ref,
                    pick_ref, pick2_ref, zo_ref, h2_ref, acc_ref, buf_ref, mid_ref, far_send, far_recv, near_send, near_recv):
    h = pl.program_id(0)
    f = pl.program_id(1)
    last_f = pl.num_programs(1) - 1
    n_rows = h2_ref.shape[0]
    block = row_block(n_rows, 80)
    width = z_ref.shape[1]
    n_far = group * cap_far
    n_near = len(RELAYS) * cap_near
    me = lax.axis_index('sp')

    def far_copies(c):
        copies = []
        for t, (chips_on, flip) in enumerate(FAR_ORDER):
            if chips_on == 0 and not flip:
                continue
            dev = peer(me, group, chips_on, flip)
            copies.append(pltpu.make_async_remote_copy(
                src_ref=buf_ref.at[pl.ds(pl.multiple_of(dev * cap_far, 16), cap_far), :],
                dst_ref=mid_ref.at[pl.ds(pl.multiple_of(c * n_far + me * cap_far, 16), cap_far), :],
                send_sem=far_send.at[c, t], recv_sem=far_recv.at[c, t],
                device_id={'sp': dev}, device_id_type=pl.DeviceIdType.MESH))
        return copies

    def near_copies(c):
        copies = []
        for t in NEAR_ORDER:
            chips_on, flip = RELAYS[t]
            src = buf_ref.at[pl.ds(t * cap_near, cap_near), :]
            dst = out_ref.at[pl.ds(c * n_near + t * cap_near, cap_near), :]
            if chips_on == 0 and not flip:
                copies.append(pltpu.make_async_copy(src, dst, near_recv.at[c, t]))
            else:
                copies.append(pltpu.make_async_remote_copy(
                    src_ref=src, dst_ref=dst, send_sem=near_send.at[c, t], recv_sem=near_recv.at[c, t],
                    device_id={'sp': peer(me, group, -chips_on, flip)}, device_id_type=pl.DeviceIdType.MESH))
        return copies

    def start_far(c):
        build_pick(far_idx_ref, pl.ds(c * n_far, n_far), pick_ref, n_rows)
        gather_rows(zo_ref.at[pl.ds(c * n_rows, n_rows), :], pick_ref, buf_ref, pl.ds(0, n_far))
        build_pick(near_idx_ref, pl.ds(c * n_near, n_near), pick2_ref, n_far)
        for copy in far_copies(c):
            copy.start()
        own = pl.multiple_of(me * cap_far, 16)
        mid_ref[pl.ds(pl.multiple_of(c * n_far + own, 16), cap_far), :] = buf_ref[pl.ds(own, cap_far), :]

    def start_near(c):
        for copy in far_copies(c):
            copy.wait()
        gather_rows(mid_ref.at[pl.ds(c * n_far, n_far), :], pick2_ref, buf_ref, pl.ds(0, n_near))
        for copy in near_copies(c):
            copy.start()

    def end_near(c):
        for copy in near_copies(c):
            copy.wait()

    @pl.when((h == 0) & (f == 0))
    def _():
        barrier = pltpu.get_barrier_semaphore()
        for other in range(1, group):
            pl.semaphore_signal(barrier, inc=1, device_id={'sp': lax.rem(me + other, group)}, device_id_type=pl.DeviceIdType.MESH)
        pl.semaphore_wait(barrier, group - 1)

    for c in range(n_chunks):
        zo = zo_ref.at[pl.ds(c * n_rows, n_rows), :]

        @pl.when((h == c) & (f == 0))
        def _():
            build_pick(chunk_idx_ref, pl.ds(c * n_rows, n_rows), pick_ref, z_ref.shape[0])
            gather_rows(z_ref, pick_ref, zo, pl.ds(0, n_rows))
            gain = gain_ref[...].astype(jnp.float32)

            @pl.loop(0, n_rows // block)
            def _(b):
                at = pl.ds(pl.multiple_of(b * block, 16), block)
                rows_f = zo[at, :].astype(jnp.float32)
                inv_rms = lax.rsqrt(jnp.mean(rows_f * rows_f, axis=-1, keepdims=True) + NORM_EPS)
                h2_ref[at, :] = (rows_f * inv_rms * gain).astype(h2_ref.dtype)
                acc_ref[at, :] = jnp.zeros((block, width), jnp.float32)

        if c > 0:
            @pl.when((h == c) & (f == (last_f + 1) // 2))
            def _():
                start_near(c - 1)

    gate = jnp.dot(h2_ref[...], wg_ref[...], preferred_element_type=jnp.float32)
    up = jnp.dot(h2_ref[...], wu_ref[...], preferred_element_type=jnp.float32)
    act = (gate * jax.nn.sigmoid(gate) * up).astype(jnp.bfloat16)
    acc_ref[...] += jnp.dot(act, wd_ref[...], preferred_element_type=jnp.float32)

    for c in range(n_chunks):
        zo = zo_ref.at[pl.ds(c * n_rows, n_rows), :]

        @pl.when((h == c) & (f == last_f))
        def _():
            if c > 0:
                end_near(c - 1)

            @pl.loop(0, n_rows // block)
            def _(b):
                at = pl.ds(pl.multiple_of(b * block, 16), block)
                down = acc_ref[at, :].astype(jnp.bfloat16).astype(jnp.float32)
                zo[at, :] = (zo[at, :].astype(jnp.float32) + down).astype(zo_ref.dtype)

            start_far(c)
            if c == n_chunks - 1:
                start_near(c)
                end_near(c)


def mlp_back(z, gain, chunk_idx, far_idx, near_idx, w_gate, w_up, w_down, group, n_rows, cap_far, cap_near, collective_id):
    n_src, width = z.shape
    ff = w_gate.shape[1]
    n_chunks = BACK_CHUNKS
    n_far, n_near = group * cap_far, len(RELAYS) * cap_near
    whole = lambda shape: pl.BlockSpec(shape, lambda h, f: (0, 0), pipeline_mode=pl.Buffered(1))
    return pl.pallas_call(
        functools.partial(mlp_back_kernel, group, n_chunks, cap_far, cap_near),
        out_shape=jax.ShapeDtypeStruct((n_chunks * n_near, width), z.dtype),
        grid=(n_chunks, ff // FF_TILE),
        in_specs=[
            whole(z.shape), whole((1, width)), whole((n_chunks * n_rows, 1)), whole((n_chunks * n_far, 1)), whole((n_chunks * n_near, 1)),
            pl.BlockSpec((width, FF_TILE), lambda h, f: (0, f)),
            pl.BlockSpec((width, FF_TILE), lambda h, f: (0, f)),
            pl.BlockSpec((FF_TILE, width), lambda h, f: (f, 0)),
        ],
        out_specs=pl.BlockSpec(memory_space=pl.ANY),
        scratch_shapes=[
            pltpu.VMEM((max(n_rows, n_far), max(n_src, n_rows)), z.dtype),
            pltpu.VMEM((n_near, n_far), z.dtype),
            pltpu.VMEM((n_chunks * n_rows, width), z.dtype),
            pltpu.VMEM((n_rows, width), z.dtype),
            pltpu.VMEM((n_rows, width), jnp.float32),
            pltpu.VMEM((max(n_far, n_near), width), z.dtype),
            pltpu.VMEM((n_chunks * n_far, width), z.dtype),
            pltpu.SemaphoreType.DMA((n_chunks, group)),
            pltpu.SemaphoreType.DMA((n_chunks, group)),
            pltpu.SemaphoreType.DMA((n_chunks, len(RELAYS))),
            pltpu.SemaphoreType.DMA((n_chunks, len(RELAYS))),
        ],
        compiler_params=pltpu.CompilerParams(collective_id=collective_id, has_side_effects=True, vmem_limit_bytes=63 * 1024 * 1024,
                                             dimension_semantics=("arbitrary", "arbitrary")),
        name="mlp_back",
    )(z, gain.reshape(1, width), chunk_idx[:, None], far_idx[:, None], near_idx[:, None], w_gate, w_up, w_down)


def solution(mesh):
    row_spec = P(('dp', 'sp'), None)
    vec_spec = P(('dp', 'sp'))
    rep_spec = P()

    def per_device(hidden, tok_perm, send_off, send_len, recv_off, recv_len, recv_doc, recv_pos, g_attn, w_q, w_k, w_v, w_o, g_mlp, w_gate, w_up, w_down):
        n_tok, model_dim = hidden.shape
        n_cap = recv_doc.shape[0]
        group = send_off.shape[0]
        relay_of, source_of = relay_tables(group)
        n_relay = relay_of.shape[1]
        round_up = lambda n, unit: -(-n // unit) * unit
        cap1 = round_up(-(-n_tok // n_relay), 16)
        cap2 = round_up((n_cap + n_relay * (n_relay - 1)) // n_relay, 16)
        n_classes = n_relay * BACK_CHUNKS
        cap1_back = round_up(-(-n_tok // n_classes), 16)
        cap2_back = round_up((n_cap + n_relay * (n_classes - 1)) // n_classes, 16)
        n_rows = round_up(-(-(n_cap + group * n_relay * (BACK_CHUNKS - 1)) // BACK_CHUNKS), 16)
        me = lax.axis_index('sp')
        len_ij = lax.all_gather(send_len, 'sp')
        send_idx, relay_idx, dest_idx = out_indices(me, len_ij, tok_perm, n_cap, cap1, cap2, relay_of, source_of)
        chunk_idx, far_idx, near_idx, final_idx = back_indices(me, len_ij, tok_perm, n_rows, cap1_back, cap2_back, source_of, BACK_CHUNKS)

        def take(rows, index):
            return rows.at[index].get(mode='promise_in_bounds')

        at_dest = two_hop(hidden, send_idx, relay_idx, group, True, 0)
        z = attn_layer(take(at_dest, dest_idx), recv_doc, recv_pos, g_attn, w_q, w_k, w_v, w_o)
        src_back = mlp_back(z, g_mlp, chunk_idx, far_idx, near_idx, w_gate, w_up, w_down, group, n_rows, cap2_back, cap1_back, 1)
        return take(src_back, final_idx)

    return jax.shard_map(per_device, mesh=mesh, in_specs=(row_spec,) + (vec_spec,) * 7 + (rep_spec,) * 9, out_specs=row_spec, check_vma=False)
```

time: 936 us -> 816 us (0.87)
  matrix products: 213 us -> 20.3 us
  Pallas kernels: 612 us -> 672 us
    pallas_call x0 -> x1, Pallas kernels: none -> 312 us  [mlp_back(): pl.pallas_call(functools.partial(mlp_back_kernel, group, n_chunks, cap_fa...]
    pallas_call x2 -> x1, Pallas kernels: 432 us -> 221 us  [two_hop(): pl.pallas_call(functools.partial(two_hop_kernel, group, near_first, rows_...]
    dot_general x4 -> x1, matrix products: 213 us -> 20.3 us  [attn_layer(): jnp.dot(attn_heads, w_o.reshape(n_heads * head_dim, model_dim), preferred...]
    pallas_call x1, Pallas kernels: 99.3 us -> 74.1 us  [attention(): pl.pallas_call(functools.partial(attn_kernel, head_dim), out_shape=jax.Sh...]
    pallas_call x3, Pallas kernels: 80.8 us -> 65.3 us  [qkv_proj(): pl.pallas_call(functools.partial(qkv_one, head_dim, kind), out_shape=jax....]
    another operation x3 -> x6, other arithmetic: 1.44 us -> 13 us  [the longest x1 11.1 us: back_indices(): base_k = jnp.cumsum(count_k, axis=2) - count_k]
where the time goes in v3:
time: 816 us; the launch traced here: 807 us
  Pallas kernels  672 us (82%)
  local copies, waits for them, and re-layouts  70.9 us (9%)
  other arithmetic  32.6 us (4%)
  matrix products  20.3 us (2%)
  blocking collectives  8.9 us (1%)
    pallas_call x1, Pallas kernels, mlp_back(): pl.pallas_call(functools.partial(mlp_back_kernel, group, n_chunks, cap_fa...  312 us
    pallas_call x1, Pallas kernels, two_hop(): pl.pallas_call(functools.partial(two_hop_kernel, group, near_first, rows_...  221 us
    pallas_call x1, Pallas kernels, attention(): pl.pallas_call(functools.partial(attn_kernel, head_dim), out_shape=jax.Sh...  74.1 us
    pallas_call x3, Pallas kernels, qkv_proj(): pl.pallas_call(functools.partial(qkv_one, head_dim, kind), out_shape=jax....  65.3 us
    gather x2, local copies, waits for them, and re-layouts, take(): return rows.at[index].get(mode='promise_in_bounds')  47.9 us
    dot_general x1, matrix products, attn_layer(): jnp.dot(attn_heads, w_o.reshape(n_heads * head_dim, model_dim), preferred...  20.3 us

profile of v3, /device:TPU:113, one launch (start us, length us, event | category | flops | bytes accessed | tf_op | source)
XLA Modules:
  0.0 806.7 jit_solution(2348106961266682660)
XLA Ops:
  0.0 1.2 dynamic-slice
  1.9 0.9 dynamic-update-slice
  2.8 8.9 %all-reduce = s32[64]{0:T(128)S(1)} all-reduce(s32[64]{0:T(128)S(1)} %dynamic-update-slice), channel_id=2, replica_groups=mesh['dp'=2,'sp'=8] {'sp'}, use_global_device_ids=true, to_apply=%add | all-reduce | flops 64 | bytes 512
  11.7 0.2 reduce_window_sum.70
  12.0 0.9 gather_fusion
  13.1 1.3 reduce_window_sum.71
  14.4 0.9 gather_fusion.1
  15.9 1.5 broadcast_in_dim_reshape.13.idx_b_ref
  17.4 0.9 reshape.302
  18.4 1.7 copy.146
  20.1 221.2 %two_hop_out.1 = bf16[2176,2048]{1,0:T(8,128)(2,1)} custom-call(bf16[3072,2048]{1,0:T(8,128)(2,1)} %src_ref.1, s32[3072,1]{1,0:T(8,128)} %bitcast.55, s32[2176,1]{1,0:T(8,128)} %broadcast_in_dim_reshape.13.idx_b_ref), custom_call_target="tpu_custom_call" | custom-call | tf_op jit(solution)/shard_map/two_hop_out/pallas_call | solution.py:338
  241.3 0.2 dynamic-slice_reduce_fusion.2
  241.5 0.2 dynamic-slice_reduce_fusion
  241.8 0.1 fusion.25
  242.0 0.8 gather_fusion.2
  242.9 0.1 copy.132
  243.2 0.1 select_reduce_fusion.1
  243.4 17.7 %gather_fusion.3 = bf16[1536,2048]{1,0:T(8,128)(2,1)} fusion(bf16[2176,2048]{1,0:T(8,128)(2,1)} %two_hop_out.1, s32[2048]{0:T(1024)S(1)} %pad_clamp_fusion), kind=kCustom, calls=%fused_computation.3 | custom fusion | bytes 12589056 | tf_op jit(solution)/shard_map/gather | solution.py:535
  261.2 4.2 fusion
  265.4 0.3 copy-done
  265.8 4.1 fusion.2.h_ref
  269.9 2.8 fusion.5
  272.7 1.3 pad_maximum_fusion
  274.0 19.0 %qkv.5.v_ref = bf16[1536,2048]{1,0:T(8,128)(2,1)} custom-call(bf16[1536,2048]{1,0:T(8,128)(2,1)} %fusion.2.h_ref, bf16[2048,2048]{1,0:T(8,128)(2,1)} %bitcast.63, f32[1536,128]{1,0:T(8,128)S(1)} %get-tuple-element.34.cos_ref, f32[1536,128]{1,0:T(8,128)S(1)} %get-tuple-element.35.sin_ref), custom_call_target="tpu_custom_call" | custom-call | flops 12884901888 | bytes 20971520 | tf_op jit(solution)/shard_map/qkv/pallas_call | solution.py:39
  292.9 23.0 %qkv.4.k_ref = bf16[1536,2048]{1,0:T(8,128)(2,1)} custom-call(bf16[1536,2048]{1,0:T(8,128)(2,1)} %fusion.2.h_ref, bf16[2048,2048]{1,0:T(8,128)(2,1)} %bitcast.64, f32[1536,128]{1,0:T(8,128)S(1)} %get-tuple-element.34.cos_ref, f32[1536,128]{1,0:T(8,128)S(1)} %get-tuple-element.35.sin_ref), custom_call_target="tpu_custom_call" | custom-call | flops 12884901888 | bytes 20971520 | tf_op jit(solution)/shard_map/qkv/pallas_call | solution.py:39
  315.9 23.3 %qkv.3.q_ref = bf16[1536,2048]{1,0:T(8,128)(2,1)} custom-call(bf16[1536,2048]{1,0:T(8,128)(2,1)} %fusion.2.h_ref, bf16[2048,2048]{1,0:T(8,128)(2,1)} %bitcast.65, f32[1536,128]{1,0:T(8,128)S(1)} %get-tuple-element.34.cos_ref, f32[1536,128]{1,0:T(8,128)S(1)} %get-tuple-element.35.sin_ref), custom_call_target="tpu_custom_call" | custom-call | flops 12884901888 | bytes 20971520 | tf_op jit(solution)/shard_map/qkv/pallas_call | solution.py:39
  339.3 1.2 copy.134
  340.6 74.1 %attention.1 = bf16[1536,2048]{1,0:T(8,128)(2,1)} custom-call(bf16[1536,2048]{1,0:T(8,128)(2,1)} %qkv.3.q_ref, bf16[1536,2048]{1,0:T(8,128)(2,1)} %qkv.4.k_ref, bf16[1536,2048]{1,0:T(8,128)(2,1)} %qkv.5.v_ref, s32[2,1536]{1,0:T(2,128)} %copy-done.2, s32[1536,2]{1,0:T(8,128)} %bitcast.57), custom_call_target="tpu_custom_call" | custom-call | flops 14495514624 | bytes 25165824 | tf_op jit(solution)/shard_map/attention/pallas_call | solution.py:119
  414.7 20.3 %fusion.3.z_ref = bf16[1536,2048]{1,0:T(8,128)(2,1)} fusion(bf16[1536,2048]{1,0:T(8,128)(2,1)} %gather_fusion.3, bf16[1536,2048]{1,0:T(8,128)(2,1)} %attention.1, bf16[2048,2048]{1,0:T(8,128)(2,1)} %bitcast.66), kind=kOutput, calls=%fused_computation.14 | convolution fusion | flops 12900630528 | bytes 27262976 | tf_op jit(solution)/shard_map/dot_general | solution.py:139
  435.0 0.1 fusion.8
  435.2 1.4 gather_fusion.4
  436.7 0.2 reshape.341
  436.9 11.1 %reduce_window_sum.75 = s32[8,3,6,8]{2,1,0,3:T(4,128)S(1)} reduce-window(s32[8,3,6,8]{2,1,0,3:T(4,128)S(1)} %reshape.341, s32[]{:T(128)} %constant.161.clone.1), window={size=1x1x6x1 pad=0_0x0_0x5_0x0_0}, to_apply=%region_12.13 | reduce-window | flops 5760 | bytes 9220 | tf_op jit(solution)/shard_map/jit(cumsum)/reduce_window_sum | solution.py:211
  448.0 1.4 gather_fusion.5
  449.5 0.2 reshape.347
  450.0 0.2 select_reduce_fusion.2
  450.2 1.9 sub.216.near_idx_ref
  452.1 0.1 fusion.51
  452.3 0.2 reduce_window_sum.73
  452.7 0.8 gather_fusion.6
  453.6 0.2 select_reduce_fusion
  453.8 1.6 sub.215.chunk_idx_ref
  455.4 0.2 reduce_window_sum.74
  455.7 2.1 select_n.166.far_idx_ref
  457.8 0.6 reshape.308.gain_ref
  458.4 311.8 %mlp_back.1 = bf16[3168,2048]{1,0:T(8,128)(2,1)} custom-call(bf16[1536,2048]{1,0:T(8,128)(2,1)} %fusion.3.z_ref, bf16[1,2048]{1,0:T(2,128)(2,1)} %reshape.308.gain_ref, s32[1632,1]{1,0:T(8,128)} %sub.215.chunk_idx_ref, s32[2304,1]{1,0:T(8,128)} %select_n.166.far_idx_ref, s32[3168,1]{1,0:T(8,128)} %sub.216.near_idx_ref, bf16[2048,8192]{1,0:T(8,128)(2,1)} %wg_ref.1, ...), custom_call_target="tpu_custom_call" | custom-call | tf_op jit(solution)/shard_map/mlp_back/pallas_call | solution.py:481
  770.2 5.8 sort.17
  776.0 30.2 %gather_fusion.7 = bf16[3072,2048]{1,0:T(8,128)(2,1)} fusion(bf16[3168,2048]{1,0:T(8,128)(2,1)} %mlp_back.1, s32[3072]{0:T(1024)S(1)} %fusion.45), kind=kCustom, calls=%fused_computation.7 | custom fusion | bytes 25178112 | tf_op jit(solution)/shard_map/gather | solution.py:535
  (92 shorter events, 2.5 us)
Async XLA Ops:
  20.1 221.9 %copy-start.11 = (s32[48]{0:T(128)S(1)}, s32[48]{0:T(128)}, u32[]{:S(2)}) copy-start(s32[48]{0:T(128)} %constant.276) | copy-start | bytes 580
  20.1 222.7 %copy-start.12 = (s32[48]{0:T(128)S(1)}, s32[48]{0:T(128)}, u32[]{:S(2)}) copy-start(s32[48]{0:T(128)} %constant.282) | copy-start | bytes 580
  243.4 22.0 %copy-start.5 = (bf16[2048]{0:T(1024)(128)(2,1)S(1)}, bf16[2048]{0:T(1024)(128)(2,1)}, u32[]{:S(2)}) copy-start(bf16[2048]{0:T(1024)(128)(2,1)} %param.48) | copy-start | bytes 12292
  261.2 4.6 copy-start
  261.2 8.7 %copy-start.3 = (s32[1536]{0:T(1024)S(1)}, s32[1536]{0:T(1024)}, u32[]{:S(2)}) copy-start(s32[1536]{0:T(1024)} %param.47) | copy-start | bytes 18436
  315.9 23.3 %copy-start.4 = (s32[1536]{0:T(1024)S(1)}, s32[1536]{0:T(1024)}, u32[]{:S(2)}) copy-start(s32[1536]{0:T(1024)} %param.46) | copy-start | bytes 18436
  339.3 1.3 copy-start.2
  414.7 20.4 %copy-start.7 = (s32[8,6]{1,0:T(8,128)S(1)}, s32[8,6]{1,0:T(8,128)}, u32[]{:S(2)}) copy-start(s32[8,6]{1,0:T(8,128)} %constant.277) | copy-start | bytes 580
  414.7 20.4 %copy-start.9 = (s32[3,6]{1,0:T(4,128)S(1)}, s32[3,6]{1,0:T(4,128)}, u32[]{:S(2)}) copy-start(s32[3,6]{1,0:T(4,128)} %constant.278) | copy-start | bytes 220
  414.7 38.0 %copy-start.10 = (s32[48]{0:T(128)S(1)}, s32[48]{0:T(128)}, u32[]{:S(2)}) copy-start(s32[48]{0:T(128)} %constant.281) | copy-start | bytes 580
  435.0 18.5 %copy-start.8 = (s32[3,6]{1,0:T(4,128)S(1)}, s32[3,6]{1,0:T(4,128)}, u32[]{:S(2)}) copy-start(s32[3,6]{1,0:T(4,128)} %constant.200) | copy-start | bytes 220
  435.0 22.8 %copy-start.6 = (bf16[2048]{0:T(1024)(128)(2,1)S(1)}, bf16[2048]{0:T(1024)(128)(2,1)}, u32[]{:S(2)}) copy-start(bf16[2048]{0:T(1024)(128)(2,1)} %param.53) | copy-start | bytes 12292
  458.4 311.8 %copy-start.1 = (s32[3072]{0:T(1024)S(1)}, s32[3072]{0:T(1024)}, u32[]{:S(2)}) copy-start(s32[3072]{0:T(1024)} %param.44) | copy-start | bytes 36868

commit v4 on v3

v4 whole, which is shorter than its diff:
```python
import functools

import jax
import jax.numpy as jnp
import numpy as np
from jax import lax
from jax.experimental import pallas as pl
from jax.experimental.pallas import tpu as pltpu
from jax.sharding import PartitionSpec as P

ROPE_BASE = 500000.0
NORM_EPS = 1e-5
Q_TILE = 256
QKV_TILE = 256


def rope_tables(positions, head_dim):
    half = head_dim // 2
    inv_freq = jnp.power(jnp.float32(ROPE_BASE), -2.0 * jnp.arange(half, dtype=jnp.float32) / head_dim)
    angles = positions.astype(jnp.float32)[:, None] * inv_freq[None, :]
    cos_t = jnp.cos(angles)
    sin_t = jnp.sin(angles)
    return jnp.concatenate([cos_t] * 4, axis=1), jnp.concatenate([-sin_t, sin_t] * 2, axis=1)


def qkv_kernel(head_dim, blocks_ref, idx_ref, gain_ref, cos_ref, sin_ref, wq_ref, wk_ref, wv_ref, r_ref, q_ref, k_ref, v_ref, pick_ref, h_ref):
    n = pl.program_id(0)
    n_each = pl.num_programs(0) // 3
    rows = r_ref.shape[0]
    lanes = cos_ref.shape[1]
    half = head_dim // 2

    @pl.when(n == 0)
    def _():
        build_pick(idx_ref, pl.ds(0, rows), pick_ref, blocks_ref.shape[0])
        gather_rows(blocks_ref, pick_ref, r_ref, pl.ds(0, rows))
        norm_rows(r_ref, gain_ref, h_ref)

    for kind, (w_ref, o_ref) in enumerate(((wq_ref, q_ref), (wk_ref, k_ref), (wv_ref, v_ref))):
        @pl.when(n // n_each == kind)
        def _():
            acc = lax.dot_general(h_ref[...], w_ref[...], (((1,), (1,)), ((), ())), preferred_element_type=jnp.float32)
            if kind == 2:
                o_ref[...] = acc.astype(o_ref.dtype)
                return
            first = lax.rem(lax.broadcasted_iota(jnp.int32, (1, lanes), 1), head_dim) < half
            for b in range(o_ref.shape[1] // lanes):
                x = acc[:, b * lanes:(b + 1) * lanes]
                swapped = jnp.where(first, pltpu.roll(x, lanes - half, 1), pltpu.roll(x, half, 1))
                rot = x * cos_ref[...] + swapped * sin_ref[...]
                if kind == 0:
                    rot = rot * (head_dim ** -0.5)
                o_ref[:, b * lanes:(b + 1) * lanes] = rot.astype(o_ref.dtype)


def qkv_proj(blocks, dest_idx, gain, w_q, w_k, w_v, cos_t, sin_t):
    rows = dest_idx.shape[0]
    model_dim = blocks.shape[1]
    n_heads, head_dim = w_q.shape[1:]
    width = n_heads * head_dim
    n_each = width // QKV_TILE
    w_all = [w.transpose(1, 2, 0).reshape(width, model_dim) for w in (w_q, w_k, w_v)]
    once = lambda shape: pl.BlockSpec(shape, lambda n: (0, 0), pipeline_mode=pl.Buffered(1))
    tile = lambda kind: (lambda n: jnp.clip(n - kind * n_each, 0, n_each - 1))
    return pl.pallas_call(
        functools.partial(qkv_kernel, head_dim),
        out_shape=[jax.ShapeDtypeStruct((rows, model_dim), blocks.dtype)] + [jax.ShapeDtypeStruct((rows, width), blocks.dtype)] * 3,
        grid=(3 * n_each,),
        in_specs=[once(blocks.shape), once((rows, 1)), once((1, model_dim)), once(cos_t.shape), once(sin_t.shape)]
        + [pl.BlockSpec((QKV_TILE, model_dim), lambda n, t=tile(kind): (t(n), 0)) for kind in range(3)],
        out_specs=[once((rows, model_dim))] + [pl.BlockSpec((rows, QKV_TILE), lambda n, t=tile(kind): (0, t(n))) for kind in range(3)],
        scratch_shapes=[pltpu.VMEM((rows, blocks.shape[0]), blocks.dtype), pltpu.VMEM((rows, model_dim), blocks.dtype)],
        compiler_params=pltpu.CompilerParams(vmem_limit_bytes=56 * 1024 * 1024, dimension_semantics=("arbitrary",)),
        cost_estimate=pl.CostEstimate(flops=6 * rows * model_dim * width, bytes_accessed=6 * model_dim * width, transcendentals=0),
        name="qkv",
    )(blocks, dest_idx[:, None], gain.reshape(1, model_dim), cos_t, sin_t, *w_all)


def attn_kernel(head_dim, n_parts, q_ref, *refs):
    k_parts, v_parts = refs[:n_parts], refs[n_parts:2 * n_parts]
    meta_row_ref, meta_col_ref, o_ref, bias_ref, k_ref, v_ref = refs[2 * n_parts:]
    rows, lanes = q_ref.shape
    n_tiles = rows // Q_TILE
    before = k_ref.shape[0] - rows

    @pl.when(pl.program_id(0) == 0)
    def _():
        for t in range(n_tiles):
            at = slice(t * Q_TILE, (t + 1) * Q_TILE)
            n_keys = before + (t + 1) * Q_TILE
            ok = (meta_col_ref[at, 0:1] == meta_row_ref[0:1, :n_keys]) & (meta_row_ref[1:2, :n_keys] <= meta_col_ref[at, 1:2])
            bias_ref[at, :n_keys] = jnp.where(ok, 0.0, -1e30).astype(jnp.float32)

    lo = 0
    for k_part, v_part in zip(k_parts, v_parts):
        hi = lo + k_part.shape[0]
        k_ref[lo:hi, :] = k_part[...]
        v_ref[lo:hi, :] = v_part[...]
        lo = hi
    low = lax.broadcasted_iota(jnp.int32, (Q_TILE, lanes), 1) < head_dim

    def scores(t):
        q = q_ref[t * Q_TILE:(t + 1) * Q_TILE, :]
        zero = jnp.zeros((), q.dtype)
        both = jnp.concatenate([jnp.where(low, q, zero), jnp.where(low, zero, q)], axis=0)
        return lax.dot_general(both, k_ref[:before + (t + 1) * Q_TILE, :], (((1,), (1,)), ((), ())), preferred_element_type=jnp.float32)

    def outputs(t, s):
        at = slice(t * Q_TILE, (t + 1) * Q_TILE)
        n_keys = before + (t + 1) * Q_TILE
        s = s.reshape(2, Q_TILE, n_keys) + bias_ref[at, :n_keys][None]
        e = jnp.exp(s - jnp.max(s, axis=2, keepdims=True))
        total = jnp.sum(e, axis=2, keepdims=True)
        o = jnp.dot(e.astype(jnp.bfloat16).reshape(2 * Q_TILE, n_keys), v_ref[:n_keys, :], preferred_element_type=jnp.float32)
        o = o.reshape(2, Q_TILE, lanes) / total
        o_ref[at, :] = jnp.where(low, o[0], o[1]).astype(o_ref.dtype)

    ahead = scores(0)
    for t in range(n_tiles):
        s = ahead
        if t + 1 < n_tiles:
            ahead = scores(t + 1)
        outputs(t, s)


def attention(q, k_parts, v_parts, doc_ids, positions, head_dim):
    rows, width = q.shape
    n_parts = len(k_parts)
    n_keys = sum(k.shape[0] for k in k_parts)
    lanes = 2 * head_dim
    meta = jnp.stack([doc_ids, positions])[:, :n_keys]
    meta_t = meta[:, n_keys - rows:].T
    head_spec = lambda a: pl.BlockSpec((a.shape[0], lanes), lambda n: (0, n))
    whole = lambda a: pl.BlockSpec(a.shape, lambda n: (0, 0))
    pairs = n_keys * n_keys // 2 - (n_keys - rows) * (n_keys - rows) // 2
    return pl.pallas_call(
        functools.partial(attn_kernel, head_dim, n_parts),
        out_shape=jax.ShapeDtypeStruct((rows, width), jnp.bfloat16),
        grid=(width // lanes,),
        in_specs=[head_spec(a) for a in (q, *k_parts, *v_parts)] + [whole(meta), whole(meta_t)],
        out_specs=head_spec(q),
        scratch_shapes=[pltpu.VMEM((rows, n_keys), jnp.float32), pltpu.VMEM((n_keys, lanes), q.dtype), pltpu.VMEM((n_keys, lanes), q.dtype)],
        compiler_params=pltpu.CompilerParams(vmem_limit_bytes=56 * 1024 * 1024),
        cost_estimate=pl.CostEstimate(flops=16 * pairs * width, bytes_accessed=8 * rows * width, transcendentals=pairs * width // head_dim),
        name="attention",
    )(q, *k_parts, *v_parts, meta, meta_t)


def attn_layer(parts, doc_ids, positions, g_attn, w_q, w_k, w_v, w_o):
    n_heads, head_dim = w_q.shape[1:]
    w_out = w_o.reshape(n_heads * head_dim, -1)
    cos_t, sin_t = rope_tables(positions, head_dim)
    k_parts, v_parts, z_parts = [], [], []
    lo = 0
    for blocks, dest_idx in parts:
        hi = lo + dest_idx.shape[0]
        rows, q, k, v = qkv_proj(blocks, dest_idx, g_attn, w_q, w_k, w_v, cos_t[lo:hi], sin_t[lo:hi])
        k_parts.append(k)
        v_parts.append(v)
        heads = attention(q, k_parts, v_parts, doc_ids, positions, head_dim)
        attn_out = jnp.dot(heads, w_out, preferred_element_type=jnp.float32).astype(jnp.bfloat16)
        z_parts.append((rows.astype(jnp.float32) + attn_out.astype(jnp.float32)).astype(jnp.bfloat16))
        lo = hi
    return z_parts


def relay_tables(group):
    def at(dev, chips_on, flip):
        return (dev // 2 + chips_on) % (group // 2) * 2 + (dev % 2 ^ int(flip))

    relay_of = np.array([[at(i, o, f) for o, f in RELAYS] for i in range(group)])
    source_of = np.array([[at(k, -o, f) for o, f in RELAYS] for k in range(group)])
    return relay_of, source_of


def ceil_div(a, b):
    return -((-a) // b)


def sum_before(x, axis):
    n = x.shape[axis]
    x = jnp.moveaxis(x, axis, -1)
    before = np.arange(n)[:, None] < np.arange(n)[None, :]
    return jnp.moveaxis(jnp.sum(jnp.where(before, x[..., :, None], 0), axis=-2), -1, axis)


def pick(table, index, n):
    return jnp.sum(jnp.where(index[:, None] == jnp.arange(n)[None, :], table[None, :], 0), axis=1)


def run_tables(off_ij, len_ij, n_classes):
    res = np.arange(n_classes)
    first = ceil_div(off_ij[:, None, :] - res[None, :, None], n_classes)
    count = ceil_div((off_ij + len_ij)[:, None, :] - res[None, :, None], n_classes) - first
    return first, count


def out_indices(me, len_ij, lo, n_rows, cap1, cap2, relay_of, source_of):
    group, n_relay = relay_of.shape
    off_all = sum_before(len_ij, 1)
    roff_all = sum_before(len_ij, 0)
    roff_ij = jnp.clip(roff_all, lo, lo + n_rows)
    off_ij = off_all + roff_ij - roff_all
    len_ij = jnp.clip(roff_all + len_ij, lo, lo + n_rows) - roff_ij
    off_ij = jnp.where(len_ij > 0, off_ij, 0)
    first, count = run_tables(off_ij, len_ij, n_relay)
    res = np.arange(n_relay)
    first_k = first[source_of, res]
    count_k = count[source_of, res]
    base_k = sum_before(count_k, 1)

    def mine(t, axis=0):
        return lax.dynamic_index_in_dim(t, me, axis, keepdims=False)

    base_me, count_me, first_me = mine(base_k), mine(count_k), mine(first_k)
    q = jnp.arange(cap2)
    in_m = (q >= base_me[:, :, None]) & (q < (base_me + count_me)[:, :, None])
    src = np.arange(n_relay)[:, None, None] * cap1 + first_me[:, :, None] + q - base_me[:, :, None]
    relay_idx = jnp.sum(jnp.where(in_m, src, 0), axis=0).reshape(-1)

    len_me, off_me, roff_me = mine(len_ij, 1), mine(off_ij, 1), mine(roff_ij, 1)
    base_to_me, first_to_me = mine(base_k, 2), mine(first, 2)
    place = np.zeros((group, n_relay), np.int32)
    place[source_of, res] = np.arange(group)[:, None] * n_relay + res
    table = relay_of * cap2 + base_to_me.reshape(-1)[place] - first_to_me
    u = lo + jnp.arange(n_rows)
    in_i = (u[:, None] >= roff_me[None, :]) & (u[:, None] < (roff_me + len_me)[None, :])
    r_of_u = jnp.sum(jnp.where(in_i, off_me[None, :] + u[:, None] - roff_me[None, :], 0), axis=1)
    i_of_u = jnp.sum(jnp.where(in_i, np.arange(group)[None, :], 0), axis=1)
    dest_idx = pick(table.reshape(-1), i_of_u * n_relay + lax.rem(r_of_u, n_relay), group * n_relay) + r_of_u // n_relay
    return relay_idx, dest_idx


def back_indices(me, len_ij, tok_perm, n_rows, cap1, cap2, source_of, n_chunks):
    group, n_relay = source_of.shape
    n_classes = n_relay * n_chunks
    off_ij = sum_before(len_ij, 1)
    roff_ij = sum_before(len_ij, 0)
    first, count = run_tables(off_ij, len_ij, n_classes)
    cls = (np.arange(n_chunks)[:, None] * n_relay + np.arange(n_relay)[None, :])
    first_k = first[source_of[:, None, :], cls[None]]
    count_k = count[source_of[:, None, :], cls[None]]
    base_k = sum_before(count_k, 2)

    def mine(t, axis=0):
        return lax.dynamic_index_in_dim(t, me, axis, keepdims=False)

    cnt = mine(count_k, 3).transpose(1, 0, 2).reshape(n_chunks, -1)
    fst = mine(first_k, 3).transpose(1, 0, 2).reshape(n_chunks, -1)
    start = sum_before(cnt, 1)
    shift = jnp.broadcast_to(cls[:, None, :] + mine(roff_ij - off_ij, 1)[source_of][None], (n_chunks, group, n_relay)).reshape(n_chunks, -1)
    p = jnp.arange(n_rows)
    in_run = (p >= start[:, :, None]) & (p < (start + cnt)[:, :, None])
    u_of_p = (fst[:, :, None] + p - start[:, :, None]) * n_classes + shift[:, :, None]
    chunk_idx = jnp.sum(jnp.where(in_run, u_of_p + 1, 0), axis=1).reshape(-1) - 1

    n_k = jnp.sum(cnt.reshape(n_chunks, group, n_relay), axis=2)
    start_k = sum_before(n_k, 1)
    q = jnp.arange(cap2)
    far_idx = jnp.where(q < n_k[:, :, None], start_k[:, :, None] + q, -1).reshape(-1)

    base_me, count_me, first_me = mine(base_k), mine(count_k), mine(first_k)
    slot = jnp.arange(cap1)
    in_j = (slot >= first_me[..., None]) & (slot < (first_me + count_me)[..., None])
    back = np.arange(group)[:, None] * cap2 + base_me[..., None] + slot - first_me[..., None]
    near_idx = jnp.sum(jnp.where(in_j, back + 1, 0), axis=2).reshape(-1) - 1

    inv_perm = jnp.argsort(tok_perm)
    group_no = inv_perm // n_relay
    final_idx = (lax.rem(group_no, n_chunks) * n_relay + lax.rem(inv_perm, n_relay)) * cap1 + group_no // n_chunks
    return chunk_idx, far_idx, near_idx, final_idx


N_TILE = 512
FAR_PER = 4
RELAYS = ((0, False), (0, True), (1, False), (1, True), (-1, False), (-1, True))
NEAR_ORDER = (2, 4, 3, 5, 1, 0)
FAR_ORDER = ((2, False), (1, False), (-1, False), (2, True), (1, True), (-1, True), (0, True), (0, False))


def peer(me, group, chips_on, flip):
    n_chips = group // 2
    chip = lax.rem(me // 2 + chips_on + n_chips, n_chips)
    core = lax.rem(me, 2)
    if flip:
        core = 1 - core
    return chip * 2 + core


def row_block(n, most):
    return max(d for d in range(16, most + 1, 16) if n % d == 0)


def build_pick(idx_ref, at, pick_ref, n_src):
    block = row_block(at.size, 288)

    @pl.loop(0, at.size // block)
    def _(b):
        off = pl.multiple_of(b * block, 16)
        lane = lax.broadcasted_iota(jnp.int32, (block, n_src), 1)
        hit = idx_ref[pl.ds(pl.multiple_of(at.start + off, 16), block), :] == lane
        pick_ref[pl.ds(off, block), :n_src] = hit.astype(jnp.float32).astype(pick_ref.dtype)


def gather_rows(src_ref, pick_ref, dst_ref, dst_at):
    n_src, width = src_ref.shape

    @pl.loop(0, width // N_TILE)
    def _(n):
        cols = pl.ds(pl.multiple_of(n * N_TILE, N_TILE), N_TILE)
        rows = jnp.dot(pick_ref[:dst_at.size, :n_src], src_ref[:, cols], preferred_element_type=jnp.float32)
        dst_ref[dst_at, cols] = rows.astype(dst_ref.dtype)


def norm_rows(src_ref, gain_ref, dst_ref):
    block = row_block(src_ref.shape[0], 128)
    gain = gain_ref[...].astype(jnp.float32)

    @pl.loop(0, src_ref.shape[0] // block)
    def _(b):
        at = pl.ds(pl.multiple_of(b * block, 16), block)
        rows_f = src_ref[at, :].astype(jnp.float32)
        inv_rms = lax.rsqrt(jnp.mean(rows_f * rows_f, axis=-1, keepdims=True) + NORM_EPS)
        dst_ref[at, :] = (rows_f * inv_rms * gain).astype(dst_ref.dtype)


def hop(src_ref, idx_ref, pick_ref, buf_ref, land_ref, land_local, cap, targets, per, send_sem, recv_sem, load=None):
    copies, ready = [], []
    for t0 in range(0, len(targets), per):
        for n in range(per):
            block = targets[t0 + n][1]
            build_pick(idx_ref, pl.ds(pl.multiple_of(block * cap, 16), cap), pick_ref.at[pl.ds(n * cap, cap), :], src_ref.shape[0])
        if t0 == 0 and load is not None:
            load.wait()
        for copy in ready:
            copy.start()
        ready = []
        dev, _, slot = targets[t0]
        if per == 1 and dev is None and land_local:
            gather_rows(src_ref, pick_ref, land_ref, pl.ds(pl.multiple_of(slot * cap, 16), cap))
            continue
        gather_rows(src_ref, pick_ref, buf_ref, pl.ds(t0 * cap, per * cap))
        for t in range(t0, t0 + per):
            dev, _, slot = targets[t]
            here = buf_ref.at[pl.ds(t * cap, cap), :]
            there = land_ref.at[pl.ds(pl.multiple_of(slot * cap, 16), cap), :]
            if dev is None:
                ready.append(pltpu.make_async_copy(here, there, recv_sem.at[t]))
            else:
                ready.append(pltpu.make_async_remote_copy(
                    src_ref=here, dst_ref=there, send_sem=send_sem.at[t], recv_sem=recv_sem.at[t],
                    device_id={'sp': dev}, device_id_type=pl.DeviceIdType.MESH))
        copies += ready
    return copies, ready


def two_hop_kernel(group, cap_a, cap_b, rows_ref, idx_a_ref, idx_b_ref, idx_c_ref, out_ref, later_ref, src_ref, pick_ref, buf_a_ref, mid_ref, buf_b_ref,
                   load_sem, sem_a_send, sem_a_recv, sem_b_send, sem_b_recv):
    me = lax.axis_index('sp')
    load = pltpu.make_async_copy(rows_ref, src_ref, load_sem)
    load.start()
    barrier = pltpu.get_barrier_semaphore()
    for other in range(1, group):
        pl.semaphore_signal(barrier, inc=1, device_id={'sp': lax.rem(me + other, group)}, device_id_type=pl.DeviceIdType.MESH)
    pl.semaphore_wait(barrier, group - 1)
    near = []
    for block in NEAR_ORDER:
        chips_on, flip = RELAYS[block]
        near.append((None if (chips_on == 0 and not flip) else peer(me, group, chips_on, flip), block, block))
    far = []
    for chips_on, flip in FAR_ORDER:
        dev = peer(me, group, chips_on, flip)
        far.append((None if (chips_on == 0 and not flip) else dev, dev, me))
    copies, _ = hop(src_ref, idx_a_ref, pick_ref, buf_a_ref, mid_ref, True, cap_a, near, 1, sem_a_send, sem_a_recv, load)
    for copy in copies:
        copy.wait()
    copies, ready = hop(mid_ref, idx_b_ref, pick_ref, buf_b_ref, out_ref, False, cap_b, far, FAR_PER, sem_b_send, sem_b_recv)
    n_later = idx_c_ref.shape[0]
    block = row_block(n_later, pick_ref.shape[0])
    for b in range(n_later // block):
        build_pick(idx_c_ref, pl.ds(b * block, block), pick_ref, mid_ref.shape[0])
        if b == 0:
            for copy in ready:
                copy.start()
        gather_rows(mid_ref, pick_ref, buf_a_ref, pl.ds(b * block, block))
    store = pltpu.make_async_copy(buf_a_ref.at[pl.ds(0, n_later), :], later_ref, load_sem)
    store.start()
    store.wait()
    for copy in copies:
        copy.wait()


def two_hop(src, idx_a, idx_b, idx_c, group, collective_id):
    width = src.shape[1]
    n_a, n_b = len(RELAYS), group
    rows_a, rows_b, rows_c = idx_a.shape[0], idx_b.shape[0], idx_c.shape[0]
    vmem = pl.BlockSpec(memory_space=pltpu.VMEM)
    anywhere = pl.BlockSpec(memory_space=pl.ANY)
    return pl.pallas_call(
        functools.partial(two_hop_kernel, group, rows_a // n_a, rows_b // n_b),
        out_shape=[jax.ShapeDtypeStruct((rows_b, width), src.dtype), jax.ShapeDtypeStruct((rows_c, width), src.dtype)],
        in_specs=[anywhere, vmem, vmem, vmem],
        out_specs=[anywhere, anywhere],
        scratch_shapes=[
            pltpu.VMEM(src.shape, src.dtype),
            pltpu.VMEM((max(rows_a // n_a, FAR_PER * rows_b // n_b), max(src.shape[0], rows_a)), src.dtype),
            pltpu.VMEM((max(rows_a, rows_c), width), src.dtype),
            pltpu.VMEM((rows_a, width), src.dtype),
            pltpu.VMEM((rows_b, width), src.dtype),
            pltpu.SemaphoreType.DMA(()),
            pltpu.SemaphoreType.DMA((n_a,)),
            pltpu.SemaphoreType.DMA((n_a,)),
            pltpu.SemaphoreType.DMA((n_b,)),
            pltpu.SemaphoreType.DMA((n_b,)),
        ],
        compiler_params=pltpu.CompilerParams(collective_id=collective_id, has_side_effects=True, vmem_limit_bytes=60 * 1024 * 1024),
        name="two_hop_out",
    )(src, idx_a[:, None], idx_b[:, None], idx_c[:, None])


FF_TILE = 512
BACK_CHUNKS = 3
PART_SHARE = 3


def mlp_back_kernel(group, n_chunks, cap_far, cap_near, z0_ref, z1_ref, gain_ref, chunk_idx_ref, far_idx_ref, near_idx_ref, wg_ref, wu_ref, wd_ref, out_ref,
                    pick_ref, pick2_ref, zo_ref, h2_ref, acc_ref, buf_ref, mid_ref, far_send, far_recv, near_send, near_recv, z_ref, z_sem):
    h = pl.program_id(0)
    f = pl.program_id(1)
    last_f = pl.num_programs(1) - 1
    n_rows = h2_ref.shape[0]
    block = row_block(n_rows, 80)
    width = z_ref.shape[1]
    n_far = group * cap_far
    n_near = len(RELAYS) * cap_near
    me = lax.axis_index('sp')

    def far_copies(c):
        copies = []
        for t, (chips_on, flip) in enumerate(FAR_ORDER):
            if chips_on == 0 and not flip:
                continue
            dev = peer(me, group, chips_on, flip)
            copies.append(pltpu.make_async_remote_copy(
                src_ref=buf_ref.at[pl.ds(pl.multiple_of(dev * cap_far, 16), cap_far), :],
                dst_ref=mid_ref.at[pl.ds(pl.multiple_of(c * n_far + me * cap_far, 16), cap_far), :],
                send_sem=far_send.at[c, t], recv_sem=far_recv.at[c, t],
                device_id={'sp': dev}, device_id_type=pl.DeviceIdType.MESH))
        return copies

    def near_copies(c):
        copies = []
        for t in NEAR_ORDER:
            chips_on, flip = RELAYS[t]
            src = buf_ref.at[pl.ds(t * cap_near, cap_near), :]
            dst = out_ref.at[pl.ds(c * n_near + t * cap_near, cap_near), :]
            if chips_on == 0 and not flip:
                copies.append(pltpu.make_async_copy(src, dst, near_recv.at[c, t]))
            else:
                copies.append(pltpu.make_async_remote_copy(
                    src_ref=src, dst_ref=dst, send_sem=near_send.at[c, t], recv_sem=near_recv.at[c, t],
                    device_id={'sp': peer(me, group, -chips_on, flip)}, device_id_type=pl.DeviceIdType.MESH))
        return copies

    def start_far(c):
        build_pick(far_idx_ref, pl.ds(c * n_far, n_far), pick_ref, n_rows)
        gather_rows(zo_ref.at[pl.ds(c * n_rows, n_rows), :], pick_ref, buf_ref, pl.ds(0, n_far))
        build_pick(near_idx_ref, pl.ds(c * n_near, n_near), pick2_ref, n_far)
        for copy in far_copies(c):
            copy.start()
        own = pl.multiple_of(me * cap_far, 16)
        mid_ref[pl.ds(pl.multiple_of(c * n_far + own, 16), cap_far), :] = buf_ref[pl.ds(own, cap_far), :]

    def start_near(c):
        for copy in far_copies(c):
            copy.wait()
        gather_rows(mid_ref.at[pl.ds(c * n_far, n_far), :], pick2_ref, buf_ref, pl.ds(0, n_near))
        for copy in near_copies(c):
            copy.start()

    def end_near(c):
        for copy in near_copies(c):
            copy.wait()

    @pl.when((h == 0) & (f == 0))
    def _():
        n_first = z0_ref.shape[0]
        loads = [pltpu.make_async_copy(z0_ref, z_ref.at[pl.ds(0, n_first), :], z_sem.at[0]),
                 pltpu.make_async_copy(z1_ref, z_ref.at[pl.ds(n_first, z1_ref.shape[0]), :], z_sem.at[1])]
        for load in loads:
            load.start()
        for load in loads:
            load.wait()
        barrier = pltpu.get_barrier_semaphore()
        for other in range(1, group):
            pl.semaphore_signal(barrier, inc=1, device_id={'sp': lax.rem(me + other, group)}, device_id_type=pl.DeviceIdType.MESH)
        pl.semaphore_wait(barrier, group - 1)

    for c in range(n_chunks):
        zo = zo_ref.at[pl.ds(c * n_rows, n_rows), :]

        @pl.when((h == c) & (f == 0))
        def _():
            build_pick(chunk_idx_ref, pl.ds(c * n_rows, n_rows), pick_ref, z_ref.shape[0])
            gather_rows(z_ref, pick_ref, zo, pl.ds(0, n_rows))
            norm_rows(zo, gain_ref, h2_ref)
            acc_ref[...] = jnp.zeros(acc_ref.shape, jnp.float32)

        if c > 0:
            @pl.when((h == c) & (f == (last_f + 1) // 2))
            def _():
                start_near(c - 1)

    gate = jnp.dot(h2_ref[...], wg_ref[...], preferred_element_type=jnp.float32)
    up = jnp.dot(h2_ref[...], wu_ref[...], preferred_element_type=jnp.float32)
    act = (gate * jax.nn.sigmoid(gate) * up).astype(jnp.bfloat16)
    acc_ref[...] += jnp.dot(act, wd_ref[...], preferred_element_type=jnp.float32)

    for c in range(n_chunks):
        zo = zo_ref.at[pl.ds(c * n_rows, n_rows), :]

        @pl.when((h == c) & (f == last_f))
        def _():
            if c > 0:
                end_near(c - 1)

            @pl.loop(0, n_rows // block)
            def _(b):
                at = pl.ds(pl.multiple_of(b * block, 16), block)
                down = acc_ref[at, :].astype(jnp.bfloat16).astype(jnp.float32)
                zo[at, :] = (zo[at, :].astype(jnp.float32) + down).astype(zo_ref.dtype)

            start_far(c)
            if c == n_chunks - 1:
                start_near(c)
                end_near(c)


def mlp_back(z_parts, gain, chunk_idx, far_idx, near_idx, w_gate, w_up, w_down, group, n_rows, cap_far, cap_near, collective_id):
    z = z_parts[0]
    width = z.shape[1]
    n_src = sum(part.shape[0] for part in z_parts)
    ff = w_gate.shape[1]
    n_chunks = BACK_CHUNKS
    n_far, n_near = group * cap_far, len(RELAYS) * cap_near
    whole = lambda shape: pl.BlockSpec(shape, lambda h, f: (0, 0), pipeline_mode=pl.Buffered(1))
    return pl.pallas_call(
        functools.partial(mlp_back_kernel, group, n_chunks, cap_far, cap_near),
        out_shape=jax.ShapeDtypeStruct((n_chunks * n_near, width), z.dtype),
        grid=(n_chunks, ff // FF_TILE),
        in_specs=[
            pl.BlockSpec(memory_space=pl.ANY), pl.BlockSpec(memory_space=pl.ANY), whole((1, width)), whole((n_chunks * n_rows, 1)), whole((n_chunks * n_far, 1)), whole((n_chunks * n_near, 1)),
            pl.BlockSpec((width, FF_TILE), lambda h, f: (0, f)),
            pl.BlockSpec((width, FF_TILE), lambda h, f: (0, f)),
            pl.BlockSpec((FF_TILE, width), lambda h, f: (f, 0)),
        ],
        out_specs=pl.BlockSpec(memory_space=pl.ANY),
        scratch_shapes=[
            pltpu.VMEM((max(n_rows, n_far), max(n_src, n_rows)), z.dtype),
            pltpu.VMEM((n_near, n_far), z.dtype),
            pltpu.VMEM((n_chunks * n_rows, width), z.dtype),
            pltpu.VMEM((n_rows, width), z.dtype),
            pltpu.VMEM((n_rows, width), jnp.float32),
            pltpu.VMEM((max(n_far, n_near), width), z.dtype),
            pltpu.VMEM((n_chunks * n_far, width), z.dtype),
            pltpu.SemaphoreType.DMA((n_chunks, group)),
            pltpu.SemaphoreType.DMA((n_chunks, group)),
            pltpu.SemaphoreType.DMA((n_chunks, len(RELAYS))),
            pltpu.SemaphoreType.DMA((n_chunks, len(RELAYS))),
            pltpu.VMEM((n_src, width), z.dtype),
            pltpu.SemaphoreType.DMA((2,)),
        ],
        compiler_params=pltpu.CompilerParams(collective_id=collective_id, has_side_effects=True, vmem_limit_bytes=63 * 1024 * 1024,
                                             dimension_semantics=("arbitrary", "arbitrary")),
        name="mlp_back",
    )(*z_parts, gain.reshape(1, width), chunk_idx[:, None], far_idx[:, None], near_idx[:, None], w_gate, w_up, w_down)


def solution(mesh):
    row_spec = P(('dp', 'sp'), None)
    vec_spec = P(('dp', 'sp'))
    rep_spec = P()

    def per_device(hidden, tok_perm, send_off, send_len, recv_off, recv_len, recv_doc, recv_pos, g_attn, w_q, w_k, w_v, w_o, g_mlp, w_gate, w_up, w_down):
        n_tok, model_dim = hidden.shape
        n_cap = recv_doc.shape[0]
        group = send_off.shape[0]
        relay_of, source_of = relay_tables(group)
        n_relay = relay_of.shape[1]
        round_up = lambda n, unit: -(-n // unit) * unit
        cap1 = round_up(-(-n_tok // n_relay), 16)
        n_first = n_cap // PART_SHARE
        n_parts = (n_first, n_cap - n_first)
        cap2 = [round_up((n + n_relay * (n_relay - 1)) // n_relay, 16) for n in n_parts]
        n_classes = n_relay * BACK_CHUNKS
        cap1_back = round_up(-(-n_tok // n_classes), 16)
        cap2_back = round_up((n_cap + n_relay * (n_classes - 1)) // n_classes, 16)
        n_rows = round_up(-(-(n_cap + group * n_relay * (BACK_CHUNKS - 1)) // BACK_CHUNKS), 16)
        me = lax.axis_index('sp')
        len_ij = lax.all_gather(send_len, 'sp')
        send_idx = jnp.pad(tok_perm, (0, cap1 * n_relay - n_tok)).reshape(cap1, n_relay).T.reshape(-1)
        relay_0, dest_0 = out_indices(me, len_ij, 0, n_parts[0], cap1, cap2[0], relay_of, source_of)
        relay_1, dest_1 = out_indices(me, len_ij, n_first, n_parts[1], cap1, cap2[1], relay_of, source_of)
        chunk_idx, far_idx, near_idx, final_idx = back_indices(me, len_ij, tok_perm, n_rows, cap1_back, cap2_back, source_of, BACK_CHUNKS)

        def take(rows, index):
            return rows.at[index].get(mode='promise_in_bounds')

        blocks_0, later = two_hop(hidden, send_idx, relay_0, relay_1, group, 0)
        blocks_1 = lax.all_to_all(later.reshape(group, cap2[1], model_dim), 'sp', 0, 0, tiled=True).reshape(group * cap2[1], model_dim)
        z_parts = attn_layer([(blocks_0, dest_0), (blocks_1, dest_1)], recv_doc, recv_pos, g_attn, w_q, w_k, w_v, w_o)
        src_back = mlp_back(z_parts, g_mlp, chunk_idx, far_idx, near_idx, w_gate, w_up, w_down, group, n_rows, cap2_back, cap1_back, 1)
        return take(src_back, final_idx)

    return jax.shard_map(per_device, mesh=mesh, in_specs=(row_spec,) + (vec_spec,) * 7 + (rep_spec,) * 9, out_specs=row_spec, check_vma=False)
```

time: 816 us -> 770 us (0.944)
  Pallas kernels: 672 us -> 646 us
  other arithmetic: 32.6 us -> 17.9 us
  local copies, waits for them, and re-layouts: 70.9 us -> 61.3 us
    pallas_call x5, Pallas kernels: 361 us -> 331 us  [the longest x1 156 us: two_hop(): pl.pallas_call(functools.partial(two_hop_kernel, group, rows_a // n_a, ro...]
    gather x2 -> x1, local copies, waits for them, and re-layouts: 47.9 us -> 30.2 us  [take(): return rows.at[index].get(mode='promise_in_bounds')]
    another operation x7 -> x3, other arithmetic: 13 us -> 0.63 us  [attention(): meta = jnp.stack([doc_ids, positions])[:, :n_keys]]
    dot_general x1 -> x2, matrix products: 20.3 us -> 23.6 us  [attn_layer(): jnp.dot(heads, w_out, preferred_element_type=jnp.float32)]
  transfers between devices with their start and end apart: 0 -> 1, of which waited for: 0 -> 0; matrix products, arithmetic and copies ran while one was open for 0% -> 6% of each run, Pallas kernels for 0% -> 7%
where the time goes in v4:
time: 770 us; the launch traced here: 765 us
  Pallas kernels  646 us (84%)
  local copies, waits for them, and re-layouts  61.3 us (8%)
  matrix products  23.6 us (3%)
  other arithmetic  17.9 us (2%)
  blocking collectives  8.9 us (1%)
    pallas_call x1, Pallas kernels, mlp_back(): pl.pallas_call(functools.partial(mlp_back_kernel, group, n_chunks, cap_fa...  315 us
    pallas_call x1, Pallas kernels, two_hop(): pl.pallas_call(functools.partial(two_hop_kernel, group, rows_a // n_a, ro...  156 us
    pallas_call x2, Pallas kernels, qkv_proj(): pl.pallas_call(functools.partial(qkv_kernel, head_dim), out_shape=[jax.Sh...  90.2 us
    pallas_call x2, Pallas kernels, attention(): pl.pallas_call(functools.partial(attn_kernel, head_dim, n_parts), out_sha...  84.7 us
    gather x1, local copies, waits for them, and re-layouts, take(): return rows.at[index].get(mode='promise_in_bounds')  30.2 us
    dot_general x2, matrix products, attn_layer(): jnp.dot(heads, w_out, preferred_element_type=jnp.float32)  23.6 us
  transfers between devices with their start and end apart: 1, of which 0 were waited for; matrix products, arithmetic and copies ran while one was open for 6% of the time, Pallas kernels for 7%

profile of v4, /device:TPU:113, one launch (start us, length us, event | category | flops | bytes accessed | tf_op | source)
XLA Modules:
  0.0 765.3 jit_solution(15863031877652843075)
XLA Ops:
  0.0 1.2 dynamic-slice.20
  1.9 0.9 dynamic-update-slice
  2.8 8.9 %all-reduce = s32[64]{0:T(128)S(1)} all-reduce(s32[64]{0:T(128)S(1)} %dynamic-update-slice), channel_id=2, replica_groups=mesh['dp'=2,'sp'=8] {'sp'}, use_global_device_ids=true, to_apply=%add | all-reduce | flops 64 | bytes 512
  11.9 0.8 select_reduce_fusion.10
  12.9 0.9 gather_fusion
  14.4 0.9 gather_fusion.2
  15.6 0.9 gather_fusion.3
  16.8 0.8 select_reduce_fusion.4
  17.6 0.9 gather_fusion.1
  19.1 1.1 broadcast_in_dim_reshape.20.idx_c_ref
  20.4 1.0 broadcast_in_dim_reshape.19.idx_b_ref
  21.4 0.9 reshape.412
  22.4 1.7 copy.288
  24.1 156.0 %two_hop_out.1 = (bf16[768,2048]{1,0:T(8,128)(2,1)}, bf16[1408,2048]{1,0:T(8,128)(2,1)}) custom-call(bf16[3072,2048]{1,0:T(8,128)(2,1)} %rows_ref.1, s32[3072,1]{1,0:T(8,128)} %bitcast.141, s32[768,1]{1,0:T(8,128)} %broadcast_in_dim_reshape.19.idx_b_ref, s32[1408,1]{1,0:T(8,128)} %broadcast_in_dim_reshape.20.idx_c_ref), custom_call_target="tpu_custom_call" | custom-call | tf_op jit(solution)/shard_map/two_hop_out/pallas_call | solution.py:399
  180.2 5.4 all-to-all-start
  186.2 1.4 gather_fusion.6
  187.9 1.4 gather_fusion.7
  189.8 0.8 gather_fusion.5
  191.1 0.2 copy.270
  191.4 0.2 copy.267
  191.6 0.6 reshape.414.gain_ref
  192.4 0.8 gather_fusion.4
  193.7 0.9 copy.261
  194.6 0.9 copy.258
  195.5 1.0 copy.271
  196.5 0.9 copy.286
  197.9 0.8 gather_fusion.8
  198.7 0.2 select_reduce_fusion.1
  199.0 1.6 sub.272.chunk_idx_ref
  200.8 0.2 copy.279
  201.4 2.0 sub.273.near_idx_ref
  203.5 2.8 fusion.3
  206.3 2.1 select_n.282.far_idx_ref
  208.4 0.6 reshape.422.gain_ref
  209.0 5.8 sort.17
  214.8 1.3 pad_maximum_fusion.6
  216.1 2.0 pad_maximum_fusion
  218.1 0.6 pad_add_fusion.refs_4_
  218.8 0.8 fusion.2.idx_ref
  219.6 1.1 fusion.idx_ref
  220.7 34.8 %qkv.2 = (bf16[512,2048]{1,0:T(8,128)(2,1)}, bf16[512,2048]{1,0:T(8,128)(2,1)}, bf16[512,2048]{1,0:T(8,128)(2,1)}, bf16[512,2048]{1,0:T(8,128)(2,1)}) custom-call(bf16[768,2048]{1,0:T(8,128)(2,1)} %get-tuple-element.16.blocks_ref, s32[512,1]{1,0:T(8,128)} %fusion.2.idx_ref, bf16[1,2048]{1,0:T(2,128)(2,1)} %reshape.414.gain_ref, ...), custom_call_target="tpu_custom_call" | custom-call | flops 12884901888 | bytes 25165824 | tf_op jit(solution)/shard_map/qkv/pallas_call | solution.py:65
  255.5 17.6 %attention.2 = bf16[512,2048]{1,0:T(8,128)(2,1)} custom-call(bf16[512,2048]{1,0:T(8,128)(2,1)} %get-tuple-element.18.q_ref, bf16[512,2048]{1,0:T(8,128)(2,1)} %get-tuple-element.19.refs_0_, bf16[512,2048]{1,0:T(8,128)(2,1)} %get-tuple-element.20.refs_1_.refs_2_, s32[2,512]{1,0:T(2,128)} %copy-done.4, s32[512,2]{1,0:T(8,128)} %bitcast.146), custom_call_target="tpu_custom_call" | custom-call | flops 4294967296 | bytes 8388608 | tf_op jit(solution)/shard_map/attention/pallas_call | solution.py:136
  273.2 9.8 %add_convert_fusion.1.z0_ref = bf16[512,2048]{1,0:T(8,128)(2,1)} fusion(bf16[512,2048]{1,0:T(8,128)(2,1)S(1)} %copy-done.19, bf16[512,2048]{1,0:T(8,128)(2,1)} %attention.2, bf16[2048,2048]{1,0:T(8,128)(2,1)} %bitcast.166), kind=kOutput, calls=%fused_computation.11 | convolution fusion | flops 4300210176 | bytes 14680064 | tf_op jit(solution)/shard_map/dot_general | solution.py:161
  283.0 55.4 %qkv.3 = (bf16[1024,2048]{1,0:T(8,128)(2,1)}, bf16[1024,2048]{1,0:T(8,128)(2,1)}, bf16[1024,2048]{1,0:T(8,128)(2,1)}, bf16[1024,2048]{1,0:T(8,128)(2,1)}) custom-call(bf16[1408,2048]{1,0:T(8,128)(2,1)} %bitcast.27.blocks_ref, s32[1024,1]{1,0:T(8,128)} %fusion.idx_ref, bf16[1,2048]{1,0:T(2,128)(2,1)} %reshape.414.gain_ref, ...), custom_call_target="tpu_custom_call" | custom-call | flops 25769803776 | bytes 25165824 | tf_op jit(solution)/shard_map/qkv/pallas_call | solution.py:65
  338.4 67.1 %attention.3 = bf16[1024,2048]{1,0:T(8,128)(2,1)} custom-call(bf16[1024,2048]{1,0:T(8,128)(2,1)} %get-tuple-element.23.q_ref, bf16[512,2048]{1,0:T(8,128)(2,1)} %get-tuple-element.19.refs_0_, bf16[1024,2048]{1,0:T(8,128)(2,1)} %get-tuple-element.24.refs_1_, bf16[512,2048]{1,0:T(8,128)(2,1)} %get-tuple-element.20.refs_1_.refs_2_, ...), custom_call_target="tpu_custom_call" | custom-call | flops 34359738368 | bytes 16777216 | tf_op jit(solution)/shard_map/attention/pallas_call | solution.py:136
  405.5 13.8 %add_convert_fusion.z1_ref = bf16[1024,2048]{1,0:T(8,128)(2,1)} fusion(bf16[1024,2048]{1,0:T(8,128)(2,1)S(1)} %copy-done.18, bf16[1024,2048]{1,0:T(8,128)(2,1)} %attention.3, bf16[2048,2048]{1,0:T(8,128)(2,1)} %bitcast.167), kind=kOutput, calls=%fused_computation.10 | convolution fusion | flops 8600420352 | bytes 20971520 | tf_op jit(solution)/shard_map/dot_general | solution.py:161
  419.3 315.4 %mlp_back.1 = bf16[3168,2048]{1,0:T(8,128)(2,1)} custom-call(bf16[512,2048]{1,0:T(8,128)(2,1)} %add_convert_fusion.1.z0_ref, bf16[1024,2048]{1,0:T(8,128)(2,1)} %add_convert_fusion.z1_ref, bf16[1,2048]{1,0:T(2,128)(2,1)} %reshape.422.gain_ref, s32[1632,1]{1,0:T(8,128)} %sub.272.chunk_idx_ref, s32[2304,1]{1,0:T(8,128)} %select_n.282.far_idx_ref, ...), custom_call_target="tpu_custom_call" | custom-call | tf_op jit(solution)/shard_map/mlp_back/pallas_call | solution.py:547
  734.7 30.2 %gather_fusion.9 = bf16[3072,2048]{1,0:T(8,128)(2,1)} fusion(bf16[3168,2048]{1,0:T(8,128)(2,1)} %mlp_back.1, s32[3072]{0:T(1024)S(1)} %fusion.62), kind=kCustom, calls=%fused_computation.9 | custom fusion | bytes 25178112 | tf_op jit(solution)/shard_map/gather | solution.py:607
  (149 shorter events, 6.1 us)
Async XLA Ops:
  180.2 5.7 copy-start.3
  180.2 5.7 copy-start.5
  180.2 5.9 copy-start.11
  180.2 5.9 copy-start.13
  180.2 9.6 %copy-start.15 = (s32[48]{0:T(128)S(1)}, s32[48]{0:T(128)}, u32[]{:S(2)}) copy-start(s32[48]{0:T(128)} %constant.332) | copy-start | bytes 580
  180.2 102.8 %all-to-all-start = ((bf16[8,176,2048]{2,1,0:T(8,128)(2,1)}), bf16[8,176,2048]{2,1,0:T(8,128)(2,1)}, u32[]{:S(2)}, u32[]{:S(2)}) async-start(bf16[8,176,2048]{2,1,0:T(8,128)(2,1)} %bitcast.142), calls=%async_computation | async-start | bytes 11534336 | tf_op jit(solution)/shard_map/all_to_all | solution.py:610
  185.6 4.9 copy-start.17
  185.7 5.9 copy-start.8
  185.9 10.6 %copy-start.4 = (s32[2,512]{1,0:T(2,128)}, s32[2,512]{1,0:T(2,128)S(1)}, u32[]{:S(2)}) copy-start(s32[2,512]{1,0:T(2,128)S(1)} %fusion.66.refs_2_) | copy-start | bytes 12292
  189.8 3.4 copy-start.16
  190.6 7.0 copy-start.6
  190.6 7.2 copy-start.14
  190.6 7.2 copy-start.12
  193.2 7.8 %copy-start.7 = (pred[6,6]{1,0:T(8,128)(4,1)S(1)}, pred[6,6]{1,0:T(8,128)(4,1)}, u32[]{:S(2)}) copy-start(pred[6,6]{1,0:T(8,128)(4,1)} %constant.192.clone) | copy-start | bytes 112
  195.5 7.9 %copy-start.10 = (pred[8,8]{1,0:T(8,128)(4,1)S(1)}, pred[8,8]{1,0:T(8,128)(4,1)}, u32[]{:S(2)}) copy-start(pred[8,8]{1,0:T(8,128)(4,1)} %constant.188.clone) | copy-start | bytes 196
  198.7 9.7 %copy-start.9 = (bf16[2048]{0:T(1024)(128)(2,1)S(1)}, bf16[2048]{0:T(1024)(128)(2,1)}, u32[]{:S(2)}) copy-start(bf16[2048]{0:T(1024)(128)(2,1)} %param.76) | copy-start | bytes 12292
  198.7 10.3 %copy-start.2 = (s32[3072]{0:T(1024)S(1)}, s32[3072]{0:T(1024)}, u32[]{:S(2)}) copy-start(s32[3072]{0:T(1024)} %param.67) | copy-start | bytes 36868
  214.8 4.0 copy-start
  214.8 4.0 copy-start.1
  255.5 17.7 %copy-start.19 = (bf16[512,2048]{1,0:T(8,128)(2,1)S(1)}, bf16[512,2048]{1,0:T(8,128)(2,1)}, u32[]{:S(2)}) copy-start(bf16[512,2048]{1,0:T(8,128)(2,1)} %get-tuple-element.17) | copy-start | bytes 6291460
  338.4 67.1 %copy-start.18 = (bf16[1024,2048]{1,0:T(8,128)(2,1)S(1)}, bf16[1024,2048]{1,0:T(8,128)(2,1)}, u32[]{:S(2)}) copy-start(bf16[1024,2048]{1,0:T(8,128)(2,1)} %get-tuple-element.22) | copy-start | bytes 12582916

commit v5 on v4

--- a/solution.py
+++ b/solution.py
@@ -94,9 +94,12 @@
     lo = 0
     for k_part, v_part in zip(k_parts, v_parts):
         hi = lo + k_part.shape[0]
-        k_ref[lo:hi, :] = k_part[...]
-        v_ref[lo:hi, :] = v_part[...]
+        if n_parts > 1:
+            k_ref[lo:hi, :] = k_part[...]
+            v_ref[lo:hi, :] = v_part[...]
         lo = hi
+    if n_parts == 1:
+        k_ref, v_ref = k_parts[0], v_parts[0]
     low = lax.broadcasted_iota(jnp.int32, (Q_TILE, lanes), 1) < head_dim
 
     def scores(t):
@@ -184,6 +187,16 @@
     return jnp.moveaxis(jnp.sum(jnp.where(before, x[..., :, None], 0), axis=-2), -1, axis)
 
 
+def by_relay(x, source_of):
+    group = source_of.shape[0]
+    mask = source_of.T[:, None, :] == np.arange(group)[:, None]
+    rows = []
+    for k in range(group):
+        mask_k = mask[:, :, k].T.reshape((group,) + (1,) * (x.ndim - 3) + (-1, 1))
+        rows.append(jnp.sum(jnp.where(mask_k, x, 0), axis=0))
+    return jnp.stack(rows)
+
+
 def pick(table, index, n):
     return jnp.sum(jnp.where(index[:, None] == jnp.arange(n)[None, :], table[None, :], 0), axis=1)
 
@@ -204,9 +217,8 @@
     len_ij = jnp.clip(roff_all + len_ij, lo, lo + n_rows) - roff_ij
     off_ij = jnp.where(len_ij > 0, off_ij, 0)
     first, count = run_tables(off_ij, len_ij, n_relay)
-    res = np.arange(n_relay)
-    first_k = first[source_of, res]
-    count_k = count[source_of, res]
+    first_k = by_relay(first, source_of)
+    count_k = by_relay(count, source_of)
     base_k = sum_before(count_k, 1)
 
     def mine(t, axis=0):
@@ -220,9 +232,8 @@
 
     len_me, off_me, roff_me = mine(len_ij, 1), mine(off_ij, 1), mine(roff_ij, 1)
     base_to_me, first_to_me = mine(base_k, 2), mine(first, 2)
-    place = np.zeros((group, n_relay), np.int32)
-    place[source_of, res] = np.arange(group)[:, None] * n_relay + res
-    table = relay_of * cap2 + base_to_me.reshape(-1)[place] - first_to_me
+    base_ic = jnp.sum(jnp.where(relay_of[:, :, None] == np.arange(group), base_to_me.T[None], 0), axis=-1)
+    table = relay_of * cap2 + base_ic - first_to_me
     u = lo + jnp.arange(n_rows)
     in_i = (u[:, None] >= roff_me[None, :]) & (u[:, None] < (roff_me + len_me)[None, :])
     r_of_u = jnp.sum(jnp.where(in_i, off_me[None, :] + u[:, None] - roff_me[None, :], 0), axis=1)
@@ -238,8 +249,8 @@
     roff_ij = sum_before(len_ij, 0)
     first, count = run_tables(off_ij, len_ij, n_classes)
     cls = (np.arange(n_chunks)[:, None] * n_relay + np.arange(n_relay)[None, :])
-    first_k = first[source_of[:, None, :], cls[None]]
-    count_k = count[source_of[:, None, :], cls[None]]
+    first_k = by_relay(first.reshape(group, n_chunks, n_relay, group), source_of)
+    count_k = by_relay(count.reshape(group, n_chunks, n_relay, group), source_of)
     base_k = sum_before(count_k, 2)
 
     def mine(t, axis=0):
@@ -248,7 +259,8 @@
     cnt = mine(count_k, 3).transpose(1, 0, 2).reshape(n_chunks, -1)
     fst = mine(first_k, 3).transpose(1, 0, 2).reshape(n_chunks, -1)
     start = sum_before(cnt, 1)
-    shift = jnp.broadcast_to(cls[:, None, :] + mine(roff_ij - off_ij, 1)[source_of][None], (n_chunks, group, n_relay)).reshape(n_chunks, -1)
+    moved = jnp.sum(jnp.where(source_of[:, :, None] == np.arange(group), mine(roff_ij - off_ij, 1), 0), axis=-1)
+    shift = (cls[:, None, :] + moved[None]).reshape(n_chunks, -1)
     p = jnp.arange(n_rows)
     in_run = (p >= start[:, :, None]) & (p < (start + cnt)[:, :, None])
     u_of_p = (fst[:, :, None] + p - start[:, :, None]) * n_classes + shift[:, :, None]
@@ -272,7 +284,7 @@
 
 
 N_TILE = 512
-FAR_PER = 4
+FAR_PER = 2
 RELAYS = ((0, False), (0, True), (1, False), (1, True), (-1, False), (-1, True))
 NEAR_ORDER = (2, 4, 3, 5, 1, 0)
 FAR_ORDER = ((2, False), (1, False), (-1, False), (2, True), (1, True), (-1, True), (0, True), (0, False))
@@ -453,7 +465,7 @@
         for t in NEAR_ORDER:
             chips_on, flip = RELAYS[t]
             src = buf_ref.at[pl.ds(t * cap_near, cap_near), :]
-            dst = out_ref.at[pl.ds(c * n_near + t * cap_near, cap_near), :]
+            dst = out_ref.at[pl.ds(pl.multiple_of(c * n_near + t * cap_near, 16), cap_near), :]
             if chips_on == 0 and not flip:
                 copies.append(pltpu.make_async_copy(src, dst, near_recv.at[c, t]))
             else:
@@ -463,9 +475,9 @@
         return copies
 
     def start_far(c):
-        build_pick(far_idx_ref, pl.ds(c * n_far, n_far), pick_ref, n_rows)
-        gather_rows(zo_ref.at[pl.ds(c * n_rows, n_rows), :], pick_ref, buf_ref, pl.ds(0, n_far))
-        build_pick(near_idx_ref, pl.ds(c * n_near, n_near), pick2_ref, n_far)
+        build_pick(far_idx_ref, pl.ds(pl.multiple_of(c * n_far, 16), n_far), pick_ref, n_rows)
+        gather_rows(zo_ref.at[pl.ds(pl.multiple_of(c * n_rows, 16), n_rows), :], pick_ref, buf_ref, pl.ds(0, n_far))
+        build_pick(near_idx_ref, pl.ds(pl.multiple_of(c * n_near, 16), n_near), pick2_ref, n_far)
         for copy in far_copies(c):
             copy.start()
         own = pl.multiple_of(me * cap_far, 16)
@@ -474,8 +486,14 @@
     def start_near(c):
         for copy in far_copies(c):
             copy.wait()
-        gather_rows(mid_ref.at[pl.ds(c * n_far, n_far), :], pick2_ref, buf_ref, pl.ds(0, n_near))
-        for copy in near_copies(c):
+        mid = mid_ref.at[pl.ds(pl.multiple_of(c * n_far, 16), n_far), :]
+        n_own = 2 * cap_near
+        gather_rows(mid, pick2_ref.at[pl.ds(n_own, n_near - n_own), :], buf_ref, pl.ds(n_own, n_near - n_own))
+        copies = near_copies(c)
+        for copy in copies[:-2]:
+            copy.start()
+        gather_rows(mid, pick2_ref, buf_ref, pl.ds(0, n_own))
+        for copy in copies[-2:]:
             copy.start()
 
     def end_near(c):
@@ -496,44 +514,42 @@
             pl.semaphore_signal(barrier, inc=1, device_id={'sp': lax.rem(me + other, group)}, device_id_type=pl.DeviceIdType.MESH)
         pl.semaphore_wait(barrier, group - 1)
 
-    for c in range(n_chunks):
-        zo = zo_ref.at[pl.ds(c * n_rows, n_rows), :]
-
-        @pl.when((h == c) & (f == 0))
-        def _():
-            build_pick(chunk_idx_ref, pl.ds(c * n_rows, n_rows), pick_ref, z_ref.shape[0])
-            gather_rows(z_ref, pick_ref, zo, pl.ds(0, n_rows))
-            norm_rows(zo, gain_ref, h2_ref)
-            acc_ref[...] = jnp.zeros(acc_ref.shape, jnp.float32)
-
-        if c > 0:
-            @pl.when((h == c) & (f == (last_f + 1) // 2))
-            def _():
-                start_near(c - 1)
+    zo = zo_ref.at[pl.ds(pl.multiple_of(h * n_rows, 16), n_rows), :]
+
+    @pl.when(f == 0)
+    def _():
+        build_pick(chunk_idx_ref, pl.ds(pl.multiple_of(h * n_rows, 16), n_rows), pick_ref, z_ref.shape[0])
+        gather_rows(z_ref, pick_ref, zo, pl.ds(0, n_rows))
+        norm_rows(zo, gain_ref, h2_ref)
+        acc_ref[...] = jnp.zeros(acc_ref.shape, jnp.float32)
+
+    @pl.when((h > 0) & (f == (last_f + 1) // 2))
+    def _():
+        start_near(h - 1)
 
     gate = jnp.dot(h2_ref[...], wg_ref[...], preferred_element_type=jnp.float32)
     up = jnp.dot(h2_ref[...], wu_ref[...], preferred_element_type=jnp.float32)
     act = (gate * jax.nn.sigmoid(gate) * up).astype(jnp.bfloat16)
     acc_ref[...] += jnp.dot(act, wd_ref[...], preferred_element_type=jnp.float32)
 
-    for c in range(n_chunks):
-        zo = zo_ref.at[pl.ds(c * n_rows, n_rows), :]
-
-        @pl.when((h == c) & (f == last_f))
-        def _():
-            if c > 0:
-                end_near(c - 1)
-
-            @pl.loop(0, n_rows // block)
-            def _(b):
-                at = pl.ds(pl.multiple_of(b * block, 16), block)
-                down = acc_ref[at, :].astype(jnp.bfloat16).astype(jnp.float32)
-                zo[at, :] = (zo[at, :].astype(jnp.float32) + down).astype(zo_ref.dtype)
-
-            start_far(c)
-            if c == n_chunks - 1:
-                start_near(c)
-                end_near(c)
+    @pl.when((h > 0) & (f == last_f))
+    def _():
+        end_near(h - 1)
+
+    @pl.when(f == last_f)
+    def _():
+        @pl.loop(0, n_rows // block)
+        def _(b):
+            at = pl.ds(pl.multiple_of(b * block, 16), block)
+            down = acc_ref[at, :].astype(jnp.bfloat16).astype(jnp.float32)
+            zo[at, :] = (zo[at, :].astype(jnp.float32) + down).astype(zo_ref.dtype)
+
+        start_far(h)
+
+    @pl.when((h == n_chunks - 1) & (f == last_f))
+    def _():
+        start_near(h)
+        end_near(h)
 
 
 def mlp_back(z_parts, gain, chunk_idx, far_idx, near_idx, w_gate, w_up, w_down, group, n_rows, cap_far, cap_near, collective_id):

time: 770 us -> 756 us (0.982)
  local copies, waits for them, and re-layouts: 61.3 us -> 52.8 us
    gather x21 -> x0, local copies, waits for them, and re-layouts: 9.89 us -> none  [the longest x6 2.16 us: out_indices(): first_k = first[source_of, res]]
  transfers between devices with their start and end apart: 1 -> 1, of which waited for: 0 -> 0; matrix products, arithmetic and copies ran while one was open for 6% -> 5% of each run, Pallas kernels for 7% -> 7%
where the time goes in v5:
time: 756 us; the launch traced here: 752 us
  Pallas kernels  640 us (85%)
  local copies, waits for them, and re-layouts  52.8 us (7%)
  matrix products  23.6 us (3%)
  other arithmetic  19.5 us (3%)
  blocking collectives  8.9 us (1%)
    pallas_call x1, Pallas kernels, mlp_back(): pl.pallas_call(functools.partial(mlp_back_kernel, group, n_chunks, cap_fa...  312 us
    pallas_call x1, Pallas kernels, two_hop(): pl.pallas_call(functools.partial(two_hop_kernel, group, rows_a // n_a, ro...  154 us
    pallas_call x2, Pallas kernels, qkv_proj(): pl.pallas_call(functools.partial(qkv_kernel, head_dim), out_shape=[jax.Sh...  90.2 us
    pallas_call x2, Pallas kernels, attention(): pl.pallas_call(functools.partial(attn_kernel, head_dim, n_parts), out_sha...  84.6 us
    gather x1, local copies, waits for them, and re-layouts, take(): return rows.at[index].get(mode='promise_in_bounds')  30.2 us
    dot_general x2, matrix products, attn_layer(): jnp.dot(heads, w_out, preferred_element_type=jnp.float32)  23.6 us
  transfers between devices with their start and end apart: 1, of which 0 were waited for; matrix products, arithmetic and copies ran while one was open for 5% of the time, Pallas kernels for 7%

profile of v5, /device:TPU:113, one launch (start us, length us, event | category | flops | bytes accessed | tf_op | source)
XLA Modules:
  0.0 752.1 jit_solution(14688361353685585828)
XLA Ops:
  0.0 1.2 dynamic-slice.20
  1.9 0.9 dynamic-update-slice
  2.8 8.9 %all-reduce = s32[64]{0:T(128)S(1)} all-reduce(s32[64]{0:T(128)S(1)} %dynamic-update-slice), channel_id=2, replica_groups=mesh['dp'=2,'sp'=8] {'sp'}, use_global_device_ids=true, to_apply=%add | all-reduce | flops 64 | bytes 512
  11.9 0.8 select_reduce_fusion.61
  12.8 1.3 select_reduce_fusion.53
  15.5 0.8 select_reduce_fusion.4
  18.0 1.1 broadcast_in_dim_reshape.20.idx_c_ref
  19.2 1.0 broadcast_in_dim_reshape.19.idx_b_ref
  20.2 0.9 reshape.398
  21.3 1.7 copy.363
  22.9 153.9 %two_hop_out.1 = (bf16[768,2048]{1,0:T(8,128)(2,1)}, bf16[1408,2048]{1,0:T(8,128)(2,1)}) custom-call(bf16[3072,2048]{1,0:T(8,128)(2,1)} %rows_ref.1, s32[3072,1]{1,0:T(8,128)} %bitcast.236, s32[768,1]{1,0:T(8,128)} %broadcast_in_dim_reshape.19.idx_b_ref, s32[1408,1]{1,0:T(8,128)} %broadcast_in_dim_reshape.20.idx_c_ref), custom_call_target="tpu_custom_call" | custom-call | tf_op jit(solution)/shard_map/two_hop_out/pallas_call | solution.py:411
  177.0 4.9 all-to-all-start
  182.3 0.1 copy.329
  182.4 0.1 copy.337
  182.9 0.2 copy.341
  183.1 0.2 copy.338
  183.4 0.6 reshape.399.gain_ref
  184.2 0.9 copy.333
  185.1 0.9 copy.330
  186.0 1.0 copy.342
  187.0 0.9 copy.361
  187.9 0.6 select_reduce_fusion.16
  188.7 0.1 constant_dynamic-slice_fusion.1
  188.8 0.3 copy.351
  189.0 0.1 bitcast_reduce_fusion
  189.4 0.3 copy.352
  190.0 0.2 select_reduce_fusion.1
  190.3 1.6 sub.276.chunk_idx_ref
  191.9 0.1 select_reduce_fusion
  192.1 0.2 select_reduce_fusion.3
  192.2 2.0 sub.277.near_idx_ref
  194.3 2.8 fusion.3
  197.2 2.1 select_n.433.far_idx_ref
  199.3 0.6 reshape.406.gain_ref
  199.9 5.8 sort.17
  205.7 1.3 pad_maximum_fusion.6
  206.9 1.9 pad_maximum_fusion
  208.8 0.6 pad_add_fusion.refs_4_
  209.5 0.8 fusion.2.idx_ref
  210.3 1.1 fusion.idx_ref
  211.4 35.0 %qkv.2 = (bf16[512,2048]{1,0:T(8,128)(2,1)}, bf16[512,2048]{1,0:T(8,128)(2,1)}, bf16[512,2048]{1,0:T(8,128)(2,1)}, bf16[512,2048]{1,0:T(8,128)(2,1)}) custom-call(bf16[768,2048]{1,0:T(8,128)(2,1)} %get-tuple-element.16.blocks_ref, s32[512,1]{1,0:T(8,128)} %fusion.2.idx_ref, bf16[1,2048]{1,0:T(2,128)(2,1)} %reshape.399.gain_ref, ...), custom_call_target="tpu_custom_call" | custom-call | flops 12884901888 | bytes 25165824 | tf_op jit(solution)/shard_map/qkv/pallas_call | solution.py:65
  246.4 17.3 %attention.2 = bf16[512,2048]{1,0:T(8,128)(2,1)} custom-call(bf16[512,2048]{1,0:T(8,128)(2,1)} %get-tuple-element.18.q_ref, bf16[512,2048]{1,0:T(8,128)(2,1)} %get-tuple-element.19.refs_0_, bf16[512,2048]{1,0:T(8,128)(2,1)} %get-tuple-element.20.refs_1_.refs_2_, s32[2,512]{1,0:T(2,128)} %copy-done.4, s32[512,2]{1,0:T(8,128)} %bitcast.241), custom_call_target="tpu_custom_call" | custom-call | flops 4294967296 | bytes 8388608 | tf_op jit(solution)/shard_map/attention/pallas_call | solution.py:139
  263.8 9.8 %add_convert_fusion.1.z0_ref = bf16[512,2048]{1,0:T(8,128)(2,1)} fusion(bf16[512,2048]{1,0:T(8,128)(2,1)S(1)} %copy-done.26, bf16[512,2048]{1,0:T(8,128)(2,1)} %attention.2, bf16[2048,2048]{1,0:T(8,128)(2,1)} %bitcast.263), kind=kOutput, calls=%fused_computation.2 | convolution fusion | flops 4300210176 | bytes 14680064 | tf_op jit(solution)/shard_map/dot_general | solution.py:164
  273.6 55.1 %qkv.3 = (bf16[1024,2048]{1,0:T(8,128)(2,1)}, bf16[1024,2048]{1,0:T(8,128)(2,1)}, bf16[1024,2048]{1,0:T(8,128)(2,1)}, bf16[1024,2048]{1,0:T(8,128)(2,1)}) custom-call(bf16[1408,2048]{1,0:T(8,128)(2,1)} %bitcast.61.blocks_ref, s32[1024,1]{1,0:T(8,128)} %fusion.idx_ref, bf16[1,2048]{1,0:T(2,128)(2,1)} %reshape.399.gain_ref, ...), custom_call_target="tpu_custom_call" | custom-call | flops 25769803776 | bytes 25165824 | tf_op jit(solution)/shard_map/qkv/pallas_call | solution.py:65
  328.8 67.3 %attention.3 = bf16[1024,2048]{1,0:T(8,128)(2,1)} custom-call(bf16[1024,2048]{1,0:T(8,128)(2,1)} %get-tuple-element.23.q_ref, bf16[512,2048]{1,0:T(8,128)(2,1)} %get-tuple-element.19.refs_0_, bf16[1024,2048]{1,0:T(8,128)(2,1)} %get-tuple-element.24.refs_1_, bf16[512,2048]{1,0:T(8,128)(2,1)} %get-tuple-element.20.refs_1_.refs_2_, ...), custom_call_target="tpu_custom_call" | custom-call | flops 34359738368 | bytes 16777216 | tf_op jit(solution)/shard_map/attention/pallas_call | solution.py:139
  396.1 13.8 %add_convert_fusion.z1_ref = bf16[1024,2048]{1,0:T(8,128)(2,1)} fusion(bf16[1024,2048]{1,0:T(8,128)(2,1)S(1)} %copy-done.25, bf16[1024,2048]{1,0:T(8,128)(2,1)} %attention.3, bf16[2048,2048]{1,0:T(8,128)(2,1)} %bitcast.264), kind=kOutput, calls=%fused_computation.1 | convolution fusion | flops 8600420352 | bytes 20971520 | tf_op jit(solution)/shard_map/dot_general | solution.py:164
  409.9 311.8 %mlp_back.1 = bf16[3168,2048]{1,0:T(8,128)(2,1)} custom-call(bf16[512,2048]{1,0:T(8,128)(2,1)} %add_convert_fusion.1.z0_ref, bf16[1024,2048]{1,0:T(8,128)(2,1)} %add_convert_fusion.z1_ref, bf16[1,2048]{1,0:T(2,128)(2,1)} %reshape.406.gain_ref, s32[1632,1]{1,0:T(8,128)} %sub.276.chunk_idx_ref, s32[2304,1]{1,0:T(8,128)} %select_n.433.far_idx_ref, ...), custom_call_target="tpu_custom_call" | custom-call | tf_op jit(solution)/shard_map/mlp_back/pallas_call | solution.py:563
  721.7 30.2 %gather_fusion = bf16[3072,2048]{1,0:T(8,128)(2,1)} fusion(bf16[3168,2048]{1,0:T(8,128)(2,1)} %mlp_back.1, s32[3072]{0:T(1024)S(1)} %fusion.60), kind=kCustom, calls=%fused_computation | custom fusion | bytes 25178112 | tf_op jit(solution)/shard_map/gather | solution.py:623
  (198 shorter events, 5.2 us)
Async XLA Ops:
  176.8 5.3 copy-start.3
  176.8 5.4 copy-start.6
  176.8 5.7 copy-start.5
  176.8 5.7 copy-start.13
  176.8 5.7 copy-start.14
  176.8 6.5 copy-start.10
  176.9 11.0 %copy-start.15 = (s32[3,6]{1,0:T(4,128)S(1)}, s32[3,6]{1,0:T(4,128)}, u32[]{:S(2)}) copy-start(s32[3,6]{1,0:T(4,128)} %constant.254) | copy-start | bytes 220
  176.9 11.0 %copy-start.17 = (pred[8,6]{0,1:T(8,128)(4,1)S(1)}, pred[8,6]{0,1:T(8,128)(4,1)}, u32[]{:S(2)}) copy-start(pred[8,6]{0,1:T(8,128)(4,1)} %constant.262) | copy-start | bytes 148
  176.9 11.0 %copy-start.18 = (pred[8,6]{0,1:T(8,128)(4,1)S(1)}, pred[8,6]{0,1:T(8,128)(4,1)}, u32[]{:S(2)}) copy-start(pred[8,6]{0,1:T(8,128)(4,1)} %constant.263) | copy-start | bytes 148
  176.9 11.0 %copy-start.19 = (pred[8,6]{0,1:T(8,128)(4,1)S(1)}, pred[8,6]{0,1:T(8,128)(4,1)}, u32[]{:S(2)}) copy-start(pred[8,6]{0,1:T(8,128)(4,1)} %constant.264) | copy-start | bytes 148
  176.9 10.9 %copy-start.20 = (pred[8,6]{0,1:T(8,128)(4,1)S(1)}, pred[8,6]{0,1:T(8,128)(4,1)}, u32[]{:S(2)}) copy-start(pred[8,6]{0,1:T(8,128)(4,1)} %constant.265) | copy-start | bytes 148
  176.9 10.9 %copy-start.21 = (pred[8,6]{0,1:T(8,128)(4,1)S(1)}, pred[8,6]{0,1:T(8,128)(4,1)}, u32[]{:S(2)}) copy-start(pred[8,6]{0,1:T(8,128)(4,1)} %constant.266) | copy-start | bytes 148
  176.9 10.9 %copy-start.22 = (pred[8,6]{0,1:T(8,128)(4,1)S(1)}, pred[8,6]{0,1:T(8,128)(4,1)}, u32[]{:S(2)}) copy-start(pred[8,6]{0,1:T(8,128)(4,1)} %constant.267) | copy-start | bytes 148
  176.9 10.9 %copy-start.23 = (pred[8,6]{0,1:T(8,128)(4,1)S(1)}, pred[8,6]{0,1:T(8,128)(4,1)}, u32[]{:S(2)}) copy-start(pred[8,6]{0,1:T(8,128)(4,1)} %constant.268) | copy-start | bytes 148
  177.0 10.9 %copy-start.24 = (pred[8,6]{0,1:T(8,128)(4,1)S(1)}, pred[8,6]{0,1:T(8,128)(4,1)}, u32[]{:S(2)}) copy-start(pred[8,6]{0,1:T(8,128)(4,1)} %constant.269) | copy-start | bytes 148
  177.0 12.3 %copy-start.8 = (pred[48,48]{1,0:T(8,128)(4,1)S(1)}, pred[48,48]{1,0:T(8,128)(4,1)}, u32[]{:S(2)}) copy-start(pred[48,48]{1,0:T(8,128)(4,1)} %constant.225.clone) | copy-start | bytes 6916
  177.0 96.6 %all-to-all-start = ((bf16[8,176,2048]{2,1,0:T(8,128)(2,1)}), bf16[8,176,2048]{2,1,0:T(8,128)(2,1)}, u32[]{:S(2)}, u32[]{:S(2)}) async-start(bf16[8,176,2048]{2,1,0:T(8,128)(2,1)} %bitcast.237), calls=%async_computation | async-start | bytes 11534336 | tf_op jit(solution)/shard_map/all_to_all | solution.py:626
  181.9 7.8 %copy-start.7 = (pred[8,6,8]{1,0,2:T(8,128)(4,1)S(1)}, pred[8,6,8]{1,0,2:T(8,128)(4,1)}, u32[]{:S(2)}) copy-start(pred[8,6,8]{1,0,2:T(8,128)(4,1)} %constant.226.clone) | copy-start | bytes 1156
  181.9 8.0 %copy-start.16 = (s32[3,6]{1,0:T(4,128)S(1)}, s32[3,6]{1,0:T(4,128)}, u32[]{:S(2)}) copy-start(s32[3,6]{1,0:T(4,128)} %constant.250) | copy-start | bytes 220
  181.9 10.0 %copy-start.9 = (pred[6,6]{1,0:T(8,128)(4,1)S(1)}, pred[6,6]{1,0:T(8,128)(4,1)}, u32[]{:S(2)}) copy-start(pred[6,6]{1,0:T(8,128)(4,1)} %constant.210.clone) | copy-start | bytes 112
  181.9 12.3 %copy-start.12 = (pred[8,8]{1,0:T(8,128)(4,1)S(1)}, pred[8,8]{1,0:T(8,128)(4,1)}, u32[]{:S(2)}) copy-start(pred[8,8]{1,0:T(8,128)(4,1)} %constant.200.clone) | copy-start | bytes 196
  182.2 14.9 %copy-start.4 = (s32[2,512]{1,0:T(2,128)}, s32[2,512]{1,0:T(2,128)S(1)}, u32[]{:S(2)}) copy-start(s32[2,512]{1,0:T(2,128)S(1)} %fusion.76.refs_2_) | copy-start | bytes 12292
  187.0 12.3 %copy-start.11 = (bf16[2048]{0:T(1024)(128)(2,1)S(1)}, bf16[2048]{0:T(1024)(128)(2,1)}, u32[]{:S(2)}) copy-start(bf16[2048]{0:T(1024)(128)(2,1)} %param.103) | copy-start | bytes 12292
  187.0 12.9 %copy-start.2 = (s32[3072]{0:T(1024)S(1)}, s32[3072]{0:T(1024)}, u32[]{:S(2)}) copy-start(s32[3072]{0:T(1024)} %param.94) | copy-start | bytes 36868
  205.7 3.8 copy-start
  205.7 3.8 copy-start.1
  246.4 17.3 %copy-start.26 = (bf16[512,2048]{1,0:T(8,128)(2,1)S(1)}, bf16[512,2048]{1,0:T(8,128)(2,1)}, u32[]{:S(2)}) copy-start(bf16[512,2048]{1,0:T(8,128)(2,1)} %get-tuple-element.17) | copy-start | bytes 6291460
  328.8 67.3 %copy-start.25 = (bf16[1024,2048]{1,0:T(8,128)(2,1)S(1)}, bf16[1024,2048]{1,0:T(8,128)(2,1)}, u32[]{:S(2)}) copy-start(bf16[1024,2048]{1,0:T(8,128)(2,1)} %get-tuple-element.22) | copy-start | bytes 12582916
